TPU v7x, 32 devices: a whole 2x2x4 slice. The times are simulated.
32 devices in a mesh: il: 2 (over core), xl: 4 (over y, x), ta: 4 (over z).
Axes of the slice: x: 2, y: 2, z: 4, core: 2. Of those that a mesh axis runs over, the one named last changes fastest.
Arguments:
- traces: float32 [32, 832, 1024], P('il', 'xl', 'ta'), may hold values from -6 to 6
- bin_steps: int32 [2, 32, 832], P(None, 'il', 'xl'), may hold values from -1 to 1
Outputs:
- regridded: float32 [16, 416, 1536], P('il', 'xl', 'ta')
Inputs may be any that keep to these rules, and one draw needn't show every extreme that they name: `bin_steps`: every entry is -1, 0 or 1.
All inputs are finite; a program needn't handle non-finite values.
Results may differ from a plain program's by a relative error of at most 0.0001.
Values sent between devices are 32-bit elements; how exact they have to be, the bound alone decides.
No kernel may reach another device: no remote copies, remote signals or barrier semaphores. Data moves between devices by JAX's collectives and lax.ppermute only.
A program may use at most 128 MiB of HBM per device.

v0:
```python
import jax
import jax.numpy as jnp
from jax import lax
from jax.sharding import PartitionSpec as P

TAPS = 16
P_SIZE = 3
Q = 2


def extended(shard, sides, width):
    for axis, dim in sides:
        devices, length = (lax.axis_size(axis), shard.shape[dim])
        up = [(i, (i + 1) % devices) for i in range(devices - 1)]
        down = [(j, i) for i, j in up]
        last = lax.slice_in_dim(shard, length - width, length, axis=dim)
        first = lax.slice_in_dim(shard, 0, width, axis=dim)
        before = lax.ppermute(last, axis, up)
        after = lax.ppermute(first, axis, down)
        shard = jnp.concatenate([before, shard, after], axis=dim)
    return shard


def shifted(shard, axis, by):
    devices = lax.axis_size(axis)
    pairs = [(i, i + by) for i in range(devices) if 0 <= i + by < devices]
    return lax.ppermute(shard, axis, pairs)


def lanczos_table(row_count, col_count, tap_reach, ratio_p, ratio_q):
    row_ids = lax.broadcasted_iota(jnp.int32, (row_count, col_count), 0)
    col_ids = lax.broadcasted_iota(jnp.int32, (row_count, col_count), 1)
    offset = (col_ids * ratio_q - (row_ids - tap_reach) * ratio_p).astype(
        jnp.float32
    ) / jnp.float32(ratio_p)
    inside = jnp.abs(offset) < jnp.float32(tap_reach)
    weights = jnp.sinc(offset) * jnp.sinc(offset / jnp.float32(tap_reach))
    return jnp.where(inside, weights, jnp.zeros_like(weights))


def widen_time(values, tap_reach):
    return extended(values, (("ta", 2),), tap_reach)


def resample(widened, tap_reach):
    row_count, col_count, length = widened.shape
    span = length - 2 * tap_reach
    block = 128
    count = span // block
    out_len = block * P_SIZE // Q
    taps_table = lanczos_table(block + 2 * tap_reach, out_len, tap_reach, P_SIZE, Q)
    flat_rows = widened.reshape(row_count * col_count, length)
    windows = jnp.stack(
        [flat_rows[:, k * block : k * block + block + 2 * tap_reach] for k in range(count)], axis=1
    )
    result = jnp.dot(
        windows, taps_table, precision=lax.Precision.HIGHEST, preferred_element_type=jnp.float32
    )
    return result.reshape(row_count, col_count, count * out_len)


def bin_sums(values, bin_steps):
    row_count, col_count, length = values.shape
    half_rows = row_count // 2
    half_cols = col_count // 2
    bin_total = jnp.zeros((half_rows + 2, half_cols + 2, length), jnp.float32)
    fold_count = jnp.zeros((half_rows + 2, half_cols + 2), jnp.float32)
    for row_phase in (0, 1):
        for col_phase in (0, 1):
            sub_values = values[row_phase::2, col_phase::2]
            step_il = bin_steps[0, row_phase::2, col_phase::2]
            step_xl = bin_steps[1, row_phase::2, col_phase::2]
            for shift_il in (-1, 0, 1):
                for shift_xl in (-1, 0, 1):
                    chosen = ((step_il == shift_il) & (step_xl == shift_xl)).astype(jnp.float32)
                    widths = ((1 + shift_il, 1 - shift_il), (1 + shift_xl, 1 - shift_xl))
                    bin_total = bin_total + jnp.pad(
                        sub_values * chosen[:, :, None], widths + ((0, 0),)
                    )
                    fold_count = fold_count + jnp.pad(chosen, widths)
    return (bin_total, fold_count)


def fold_rims(bin_total, fold_count):
    from_lower = shifted((bin_total[:, -1:], fold_count[:, -1:]), "xl", 1)
    from_upper = shifted((bin_total[:, :1], fold_count[:, :1]), "xl", -1)
    owned_sums = bin_total[:, 1:-1].at[:, :1].add(from_lower[0]).at[:, -1:].add(from_upper[0])
    owned_folds = fold_count[:, 1:-1].at[:, :1].add(from_lower[1]).at[:, -1:].add(from_upper[1])
    from_lower = shifted((owned_sums[-1:], owned_folds[-1:]), "il", 1)
    from_upper = shifted((owned_sums[:1], owned_folds[:1]), "il", -1)
    owned_sums = owned_sums[1:-1].at[:1].add(from_lower[0]).at[-1:].add(from_upper[0])
    owned_folds = owned_folds[1:-1].at[:1].add(from_lower[1]).at[-1:].add(from_upper[1])
    return (owned_sums, owned_folds)


def shards(traces, bin_steps):
    tap_reach = TAPS // 2
    bin_total, fold_count = bin_sums(traces, bin_steps)
    owned_sums, owned_folds = fold_rims(bin_total, fold_count)
    stacked = owned_sums / jnp.maximum(owned_folds, 1.0)[:, :, None]
    return resample(widen_time(stacked, tap_reach), tap_reach)


def solution(mesh):
    return jax.shard_map(
        shards,
        mesh=mesh,
        in_specs=(P("il", "xl", "ta"), P(None, "il", "xl")),
        out_specs=P("il", "xl", "ta"),
        check_vma=False,
    )
```

profile of v0, /device:TPU:4, one launch (start us, length us, event | category | flops | bytes accessed | tf_op | source)
XLA Modules:
  0.0 93.3 jit_solution(2392127374856807084)
XLA Ops:
  0.0 0.9 slice.261
  0.9 0.9 slice.262
  1.8 0.9 slice.264
  2.7 0.9 slice.265
  3.6 0.9 slice.267
  4.5 0.9 slice.268
  5.4 0.9 slice.270
  6.3 0.9 slice.271
  7.4 0.5 copy-done.4
  7.9 0.1 pad_add_fusion.1
  8.1 0.7 fusion.77
  8.7 3.5 %collective-permute-start.4 = (f32[10,1]{1,0:T(8,128)}, f32[10,1]{1,0:T(8,128)}, u32[]{:S(2)}, u32[]{:S(2)}) collective-permute-start(f32[10,1]{1,0:T(8,128)} %get-tuple-element.193), channel_id=1, source_target_pairs={{0,4},{4,8},{8,12},{1,5},{5,9},{9,13},{2,6},{6,10},{10,14},{3,7},{... | collective-permute-start | bytes 128 | tf_op jit(solution)/shard_map/ppermute | solution.py:27
  12.3 3.3 %collective-permute-start.5 = (f32[10,1]{1,0:T(8,128)}, f32[10,1]{1,0:T(8,128)}, u32[]{:S(2)}, u32[]{:S(2)}) collective-permute-start(f32[10,1]{1,0:T(8,128)} %get-tuple-element.192), channel_id=1, source_target_pairs={{4,0},{8,4},{12,8},{5,1},{9,5},{13,9},{6,2},{10,6},{14,10},{7,3},{... | collective-permute-start | bytes 128 | tf_op jit(solution)/shard_map/ppermute | solution.py:27
  15.6 5.6 %slice.260 = f32[8,104,256]{2,1,0:T(8,128)} slice(f32[16,208,256]{2,1,0:T(8,128)} %param.19), slice={[0:16:2], [0:208:2], [0:256:1]} | slice | bytes 1703936 | tf_op jit(solution)/shard_map/slice | solution.py:70
  21.2 5.6 %slice.263 = f32[8,104,256]{2,1,0:T(8,128)} slice(f32[16,208,256]{2,1,0:T(8,128)} %param.19), slice={[0:16:2], [1:208:2], [0:256:1]} | slice | bytes 1703936 | tf_op jit(solution)/shard_map/slice | solution.py:70
  26.8 3.3 %slice.266 = f32[8,104,256]{2,1,0:T(8,128)} slice(f32[16,208,256]{2,1,0:T(8,128)S(1)} %copy-done), slice={[1:16:2], [0:208:2], [0:256:1]} | slice | bytes 1703936 | tf_op jit(solution)/shard_map/slice | solution.py:70
  30.1 3.3 %slice.269 = f32[8,104,256]{2,1,0:T(8,128)} slice(f32[16,208,256]{2,1,0:T(8,128)S(1)} %copy-done), slice={[1:16:2], [1:208:2], [0:256:1]} | slice | bytes 1703936 | tf_op jit(solution)/shard_map/slice | solution.py:70
  33.4 2.3 %broadcast_multiply_fusion.35 = (f32[8,104,256]{2,1,0:T(8,128)S(1)}, f32[8,104,256]{2,1,0:T(8,128)S(1)}, f32[8,104,256]{2,1,0:T(8,128)S(1)}, f32[8,104,256]{2,1,...) fusion(f32[8,104,256]{2,1,0:T(8,128)} %slice.260, ...), kind=kLoop, calls=%fused_computation.42 | loop fusion | flops 1916928 | bytes 8549632 | tf_op jit(solution)/shard_map/mul | solution.py:78
  35.7 1.2 %broadcast_multiply_fusion.26 = (f32[8,104,256]{2,1,0:T(8,128)S(1)}, f32[8,104,256]{2,1,0:T(8,128)S(1)}, f32[8,104,256]{2,1,0:T(8,128)S(1)}, f32[8,104,256]{2,1,...) fusion(f32[8,104,256]{2,1,0:T(8,128)S(1)} %copy-done.3, ...), kind=kLoop, calls=%fused_computation.33 | loop fusion | flops 1916928 | bytes 8549632 | tf_op jit(solution)/shard_map/mul | solution.py:78
  37.0 2.8 %broadcast_multiply_fusion.17 = (f32[8,104,256]{2,1,0:T(8,128)S(1)}, f32[8,104,256]{2,1,0:T(8,128)S(1)}, f32[8,104,256]{2,1,0:T(8,128)S(1)}, f32[8,104,256]{2,1,...) fusion(f32[8,104,256]{2,1,0:T(8,128)S(1)} %copy-done.2, ...), kind=kLoop, calls=%fused_computation.24 | loop fusion | flops 1916928 | bytes 8549632 | tf_op jit(solution)/shard_map/mul | solution.py:78
  39.8 3.6 %broadcast_multiply_fusion.8 = (f32[8,104,256]{2,1,0:T(8,128)}, f32[8,104,256]{2,1,0:T(8,128)}, f32[8,104,256]{2,1,0:T(8,128)}, f32[8,104,256]{2,1,0:T(8,128)}, ...) fusion(f32[8,104,256]{2,1,0:T(8,128)S(1)} %copy-done.1, ...), kind=kLoop, calls=%fused_computation.15 | loop fusion | flops 1916928 | bytes 8549632 | tf_op jit(solution)/shard_map/mul | solution.py:78
  43.4 7.2 %pad_add_fusion = f32[10,106,256]{2,1,0:T(8,128)S(1)} fusion(f32[8,104,256]{2,1,0:T(8,128)} %get-tuple-element.182, f32[8,104,256]{2,1,0:T(8,128)} %get-tuple-element.183, f32[8,104,256]{2,1,0:T(8,128)} %get-tuple-element.184, f32[8,104,256]{2,1,0:T(8,128)} %get-tuple-element.185, f32[8,104,256]{2,1,0:T(8,128)} %get-tuple-element.186, ...), kind=kLoop, calls=%fused_computation.1 | loop fusion | flops 9497600 | bytes 31756288 | tf_op jit(solution)/shard_map/add | solution.py:77
  50.6 3.1 %collective-permute-start = (f32[10,1,256]{2,1,0:T(1,128)S(1)}, f32[10,1,256]{2,1,0:T(1,128)S(1)}, u32[]{:S(2)}, u32[]{:S(2)}) collective-permute-start(f32[10,1,256]{2,1,0:T(1,128)S(1)} %get-tuple-element.149), channel_id=1, source_target_pairs={{0,4},{4,8},{8,12},{1,5},{5,9},{9,13},{2,6},{6,10},{10,14},{3,7},{... | collective-permute-start | bytes 30728 | tf_op jit(solution)/shard_map/ppermute | solution.py:27
  53.7 3.7 %collective-permute-start.1 = (f32[10,1,256]{2,1,0:T(1,128)S(1)}, f32[10,1,256]{2,1,0:T(1,128)S(1)}, u32[]{:S(2)}, u32[]{:S(2)}) collective-permute-start(f32[10,1,256]{2,1,0:T(1,128)S(1)} %get-tuple-element.148), channel_id=1, source_target_pairs={{4,0},{8,4},{12,8},{5,1},{9,5},{13,9},{6,2},{10,6},{14,10},{7,3},{... | collective-permute-start | bytes 30728 | tf_op jit(solution)/shard_map/ppermute | solution.py:27
  57.4 0.6 compare_reduce_fusion
  58.1 1.4 %add_select_fusion = f32[10,1]{1,0:T(8,128)S(1)} fusion(f32[10,1]{1,0:T(8,128)} %collective-permute-done.4, f32[10,106]{1,0:T(8,128)S(1)} %pad_add_fusion.1, pred[]{:T(512)} %compare_reduce_fusion), kind=kLoop, calls=%fused_computation.117 | loop fusion | flops 20 | bytes 121 | tf_op jit(solution)/shard_map/select.12
  59.6 0.8 slice_add_fusion.4
  60.4 0.1 scatter-add.35
  60.4 1.3 %collective-permute-start.6 = (f32[1,104]{1,0:T(1,128)S(1)}, f32[1,104]{1,0:T(1,128)S(1)}, u32[]{:S(2)}, u32[]{:S(2)}) collective-permute-start(f32[1,104]{1,0:T(1,128)S(1)} %get-tuple-element.191), channel_id=1, source_target_pairs={{0,16},{1,17},{2,18},{3,19},{4,20},{5,21},{6,22},{7,23},{8,24},{9,... | collective-permute-start | bytes 1256 | tf_op jit(solution)/shard_map/ppermute | solution.py:27
  61.8 0.1 slice.296
  61.9 1.3 %collective-permute-start.7 = (f32[1,104]{1,0:T(1,128)S(1)}, f32[1,104]{1,0:T(1,128)S(1)}, u32[]{:S(2)}, u32[]{:S(2)}) collective-permute-start(f32[1,104]{1,0:T(1,128)S(1)} %get-tuple-element.190), channel_id=1, source_target_pairs={{16,0},{17,1},{18,2},{19,3},{20,4},{21,5},{22,6},{23,7},{24,8},{25... | collective-permute-start | bytes 1256 | tf_op jit(solution)/shard_map/ppermute | solution.py:27
  63.2 1.7 %collective-permute-done.7 = f32[1,104]{1,0:T(1,128)S(1)} collective-permute-done((f32[1,104]{1,0:T(1,128)S(1)}, f32[1,104]{1,0:T(1,128)S(1)}, u32[]{:S(2)}, u32[]{:S(2)}) %collective-permute-start.7) | collective-permute-done | bytes 448 | tf_op jit(solution)/shard_map/ppermute | solution.py:27
  65.2 2.1 %collective-permute-start.2 = (f32[1,104,256]{2,1,0:T(8,128)S(1)}, f32[1,104,256]{2,1,0:T(8,128)S(1)}, u32[]{:S(2)}, u32[]{:S(2)}) collective-permute-start(f32[1,104,256]{2,1,0:T(8,128)S(1)} %get-tuple-element.151), channel_id=1, source_target_pairs={{0,16},{1,17},{2,18},{3,19},{4,20},{5,21},{6,22},{7,23},{8,24},{9,... | collective-permute-start | bytes 319496 | tf_op jit(solution)/shard_map/ppermute | solution.py:27
  67.3 1.3 %collective-permute-start.3 = (f32[1,104,256]{2,1,0:T(8,128)S(1)}, f32[1,104,256]{2,1,0:T(8,128)S(1)}, u32[]{:S(2)}, u32[]{:S(2)}) collective-permute-start(f32[1,104,256]{2,1,0:T(8,128)S(1)} %get-tuple-element.150), channel_id=1, source_target_pairs={{16,0},{17,1},{18,2},{19,3},{20,4},{21,5},{22,6},{23,7},{24,8},{25... | collective-permute-start | bytes 319496 | tf_op jit(solution)/shard_map/ppermute | solution.py:27
  68.7 1.9 %collective-permute-done.3 = f32[1,104,256]{2,1,0:T(8,128)S(1)} collective-permute-done((f32[1,104,256]{2,1,0:T(8,128)S(1)}, f32[1,104,256]{2,1,0:T(8,128)S(1)}, u32[]{:S(2)}, u32[]{:S(2)}) %collective-permute-start.3) | collective-permute-done | bytes 106528 | tf_op jit(solution)/shard_map/ppermute | solution.py:27
  70.6 0.2 broadcast_divide_fusion
  70.8 0.2 fusion.75
  70.9 3.5 %collective-permute-start.8 = (f32[8,104,8]{2,1,0:T(8,128)S(1)}, f32[8,104,8]{2,1,0:T(8,128)S(1)}, u32[]{:S(2)}, u32[]{:S(2)}) collective-permute-start(f32[8,104,8]{2,1,0:T(8,128)S(1)} %get-tuple-element.152), channel_id=1, source_target_pairs={{0,1},{1,2},{2,3},{4,5},{5,6},{6,7},{8,9},{9,10},{10,11},{12,13},{... | collective-permute-start | bytes 79880 | tf_op jit(solution)/shard_map/ppermute | solution.py:18
  74.5 1.3 %collective-permute-start.9 = (f32[8,104,8]{2,1,0:T(8,128)S(1)}, f32[8,104,8]{2,1,0:T(8,128)S(1)}, u32[]{:S(2)}, u32[]{:S(2)}) collective-permute-start(f32[8,104,8]{2,1,0:T(8,128)S(1)} %get-tuple-element.153), channel_id=1, source_target_pairs={{1,0},{2,1},{3,2},{5,4},{6,5},{7,6},{9,8},{10,9},{11,10},{13,12},{... | collective-permute-start | bytes 79880 | tf_op jit(solution)/shard_map/ppermute | solution.py:19
  75.8 8.0 %collective-permute-done.8 = f32[8,104,8]{2,1,0:T(8,128)S(1)} collective-permute-done((f32[8,104,8]{2,1,0:T(8,128)S(1)}, f32[8,104,8]{2,1,0:T(8,128)S(1)}, u32[]{:S(2)}, u32[]{:S(2)}) %collective-permute-start.8) | collective-permute-done | bytes 26656 | tf_op jit(solution)/shard_map/ppermute | solution.py:18
  83.8 4.1 %collective-permute-done.9 = f32[8,104,8]{2,1,0:T(8,128)S(1)} collective-permute-done((f32[8,104,8]{2,1,0:T(8,128)S(1)}, f32[8,104,8]{2,1,0:T(8,128)S(1)}, u32[]{:S(2)}, u32[]{:S(2)}) %collective-permute-start.9) | collective-permute-done | bytes 26656 | tf_op jit(solution)/shard_map/ppermute | solution.py:19
  87.9 0.5 pad_maximum_fusion
  88.4 0.1 fusion.72
  88.6 0.3 copy.8
  88.8 0.3 copy.9
  89.1 1.8 %fusion = f32[832,2,192]{0,2,1:T(8,128)S(1)} fusion(f32[832,1,144]{0,2,1:T(8,128)S(1)} %bitcast.82, f32[832,1,144]{0,2,1:T(8,128)S(1)} %bitcast.81, s32[144]{0:T(256)S(1)} %add_multiply_fusion, s32[192]{0:T(256)S(1)} %iota_multiply_fusion), kind=kOutput, calls=%fused_computation.2 | convolution fusion | flops 554333184 | bytes 2237760 | tf_op jit(solution)/shard_map/dot_general | solution.py:56
  90.9 0.8 reshape.710
  91.7 1.6 %copy.6 = f32[8,104,384]{2,1,0:T(8,128)} copy(f32[8,104,384]{1,0,2:T(8,128)S(1)} %reshape.710) | data formatting | bytes 2555904 | tf_op jit(solution)/shard_map/reshape | solution.py:59
  (49 shorter events, 0.6 us)
Async XLA Ops:
  7.3 0.6 copy-start.4
  7.4 0.7 copy-start.5
  7.9 18.9 %copy-start = (f32[16,208,256]{2,1,0:T(8,128)S(1)}, f32[16,208,256]{2,1,0:T(8,128)}, u32[]{:S(2)}) copy-start(f32[16,208,256]{2,1,0:T(8,128)} %param.19) | copy-start | bytes 10223620
  8.7 49.4 %collective-permute-start.4 = (f32[10,1]{1,0:T(8,128)}, f32[10,1]{1,0:T(8,128)}, u32[]{:S(2)}, u32[]{:S(2)}) collective-permute-start(f32[10,1]{1,0:T(8,128)} %get-tuple-element.193), channel_id=1, source_target_pairs={{0,4},{4,8},{8,12},{1,5},{5,9},{9,13},{2,6},{6,10},{10,14},{3,7},{... | collective-permute-start | bytes 128 | tf_op jit(solution)/shard_map/ppermute | solution.py:27
  12.3 47.3 %collective-permute-start.5 = (f32[10,1]{1,0:T(8,128)}, f32[10,1]{1,0:T(8,128)}, u32[]{:S(2)}, u32[]{:S(2)}) collective-permute-start(f32[10,1]{1,0:T(8,128)} %get-tuple-element.192), channel_id=1, source_target_pairs={{4,0},{8,4},{12,8},{5,1},{9,5},{13,9},{6,2},{10,6},{14,10},{7,3},{... | collective-permute-start | bytes 128 | tf_op jit(solution)/shard_map/ppermute | solution.py:27
  33.4 2.3 %copy-start.3 = (f32[8,104,256]{2,1,0:T(8,128)S(1)}, f32[8,104,256]{2,1,0:T(8,128)}, u32[]{:S(2)}) copy-start(f32[8,104,256]{2,1,0:T(8,128)} %slice.263) | copy-start | bytes 2555908
  35.7 1.2 %copy-start.2 = (f32[8,104,256]{2,1,0:T(8,128)S(1)}, f32[8,104,256]{2,1,0:T(8,128)}, u32[]{:S(2)}) copy-start(f32[8,104,256]{2,1,0:T(8,128)} %slice.266) | copy-start | bytes 2555908
  37.0 2.8 %copy-start.1 = (f32[8,104,256]{2,1,0:T(8,128)S(1)}, f32[8,104,256]{2,1,0:T(8,128)}, u32[]{:S(2)}) copy-start(f32[8,104,256]{2,1,0:T(8,128)} %slice.269) | copy-start | bytes 2555908
  50.6 14.3 %collective-permute-start = (f32[10,1,256]{2,1,0:T(1,128)S(1)}, f32[10,1,256]{2,1,0:T(1,128)S(1)}, u32[]{:S(2)}, u32[]{:S(2)}) collective-permute-start(f32[10,1,256]{2,1,0:T(1,128)S(1)} %get-tuple-element.149), channel_id=1, source_target_pairs={{0,4},{4,8},{8,12},{1,5},{5,9},{9,13},{2,6},{6,10},{10,14},{3,7},{... | collective-permute-start | bytes 30728 | tf_op jit(solution)/shard_map/ppermute | solution.py:27
  53.7 11.3 %collective-permute-start.1 = (f32[10,1,256]{2,1,0:T(1,128)S(1)}, f32[10,1,256]{2,1,0:T(1,128)S(1)}, u32[]{:S(2)}, u32[]{:S(2)}) collective-permute-start(f32[10,1,256]{2,1,0:T(1,128)S(1)} %get-tuple-element.148), channel_id=1, source_target_pairs={{4,0},{8,4},{12,8},{5,1},{9,5},{13,9},{6,2},{10,6},{14,10},{7,3},{... | collective-permute-start | bytes 30728 | tf_op jit(solution)/shard_map/ppermute | solution.py:27
  60.4 2.7 %collective-permute-start.6 = (f32[1,104]{1,0:T(1,128)S(1)}, f32[1,104]{1,0:T(1,128)S(1)}, u32[]{:S(2)}, u32[]{:S(2)}) collective-permute-start(f32[1,104]{1,0:T(1,128)S(1)} %get-tuple-element.191), channel_id=1, source_target_pairs={{0,16},{1,17},{2,18},{3,19},{4,20},{5,21},{6,22},{7,23},{8,24},{9,... | collective-permute-start | bytes 1256 | tf_op jit(solution)/shard_map/ppermute | solution.py:27
  61.9 3.1 %collective-permute-start.7 = (f32[1,104]{1,0:T(1,128)S(1)}, f32[1,104]{1,0:T(1,128)S(1)}, u32[]{:S(2)}, u32[]{:S(2)}) collective-permute-start(f32[1,104]{1,0:T(1,128)S(1)} %get-tuple-element.190), channel_id=1, source_target_pairs={{16,0},{17,1},{18,2},{19,3},{20,4},{21,5},{22,6},{23,7},{24,8},{25... | collective-permute-start | bytes 1256 | tf_op jit(solution)/shard_map/ppermute | solution.py:27
  65.2 3.5 %collective-permute-start.2 = (f32[1,104,256]{2,1,0:T(8,128)S(1)}, f32[1,104,256]{2,1,0:T(8,128)S(1)}, u32[]{:S(2)}, u32[]{:S(2)}) collective-permute-start(f32[1,104,256]{2,1,0:T(8,128)S(1)} %get-tuple-element.151), channel_id=1, source_target_pairs={{0,16},{1,17},{2,18},{3,19},{4,20},{5,21},{6,22},{7,23},{8,24},{9,... | collective-permute-start | bytes 319496 | tf_op jit(solution)/shard_map/ppermute | solution.py:27
  67.3 3.2 %collective-permute-start.3 = (f32[1,104,256]{2,1,0:T(8,128)S(1)}, f32[1,104,256]{2,1,0:T(8,128)S(1)}, u32[]{:S(2)}, u32[]{:S(2)}) collective-permute-start(f32[1,104,256]{2,1,0:T(8,128)S(1)} %get-tuple-element.150), channel_id=1, source_target_pairs={{16,0},{17,1},{18,2},{19,3},{20,4},{21,5},{22,6},{23,7},{24,8},{25... | collective-permute-start | bytes 319496 | tf_op jit(solution)/shard_map/ppermute | solution.py:27
  70.9 12.9 %collective-permute-start.8 = (f32[8,104,8]{2,1,0:T(8,128)S(1)}, f32[8,104,8]{2,1,0:T(8,128)S(1)}, u32[]{:S(2)}, u32[]{:S(2)}) collective-permute-start(f32[8,104,8]{2,1,0:T(8,128)S(1)} %get-tuple-element.152), channel_id=1, source_target_pairs={{0,1},{1,2},{2,3},{4,5},{5,6},{6,7},{8,9},{9,10},{10,11},{12,13},{... | collective-permute-start | bytes 79880 | tf_op jit(solution)/shard_map/ppermute | solution.py:18
  74.5 13.5 %collective-permute-start.9 = (f32[8,104,8]{2,1,0:T(8,128)S(1)}, f32[8,104,8]{2,1,0:T(8,128)S(1)}, u32[]{:S(2)}, u32[]{:S(2)}) collective-permute-start(f32[8,104,8]{2,1,0:T(8,128)S(1)} %get-tuple-element.153), channel_id=1, source_target_pairs={{1,0},{2,1},{3,2},{5,4},{6,5},{7,6},{9,8},{10,9},{11,10},{13,12},{... | collective-permute-start | bytes 79880 | tf_op jit(solution)/shard_map/ppermute | solution.py:19
where the time goes:
time: 94.4 us; the launch traced here: 93.3 us
  local copies, waits for them, and re-layouts  30 us (32%)
  starting transfers between devices  24.4 us (26%)
  other arithmetic  20.9 us (22%)
  waiting for transfers between devices  15.8 us (17%)
  matrix products  1.78 us (2%)
    ppermute x8, starting transfers between devices, shifted(): return lax.ppermute(shard, axis, pairs)  19.6 us
    slice x4, local copies, waits for them, and re-layouts, bin_sums(): sub_values = values[row_phase::2, col_phase::2]  17.8 us
    mul x4, other arithmetic, bin_sums(): sub_values * chosen[:, :, None]  9.91 us
    ppermute x1, waiting for transfers between devices, extended(): before = lax.ppermute(last, axis, up)  8.04 us
    add x1, other arithmetic, bin_sums(): bin_total + jnp.pad(sub_values * chosen[:, :, None], widths + ((0, 0),))  7.18 us
    ppermute x1, waiting for transfers between devices, extended(): after = lax.ppermute(first, axis, down)  4.14 us
    slice x4, local copies, waits for them, and re-layouts, bin_sums(): step_xl = bin_steps[1, row_phase::2, col_phase::2]  3.59 us
    ppermute x8, waiting for transfers between devices, shifted(): return lax.ppermute(shard, axis, pairs)  3.59 us
  transfers between devices with their start and end apart: 10, of which 4 were waited for; matrix products, arithmetic and copies ran while one was open for 41% of the time, Pallas kernels for 0%

commit v1 on v0

v1 whole, which is shorter than its diff:
```python
import functools

import jax
import jax.numpy as jnp
import numpy as np
from jax import lax
from jax.experimental import pallas as pl
from jax.experimental.pallas import tpu as pltpu
from jax.sharding import PartitionSpec as P

TAPS = 16
P_SIZE = 3
Q = 2
REACH = TAPS // 2
LANES = 128
F32 = jnp.float32
BF16 = jnp.bfloat16


def weight(x):
    inside = np.abs(x) < REACH
    return np.where(inside, np.sinc(x) * np.sinc(x / REACH), 0.0)


def split_table(table):
    high = table.astype(BF16)
    return high, (table - high.astype(np.float64)).astype(BF16)


def main_table(length):
    n = np.arange(length)[:, None]
    m = np.arange(length * P_SIZE // Q)[None, :]
    return weight((m * Q - n * P_SIZE) / P_SIZE)


def edge_table(length):
    out_len = length * P_SIZE // Q
    table = np.zeros((LANES, 2 * LANES))
    k = np.arange(REACH)[:, None]
    m = np.arange(LANES)[None, :]
    table[:REACH, :LANES] = weight((m * Q - (k - REACH) * P_SIZE) / P_SIZE)
    m = m + out_len - LANES
    table[LANES // 2 : LANES // 2 + REACH, LANES:] = weight((m * Q - (length + k) * P_SIZE) / P_SIZE)
    return table


def split(values):
    high = values.astype(BF16)
    return high, (values - high.astype(F32)).astype(BF16)


def dot(a, b, precision=None):
    return jnp.dot(a, b, precision=precision, preferred_element_type=F32)


def rim_kernel(traces, steps, left_out, right_out, left, right, sems):
    rows, cols, length = traces.shape
    copy_l = pltpu.make_async_copy(traces.at[:, 0:8, :], left, sems.at[0])
    copy_r = pltpu.make_async_copy(traces.at[:, cols - 8 : cols, :], right, sems.at[1])
    copy_l.start()
    copy_r.start()
    step_il = steps[0]
    step_xl = steps[1]
    masks = {}
    for side, spots in ((-1, (0, 1)), (1, (cols - 2, cols - 1))):
        for j in spots:
            for shift in (-1, 0, 1):
                hit = (step_xl[:, j : j + 1] == side) & (step_il[:, j : j + 1] == shift)
                masks[side, j, shift] = hit.astype(F32)
    copy_l.wait()
    copy_r.wait()
    parts = []
    for shift in (-1, 0, 1):
        row = []
        for side, buf, spots in ((-1, left, ((0, 0), (1, 1))), (1, right, ((cols - 2, 6), (cols - 1, 7)))):
            total, count = None, None
            for j, place in spots:
                mask = masks[side, j, shift]
                term = buf[:, place, :] * mask
                total = term if total is None else total + term
                count = mask if count is None else count + mask
            row += [total, jnp.broadcast_to(count, (rows, LANES))]
        parts.append(jnp.concatenate(row, axis=1))
    stacked = jnp.concatenate(parts, axis=0)
    r = lax.broadcasted_iota(jnp.int32, (rows, 3 * rows), 0)
    k = lax.broadcasted_iota(jnp.int32, (rows, 3 * rows), 1)
    pick = ((k % rows) // 2 + k // rows == r).astype(F32)
    both = dot(pick, stacked, lax.Precision.HIGHEST)
    left_out[...] = both[:, : length + LANES]
    right_out[...] = both[:, length + LANES :]


def bin_kernel(traces, steps, sums, keys, counts):
    rows, cols, length = traces.shape
    bins = cols // 2
    wide = pl.cdiv(cols, LANES) * LANES
    tall = pl.cdiv(3 * bins, 16) * 16
    column = lax.broadcasted_iota(jnp.int32, (rows, cols), 1) // 2 + steps[1]
    inside = (column >= 0) & (column < bins)
    key = jnp.where(inside, column + (steps[0] + 1) * bins, -1)
    keys[...] = jnp.concatenate([key, jnp.full((rows, wide - cols), -1, jnp.int32)], axis=1)
    sums[...] = jnp.zeros(sums.shape, F32)
    counts[...] = jnp.zeros(counts.shape, F32)
    slot = lax.broadcasted_iota(jnp.int32, (tall, wide), 0)
    pad = jnp.zeros((wide - cols, length), BF16)

    def body(a, _):
        total, count = None, None
        for p in (0, 1):
            i = 2 * a + p
            hot = jnp.where(slot == keys[pl.ds(i, 1), :], 1.0, 0.0).astype(F32)
            for c in range(wide // LANES):
                piece = hot[:, c * LANES : (c + 1) * LANES]
                count = piece if count is None else count + piece
            hot = hot.astype(BF16)
            for part in split(traces[i]):
                term = dot(hot, jnp.concatenate([part, pad], axis=0))
                total = term if total is None else total + term
        for s in range(3):
            sums[a + s, :, :length] += total[s * bins : (s + 1) * bins]
            counts[a + s] += count[s * bins : (s + 1) * bins]
        return 0

    lax.fori_loop(0, rows // 2, body, 0)
    for r in range(rows // 2 + 2):
        whole = jnp.sum(counts[r], axis=1, keepdims=True)
        sums[r, :, length:] = jnp.broadcast_to(whole, (bins, LANES))


def rightward(il, ta):
    return (il + ta) % 2 == 0


def edges(plane, length, lane0, right):
    if right:
        return pltpu.roll(plane[:, length - LANES : length], (lane0 + REACH) % LANES, 1)
    return pltpu.roll(plane[:, :LANES], lane0, 1) if lane0 else plane[:, :LANES]


def join_xl_kernel(sums_in, from_left, from_right, sums, payload, mine):
    rows, bins, width = sums.shape
    length = width - LANES
    inner = rows - 2
    xl, il, ta = lax.axis_index("xl"), lax.axis_index("il"), lax.axis_index("ta")
    has_left = xl > 0
    has_right = xl < lax.axis_size("xl") - 1
    sub = lax.broadcasted_iota(jnp.int32, (8, width), 0)
    for r in range(rows):
        gain = jnp.where((sub == 0) & has_left, jnp.broadcast_to(from_left[r : r + 1, :], (8, width)), 0.0)
        sums[r, 0:8, :] = sums_in[r, 0:8, :] + gain
        gain = jnp.where((sub == 7) & has_right, jnp.broadcast_to(from_right[r : r + 1, :], (8, width)), 0.0)
        sums[r, bins - 8 : bins, :] = sums_in[r, bins - 8 : bins, :] + gain
    lane = lax.broadcasted_iota(jnp.int32, (bins, LANES), 1)
    first = jnp.zeros((bins, LANES), F32)
    last = jnp.zeros((bins, LANES), F32)
    for b in range(inner):
        here = lane // REACH == b
        first = jnp.where(here, edges(sums[b + 1], length, b * REACH, False), first)
        last = jnp.where(here, edges(sums[b + 1], length, b * REACH, True), last)
    right = rightward(il, ta)
    payload[:, :width] = sums[jnp.where(il == 0, rows - 1, 0)]
    payload[:, width:] = jnp.where(right, first, last)
    mine[...] = jnp.where(right, last, first)


def join_il_kernel(payload, mine, got, out):
    bins, width = payload.shape
    width -= LANES
    length = width - LANES
    il, ta = lax.axis_index("il"), lax.axis_index("ta")
    right = rightward(il, ta)
    low = il == 0
    lane = lax.broadcasted_iota(jnp.int32, (bins, LANES), 1)
    other = got[:, width:]
    own = mine[...]
    near = jnp.where(low, own, other)
    far = pltpu.roll(jnp.where(low, other, own), LANES // 2, 1)
    chip = jnp.where(lane < LANES // 2, near, far)
    up = jnp.where(low, got[:, :length], payload[:, :length])
    down = jnp.where(low, payload[:, :length], got[:, :length])
    for plane, lane0 in ((up, LANES // 2 - REACH), (down, LANES // 2)):
        edge = jnp.where(right, edges(plane, length, lane0, True), edges(plane, length, lane0, False))
        chip = chip + jnp.where(lane // REACH == lane0 // REACH, edge, 0.0)
    out[...] = chip


def resampled(planes, table_h, table_l):
    count, bins, width = planes.shape
    length = width - LANES
    scale = 1.0 / jnp.maximum(planes[:, :, length:], 1.0)
    values = planes[:, :, :length] * jnp.concatenate([scale] * (length // LANES), axis=2)
    high, low = split(values.reshape(count * bins, length))
    out = dot(high, table_h) + dot(low, table_h) + dot(high, table_l)
    return out.reshape(count, bins, -1)


def resample_inner_kernel(sums, table_h, table_l, out):
    rows = sums.shape[0]
    out[...] = resampled(sums[2 : rows - 2], table_h[...], table_l[...])


def resample_outer_kernel(sums, got, table_h, table_l, out, folds):
    rows, bins, width = sums.shape
    low = lax.axis_index("il") == 0
    rim = got[:, :width]
    first = sums[1] + jnp.where(low, 0.0, rim)
    last = sums[rows - 2] + jnp.where(low, rim, 0.0)
    folds[0] = first[:, width - LANES :]
    folds[1] = last[:, width - LANES :]
    out[...] = resampled(jnp.stack([first, last]), table_h[...], table_l[...])


def finish_kernel(sums, folds, inner, outer, own, other, table_h, table_l, out):
    rows, bins, width = sums.shape
    length = width - LANES
    count = rows - 2
    il, ta = lax.axis_index("il"), lax.axis_index("ta")
    right = rightward(il, ta)
    low = il == 0
    half = LANES // 2
    lane = lax.broadcasted_iota(jnp.int32, (bins, LANES), 1)
    after = jnp.where(right, own[...], other[...])
    before = jnp.where(right, other[...], own[...])
    after = jnp.where(ta < lax.axis_size("ta") - 1, after, 0.0)
    before = jnp.where(ta > 0, before, 0.0)
    before = jnp.where(low, before, pltpu.roll(before, half, 1))
    after = jnp.where(low, pltpu.roll(after, half, 1), after)
    both = jnp.where(lane < half, before, after)
    pieces = []
    for b in range(count):
        if b in (0, count - 1):
            fold = folds[0 if b == 0 else 1]
        else:
            fold = sums[b + 1, :, length:]
        moved = pltpu.roll(both, LANES - b * REACH, 1) if b else both
        pieces.append(moved * (1.0 / jnp.maximum(fold, 1.0)))
    high, low_part = split(jnp.concatenate(pieces, axis=0))
    fix = dot(high, table_h[...]) + dot(low_part, table_h[...]) + dot(high, table_l[...])
    for b in range(count):
        base = outer.at[0 if b == 0 else 1] if b in (0, count - 1) else inner.at[b - 1]
        part = fix[b * bins : (b + 1) * bins]
        out[b, :, :LANES] = base[:, :LANES] + part[:, :LANES]
        out[b, :, LANES : out.shape[2] - LANES] = base[:, LANES : out.shape[2] - LANES]
        out[b, :, out.shape[2] - LANES :] = base[:, out.shape[2] - LANES :] + part[:, LANES:]


def call(kernel, outs, scratch=(), in_specs=None, aliases={}):
    shapes = [jax.ShapeDtypeStruct(dims, F32) for dims in outs]
    more = {} if in_specs is None else {"in_specs": in_specs}
    return pl.pallas_call(
        kernel,
        out_shape=shapes,
        scratch_shapes=list(scratch),
        input_output_aliases=aliases,
        compiler_params=pltpu.CompilerParams(vmem_limit_bytes=24 << 20),
        **more,
    )


def shards(sizes, traces, bin_steps):
    n_il, n_xl, n_ta = sizes
    rows, cols, length = traces.shape
    half, bins = rows // 2, cols // 2
    width = length + LANES
    out_len = length * P_SIZE // Q
    main = split_table(main_table(length))
    edge = split_table(edge_table(length))
    vmem = pl.BlockSpec(memory_space=pltpu.VMEM)

    rim = call(
        rim_kernel,
        [(rows, width)] * 2,
        [pltpu.VMEM((rows, 8, length), F32)] * 2 + [pltpu.SemaphoreType.DMA((2,))],
        [pl.BlockSpec(memory_space=pl.ANY), vmem],
    )
    to_left, to_right = rim(traces, bin_steps)
    up = [(i, (i + 1) % n_xl) for i in range(n_xl)]
    down = [(j, i) for i, j in up]
    from_left = lax.ppermute(to_right, "xl", up)
    from_right = lax.ppermute(to_left, "xl", down)

    wide = pl.cdiv(cols, LANES) * LANES
    (sums,) = call(
        bin_kernel,
        [(half + 2, bins, width)],
        [pltpu.VMEM((rows, wide), jnp.int32), pltpu.VMEM((half + 2, bins, LANES), F32)],
    )(traces, bin_steps)
    sums, payload, mine = call(
        join_xl_kernel,
        [(half + 2, bins, width), (bins, width + LANES), (bins, LANES)],
        aliases={0: 0},
    )(sums, from_left, from_right)

    swap = [(0, 1), (1, 0)]
    got = lax.ppermute(payload, "il", swap)
    (inner,) = call(resample_inner_kernel, [(half - 2, bins, out_len)])(sums, *main)
    (chip,) = call(join_il_kernel, [(bins, LANES)])(payload, mine, got)

    trades = []
    for core in range(2):
        for t in range(core, n_ta - 1, 2):
            trades += [(core * n_ta + t, core * n_ta + t + 1), (core * n_ta + t + 1, core * n_ta + t)]
    own = lax.ppermute(chip, ("il", "ta"), trades)
    outer, folds = call(resample_outer_kernel, [(2, bins, out_len), (2, bins, LANES)])(sums, got, *main)
    other = lax.ppermute(own, "il", swap)
    (out,) = call(finish_kernel, [(half, bins, out_len)])(sums, folds, inner, outer, own, other, *edge)
    return out


def solution(mesh):
    sizes = tuple(mesh.shape[axis] for axis in ("il", "xl", "ta"))
    assert sizes[0] == 2
    return jax.shard_map(
        functools.partial(shards, sizes),
        mesh=mesh,
        in_specs=(P("il", "xl", "ta"), P(None, "il", "xl")),
        out_specs=P("il", "xl", "ta"),
        check_vma=False,
    )
```

time: 94.4 us -> 22.2 us (0.24)
  the two profiles are of different devices: /device:TPU:4 before, /device:TPU:1 now
where the time goes in v1:
time: 22.2 us; the launch traced here: 21.9 us
  starting transfers between devices  10.5 us (47%)
  Pallas kernels  6.98 us (31%)
  local copies, waits for them, and re-layouts  3.24 us (15%)
  waiting for transfers between devices  1.1 us (5%)
    ppermute x1, starting transfers between devices, shards(): other = lax.ppermute(own, 'il', swap)  5.72 us
    pallas_call x1, Pallas kernels, shards(): call(bin_kernel, [(half + 2, bins, width)], [pltpu.VMEM((rows, wide), jnp...  3.46 us
    unnamed x12, local copies, waits for them, and re-layouts  3.24 us
    ppermute x1, starting transfers between devices, shards(): from_left = lax.ppermute(to_right, 'xl', up)  2.08 us
    pallas_call x1, Pallas kernels, shards(): call(finish_kernel, [(half, bins, out_len)])  1.67 us
    ppermute x1, waiting for transfers between devices, shards(): got = lax.ppermute(payload, 'il', swap)  1.09 us
    ppermute x1, starting transfers between devices, shards(): from_right = lax.ppermute(to_left, 'xl', down)  1.02 us
    ppermute x1, starting transfers between devices, shards(): got = lax.ppermute(payload, 'il', swap)  1.02 us
  transfers between devices with their start and end apart: 5, of which 1 were waited for; matrix products, arithmetic and copies ran while one was open for 0% of the time, Pallas kernels for 20%

profile of v1, /device:TPU:1, one launch (start us, length us, event | category | flops | bytes accessed | tf_op | source)
XLA Modules:
  0.0 21.9 jit_solution(4116571231560589322)
XLA Ops:
  0.0 0.0 copy-start
  0.0 2.0 %copy-done = f32[16,208,256]{2,1,0:T(8,128)S(1)} copy-done((f32[16,208,256]{2,1,0:T(8,128)S(1)}, f32[16,208,256]{2,1,0:T(8,128)}, u32[]{:S(2)}) %copy-start) | copy-done | bytes 3407896
  2.0 0.0 copy-start.3
  2.0 0.8 %copy-done.3 = s32[2,16,208]{2,1,0:T(8,128)S(1)} copy-done((s32[2,16,208]{2,1,0:T(8,128)S(1)}, s32[2,16,208]{2,1,0:T(8,128)}, u32[]{:S(2)}) %copy-start.3) | copy-done | bytes 26648
  2.7 0.4 %shard_map.65 = (f32[16,384]{1,0:T(8,128)S(1)}, f32[16,384]{1,0:T(8,128)S(1)}) custom-call(f32[16,208,256]{2,1,0:T(8,128)S(1)} %copy-done, s32[2,16,208]{2,1,0:T(8,128)S(1)} %copy-done.3), custom_call_target="tpu_custom_call" | custom-call | tf_op jit(solution)/shard_map/pallas_call | solution.py:276
  3.1 2.1 %collective-permute-start = (f32[16,384]{1,0:T(8,128)S(1)}, f32[16,384]{1,0:T(8,128)S(1)}, u32[]{:S(2)}, u32[]{:S(2)}) collective-permute-start(f32[16,384]{1,0:T(8,128)S(1)} %get-tuple-element.12), channel_id=1, source_target_pairs={{0,4},{4,8},{8,12},{12,0},{1,5},{5,9},{9,13},{13,1},{2,6},{6,10},{... | collective-permute-start | bytes 73736 | tf_op jit(solution)/shard_map/ppermute | solution.py:279
  5.2 1.0 %collective-permute-start.1 = (f32[16,384]{1,0:T(8,128)S(1)}, f32[16,384]{1,0:T(8,128)S(1)}, u32[]{:S(2)}, u32[]{:S(2)}) collective-permute-start(f32[16,384]{1,0:T(8,128)S(1)} %get-tuple-element.13), channel_id=1, source_target_pairs={{4,0},{8,4},{12,8},{0,12},{5,1},{9,5},{13,9},{1,13},{6,2},{10,6},{... | collective-permute-start | bytes 73736 | tf_op jit(solution)/shard_map/ppermute | solution.py:280
  6.2 3.5 %shard_map.64.sums_in = f32[10,104,384]{2,1,0:T(8,128)S(1)} custom-call(f32[16,208,256]{2,1,0:T(8,128)S(1)} %copy-done, s32[2,16,208]{2,1,0:T(8,128)S(1)} %copy-done.3), custom_call_target="tpu_custom_call" | custom-call | tf_op jit(solution)/shard_map/pallas_call | solution.py:283
  9.7 0.0 copy-start.1
  9.7 0.0 copy-start.2
  9.7 0.0 collective-permute-done.from_left
  9.7 0.0 collective-permute-done.1.from_right
  9.7 0.3 %shard_map.66 = (f32[10,104,384]{2,1,0:T(8,128)S(1)}, f32[104,512]{1,0:T(8,128)S(1)}, f32[104,128]{1,0:T(8,128)S(1)}) custom-call(f32[10,104,384]{2,1,0:T(8,128)S(1)} %shard_map.64.sums_in, f32[16,384]{1,0:T(8,128)S(1)} %collective-permute-done.from_left, f32[16,384]{1,0:T(8,128)S(1)} %collective-permute-done.1.from_right), custom_call_target="tpu_custom_call", output_to_operand_aliasing={{0}: (0, {})} | custom-call | tf_op jit(solution)/shard_map/pallas_call | solution.py:288
  10.0 1.0 %collective-permute-start.2 = (f32[104,512]{1,0:T(8,128)S(1)}, f32[104,512]{1,0:T(8,128)S(1)}, u32[]{:S(2)}, u32[]{:S(2)}) collective-permute-start(f32[104,512]{1,0:T(8,128)S(1)} %get-tuple-element.15.payload), channel_id=1, source_target_pairs={{0,16},{16,0},{1,17},{17,1},{2,18},{18,2},{3,19},{19,3},{4,20},{20... | collective-permute-start | bytes 638984 | tf_op jit(solution)/shard_map/ppermute | solution.py:295
  11.1 1.1 %collective-permute-done.2.got = f32[104,512]{1,0:T(8,128)S(1)} collective-permute-done((f32[104,512]{1,0:T(8,128)S(1)}, f32[104,512]{1,0:T(8,128)S(1)}, u32[]{:S(2)}, u32[]{:S(2)}) %collective-permute-start.2) | collective-permute-done | bytes 213024 | tf_op jit(solution)/shard_map/ppermute | solution.py:295
  12.2 0.1 shard_map.69
  12.3 0.7 %collective-permute-start.3 = (f32[104,128]{1,0:T(8,128)S(1)}, f32[104,128]{1,0:T(8,128)S(1)}, u32[]{:S(2)}, u32[]{:S(2)}) collective-permute-start(f32[104,128]{1,0:T(8,128)S(1)} %shard_map.69), channel_id=1, source_target_pairs={{0,1},{1,0},{2,3},{3,2},{17,18},{18,17},{4,5},{5,4},{6,7},{7,6},{2... | collective-permute-start | bytes 159752 | tf_op jit(solution)/shard_map/ppermute | solution.py:303
  13.0 0.0 collective-permute-done.3.own
  13.0 5.7 %collective-permute-start.4 = (f32[104,128]{1,0:T(8,128)S(1)}, f32[104,128]{1,0:T(8,128)S(1)}, u32[]{:S(2)}, u32[]{:S(2)}) collective-permute-start(f32[104,128]{1,0:T(8,128)S(1)} %collective-permute-done.3.own), channel_id=1, source_target_pairs={{0,16},{16,0},{1,17},{17,1},{2,18},{18,2},{3,19},{19,3},{4,20},{20... | collective-permute-start | bytes 159752 | tf_op jit(solution)/shard_map/ppermute | solution.py:305
  18.7 0.0 copy-done.1
  18.7 0.0 copy-done.2
  18.7 0.7 %shard_map.68.inner = f32[6,104,384]{2,1,0:T(8,128)S(1)} custom-call(f32[10,104,384]{2,1,0:T(8,128)S(1)} %get-tuple-element.14.sums, bf16[256,384]{1,0:T(8,128)(2,1)S(1)} %copy-done.2, bf16[256,384]{1,0:T(8,128)(2,1)S(1)} %copy-done.1), custom_call_target="tpu_custom_call" | custom-call | tf_op jit(solution)/shard_map/pallas_call | solution.py:296
  19.4 0.0 copy-start.4
  19.4 0.0 copy-start.5
  19.4 0.3 %shard_map.67 = (f32[2,104,384]{2,1,0:T(8,128)S(1)}, f32[2,104,128]{2,1,0:T(8,128)S(1)}) custom-call(f32[10,104,384]{2,1,0:T(8,128)S(1)} %get-tuple-element.14.sums, f32[104,512]{1,0:T(8,128)S(1)} %collective-permute-done.2.got, bf16[256,384]{1,0:T(8,128)(2,1)S(1)} %copy-done.2, bf16[256,384]{1,0:T(8,128)(2,1)S(1)} %copy-done.1), custom_call_target="tpu_custom_call" | custom-call | tf_op jit(solution)/shard_map/pallas_call | solution.py:304
  19.8 0.0 collective-permute-done.4.other
  19.8 0.5 %copy-done.4 = bf16[128,256]{1,0:T(8,128)(2,1)S(1)} copy-done((bf16[128,256]{1,0:T(8,128)(2,1)S(1)}, bf16[128,256]{1,0:T(8,128)(2,1)}, u32[]{:S(2)}) %copy-start.4) | copy-done | bytes 65560
  20.2 0.0 copy-done.5
  20.3 1.7 %shard_map.70 = f32[8,104,384]{2,1,0:T(8,128)} custom-call(f32[10,104,384]{2,1,0:T(8,128)S(1)} %get-tuple-element.14.sums, f32[2,104,128]{2,1,0:T(8,128)S(1)} %get-tuple-element.16.folds, f32[6,104,384]{2,1,0:T(8,128)S(1)} %shard_map.68.inner, f32[2,104,384]{2,1,0:T(8,128)S(1)} %get-tuple-element.17.outer, f32[104,128]{1,0:T(8,128)S(1)} %collective-permute-done.3.own, ...), custom_call_target="tpu_custom_call" | custom-call | tf_op jit(solution)/shard_map/pallas_call | solution.py:306
Async XLA Ops:
  0.0 2.0 %copy-start = (f32[16,208,256]{2,1,0:T(8,128)S(1)}, f32[16,208,256]{2,1,0:T(8,128)}, u32[]{:S(2)}) copy-start(f32[16,208,256]{2,1,0:T(8,128)} %traces.3) | copy-start | bytes 10223620
  2.0 0.8 %copy-start.3 = (s32[2,16,208]{2,1,0:T(8,128)S(1)}, s32[2,16,208]{2,1,0:T(8,128)}, u32[]{:S(2)}) copy-start(s32[2,16,208]{2,1,0:T(8,128)} %steps.3) | copy-start | bytes 79876
  3.1 6.6 %collective-permute-start = (f32[16,384]{1,0:T(8,128)S(1)}, f32[16,384]{1,0:T(8,128)S(1)}, u32[]{:S(2)}, u32[]{:S(2)}) collective-permute-start(f32[16,384]{1,0:T(8,128)S(1)} %get-tuple-element.12), channel_id=1, source_target_pairs={{0,4},{4,8},{8,12},{12,0},{1,5},{5,9},{9,13},{13,1},{2,6},{6,10},{... | collective-permute-start | bytes 73736 | tf_op jit(solution)/shard_map/ppermute | solution.py:279
  5.2 4.5 %collective-permute-start.1 = (f32[16,384]{1,0:T(8,128)S(1)}, f32[16,384]{1,0:T(8,128)S(1)}, u32[]{:S(2)}, u32[]{:S(2)}) collective-permute-start(f32[16,384]{1,0:T(8,128)S(1)} %get-tuple-element.13), channel_id=1, source_target_pairs={{4,0},{8,4},{12,8},{0,12},{5,1},{9,5},{13,9},{1,13},{6,2},{10,6},{... | collective-permute-start | bytes 73736 | tf_op jit(solution)/shard_map/ppermute | solution.py:280
  9.7 9.0 %copy-start.1 = (bf16[256,384]{1,0:T(8,128)(2,1)S(1)}, bf16[256,384]{1,0:T(8,128)(2,1)}, u32[]{:S(2)}) copy-start(bf16[256,384]{1,0:T(8,128)(2,1)} %constant.9.clone.table_l) | copy-start | bytes 589828
  9.7 9.0 %copy-start.2 = (bf16[256,384]{1,0:T(8,128)(2,1)S(1)}, bf16[256,384]{1,0:T(8,128)(2,1)}, u32[]{:S(2)}) copy-start(bf16[256,384]{1,0:T(8,128)(2,1)} %constant.8.clone.table_h) | copy-start | bytes 589828
  10.0 2.1 %collective-permute-start.2 = (f32[104,512]{1,0:T(8,128)S(1)}, f32[104,512]{1,0:T(8,128)S(1)}, u32[]{:S(2)}, u32[]{:S(2)}) collective-permute-start(f32[104,512]{1,0:T(8,128)S(1)} %get-tuple-element.15.payload), channel_id=1, source_target_pairs={{0,16},{16,0},{1,17},{17,1},{2,18},{18,2},{3,19},{19,3},{4,20},{20... | collective-permute-start | bytes 638984 | tf_op jit(solution)/shard_map/ppermute | solution.py:295
  12.3 0.7 %collective-permute-start.3 = (f32[104,128]{1,0:T(8,128)S(1)}, f32[104,128]{1,0:T(8,128)S(1)}, u32[]{:S(2)}, u32[]{:S(2)}) collective-permute-start(f32[104,128]{1,0:T(8,128)S(1)} %shard_map.69), channel_id=1, source_target_pairs={{0,1},{1,0},{2,3},{3,2},{17,18},{18,17},{4,5},{5,4},{6,7},{7,6},{2... | collective-permute-start | bytes 159752 | tf_op jit(solution)/shard_map/ppermute | solution.py:303
  13.0 6.8 %collective-permute-start.4 = (f32[104,128]{1,0:T(8,128)S(1)}, f32[104,128]{1,0:T(8,128)S(1)}, u32[]{:S(2)}, u32[]{:S(2)}) collective-permute-start(f32[104,128]{1,0:T(8,128)S(1)} %collective-permute-done.3.own), channel_id=1, source_target_pairs={{0,16},{16,0},{1,17},{17,1},{2,18},{18,2},{3,19},{19,3},{4,20},{20... | collective-permute-start | bytes 159752 | tf_op jit(solution)/shard_map/ppermute | solution.py:305
  19.4 0.8 %copy-start.4 = (bf16[128,256]{1,0:T(8,128)(2,1)S(1)}, bf16[128,256]{1,0:T(8,128)(2,1)}, u32[]{:S(2)}) copy-start(bf16[128,256]{1,0:T(8,128)(2,1)} %constant.11.clone.table_l) | copy-start | bytes 196612
  19.4 0.9 %copy-start.5 = (bf16[128,256]{1,0:T(8,128)(2,1)S(1)}, bf16[128,256]{1,0:T(8,128)(2,1)}, u32[]{:S(2)}) copy-start(bf16[128,256]{1,0:T(8,128)(2,1)} %constant.10.clone.table_h) | copy-start | bytes 196612

commit v2 on v1

--- a/solution.py
+++ b/solution.py
@@ -8,6 +8,7 @@
 from jax.experimental.pallas import tpu as pltpu
 from jax.sharding import PartitionSpec as P
 
+
 TAPS = 16
 P_SIZE = 3
 Q = 2
@@ -35,12 +36,12 @@
 
 def edge_table(length):
     out_len = length * P_SIZE // Q
-    table = np.zeros((LANES, 2 * LANES))
+    table = np.zeros((2, LANES, LANES))
     k = np.arange(REACH)[:, None]
     m = np.arange(LANES)[None, :]
-    table[:REACH, :LANES] = weight((m * Q - (k - REACH) * P_SIZE) / P_SIZE)
+    table[0, :REACH] = weight((m * Q - (k - REACH) * P_SIZE) / P_SIZE)
     m = m + out_len - LANES
-    table[LANES // 2 : LANES // 2 + REACH, LANES:] = weight((m * Q - (length + k) * P_SIZE) / P_SIZE)
+    table[1, :REACH] = weight((m * Q - (length + k) * P_SIZE) / P_SIZE)
     return table
 
 
@@ -53,12 +54,15 @@
     return jnp.dot(a, b, precision=precision, preferred_element_type=F32)
 
 
-def rim_kernel(traces, steps, left_out, right_out, left, right, sems):
+def rim_kernel(traces, steps_hbm, left_out, right_out, left, right, steps, sems):
     rows, cols, length = traces.shape
+    copy_s = pltpu.make_async_copy(steps_hbm, steps, sems.at[2])
     copy_l = pltpu.make_async_copy(traces.at[:, 0:8, :], left, sems.at[0])
     copy_r = pltpu.make_async_copy(traces.at[:, cols - 8 : cols, :], right, sems.at[1])
+    copy_s.start()
     copy_l.start()
     copy_r.start()
+    copy_s.wait()
     step_il = steps[0]
     step_xl = steps[1]
     masks = {}
@@ -90,7 +94,11 @@
     right_out[...] = both[:, length + LANES :]
 
 
-def bin_kernel(traces, steps, sums, keys, counts):
+def bin_kernel(traces, steps, *refs):
+    tables, (sums, *copies), (keys, counts, sems) = refs[:4], refs[4:9], refs[9:]
+    loads = [pltpu.make_async_copy(a, b, sems.at[n]) for n, (a, b) in enumerate(zip(tables, copies))]
+    for load in loads:
+        load.start()
     rows, cols, length = traces.shape
     bins = cols // 2
     wide = pl.cdiv(cols, LANES) * LANES
@@ -125,10 +133,8 @@
     for r in range(rows // 2 + 2):
         whole = jnp.sum(counts[r], axis=1, keepdims=True)
         sums[r, :, length:] = jnp.broadcast_to(whole, (bins, LANES))
-
-
-def rightward(il, ta):
-    return (il + ta) % 2 == 0
+    for load in loads:
+        load.wait()
 
 
 def edges(plane, length, lane0, right):
@@ -141,7 +147,7 @@
     rows, bins, width = sums.shape
     length = width - LANES
     inner = rows - 2
-    xl, il, ta = lax.axis_index("xl"), lax.axis_index("il"), lax.axis_index("ta")
+    xl, il = lax.axis_index("xl"), lax.axis_index("il")
     has_left = xl > 0
     has_right = xl < lax.axis_size("xl") - 1
     sub = lax.broadcasted_iota(jnp.int32, (8, width), 0)
@@ -157,19 +163,17 @@
         here = lane // REACH == b
         first = jnp.where(here, edges(sums[b + 1], length, b * REACH, False), first)
         last = jnp.where(here, edges(sums[b + 1], length, b * REACH, True), last)
-    right = rightward(il, ta)
-    payload[:, :width] = sums[jnp.where(il == 0, rows - 1, 0)]
-    payload[:, width:] = jnp.where(right, first, last)
-    mine[...] = jnp.where(right, last, first)
+    low = il == 0
+    payload[:, :width] = sums[jnp.where(low, rows - 1, 0)]
+    payload[:, width:] = jnp.where(low, first, last)
+    mine[...] = jnp.where(low, last, first)
 
 
 def join_il_kernel(payload, mine, got, out):
     bins, width = payload.shape
     width -= LANES
     length = width - LANES
-    il, ta = lax.axis_index("il"), lax.axis_index("ta")
-    right = rightward(il, ta)
-    low = il == 0
+    low = lax.axis_index("il") == 0
     lane = lax.broadcasted_iota(jnp.int32, (bins, LANES), 1)
     other = got[:, width:]
     own = mine[...]
@@ -179,7 +183,7 @@
     up = jnp.where(low, got[:, :length], payload[:, :length])
     down = jnp.where(low, payload[:, :length], got[:, :length])
     for plane, lane0 in ((up, LANES // 2 - REACH), (down, LANES // 2)):
-        edge = jnp.where(right, edges(plane, length, lane0, True), edges(plane, length, lane0, False))
+        edge = jnp.where(low, edges(plane, length, lane0, True), edges(plane, length, lane0, False))
         chip = chip + jnp.where(lane // REACH == lane0 // REACH, edge, 0.0)
     out[...] = chip
 
@@ -194,116 +198,174 @@
     return out.reshape(count, bins, -1)
 
 
-def resample_inner_kernel(sums, table_h, table_l, out):
+def write_middle(values, ends, middle, places, out, sem):
+    ends[:, :, :LANES] = values[:, :, :LANES]
+    ends[:, :, LANES:] = values[:, :, values.shape[2] - LANES :]
+    middle[...] = values[:, :, LANES : values.shape[2] - LANES]
+    copies = []
+    for n, place in enumerate(places):
+        copies.append(
+            pltpu.make_async_copy(middle.at[n], out.at[place, :, LANES : out.shape[2] - LANES], sem.at[n])
+        )
+    for copy in copies:
+        copy.start()
+    for copy in copies:
+        copy.wait()
+
+
+def resample_inner_kernel(sums, table_h, table_l, out, ends, middle, sem):
     rows = sums.shape[0]
-    out[...] = resampled(sums[2 : rows - 2], table_h[...], table_l[...])
-
-
-def resample_outer_kernel(sums, got, table_h, table_l, out, folds):
-    rows, bins, width = sums.shape
+    values = resampled(sums[2 : rows - 2], table_h[...], table_l[...])
+    write_middle(values, ends, middle, range(1, rows - 3), out, sem)
+
+
+def resample_outer_kernel(out_in, sums, got, table_h, table_l, out, ends, folds, middle, sem):
+    rows, _, width = sums.shape
     low = lax.axis_index("il") == 0
     rim = got[:, :width]
     first = sums[1] + jnp.where(low, 0.0, rim)
     last = sums[rows - 2] + jnp.where(low, rim, 0.0)
     folds[0] = first[:, width - LANES :]
     folds[1] = last[:, width - LANES :]
-    out[...] = resampled(jnp.stack([first, last]), table_h[...], table_l[...])
-
-
-def finish_kernel(sums, folds, inner, outer, own, other, table_h, table_l, out):
+    values = resampled(jnp.stack([first, last]), table_h[...], table_l[...])
+    write_middle(values, ends, middle, (0, rows - 3), out, sem)
+
+
+def finish_kernel(own_side, out_in, sums, folds, inner, outer, got, table_h, table_l, out, piece, sem):
     rows, bins, width = sums.shape
     length = width - LANES
     count = rows - 2
     il, ta = lax.axis_index("il"), lax.axis_index("ta")
-    right = rightward(il, ta)
     low = il == 0
     half = LANES // 2
-    lane = lax.broadcasted_iota(jnp.int32, (bins, LANES), 1)
-    after = jnp.where(right, own[...], other[...])
-    before = jnp.where(right, other[...], own[...])
-    after = jnp.where(ta < lax.axis_size("ta") - 1, after, 0.0)
-    before = jnp.where(ta > 0, before, 0.0)
-    before = jnp.where(low, before, pltpu.roll(before, half, 1))
-    after = jnp.where(low, pltpu.roll(after, half, 1), after)
-    both = jnp.where(lane < half, before, after)
+    before = low if own_side else ~low
+    there = jnp.where(before, ta > 0, ta < lax.axis_size("ta") - 1)
+    values = jnp.where(there, got[...], 0.0)
+    values = jnp.where(low, values, pltpu.roll(values, half, 1))
     pieces = []
     for b in range(count):
         if b in (0, count - 1):
             fold = folds[0 if b == 0 else 1]
         else:
             fold = sums[b + 1, :, length:]
-        moved = pltpu.roll(both, LANES - b * REACH, 1) if b else both
+        moved = pltpu.roll(values, LANES - b * REACH, 1) if b else values
         pieces.append(moved * (1.0 / jnp.maximum(fold, 1.0)))
     high, low_part = split(jnp.concatenate(pieces, axis=0))
-    fix = dot(high, table_h[...]) + dot(low_part, table_h[...]) + dot(high, table_l[...])
+    side = jnp.where(before, 0, 1)
+    start_h, start_l = table_h[side], table_l[side]
+    fix = dot(high, start_h) + dot(low_part, start_h) + dot(high, start_l)
+    start = pl.multiple_of(jnp.where(before, 0, out.shape[2] - LANES), LANES)
+    copies = []
     for b in range(count):
-        base = outer.at[0 if b == 0 else 1] if b in (0, count - 1) else inner.at[b - 1]
-        part = fix[b * bins : (b + 1) * bins]
-        out[b, :, :LANES] = base[:, :LANES] + part[:, :LANES]
-        out[b, :, LANES : out.shape[2] - LANES] = base[:, LANES : out.shape[2] - LANES]
-        out[b, :, out.shape[2] - LANES :] = base[:, out.shape[2] - LANES :] + part[:, LANES:]
-
-
-def call(kernel, outs, scratch=(), in_specs=None, aliases={}):
-    shapes = [jax.ShapeDtypeStruct(dims, F32) for dims in outs]
-    more = {} if in_specs is None else {"in_specs": in_specs}
-    return pl.pallas_call(
-        kernel,
-        out_shape=shapes,
-        scratch_shapes=list(scratch),
-        input_output_aliases=aliases,
-        compiler_params=pltpu.CompilerParams(vmem_limit_bytes=24 << 20),
-        **more,
-    )
+        ends = outer.at[0 if b == 0 else 1] if b in (0, count - 1) else inner.at[b - 1]
+        end = jnp.where(before, ends[:, :LANES], ends[:, LANES:])
+        piece[b] = end + fix[b * bins : (b + 1) * bins]
+        copies.append(pltpu.make_async_copy(piece.at[b], out.at[b, :, pl.ds(start, LANES)], sem.at[b]))
+        copies[-1].start()
+    for copy in copies:
+        copy.wait()
+
+
+VMEM = pl.BlockSpec(memory_space=pltpu.VMEM)
+HBM = pl.BlockSpec(memory_space=pltpu.HBM)
+
+
+def call(kernel, ins, outs, scratch=(), aliases={}):
+    def run(*args):
+        return pl.pallas_call(
+            kernel,
+            in_specs=ins,
+            out_specs=[spec for spec, _ in outs],
+            out_shape=[shape for _, shape in outs],
+            scratch_shapes=list(scratch),
+            input_output_aliases=aliases,
+            compiler_params=pltpu.CompilerParams(vmem_limit_bytes=24 << 20),
+        )(*args)
+
+    return run
+
+
+def in_hbm(values):
+    return pltpu.with_memory_space_constraint(values, pltpu.HBM)
+
+
+def vmem(*dims, kind=F32):
+    return VMEM, jax.ShapeDtypeStruct(dims, kind)
 
 
 def shards(sizes, traces, bin_steps):
-    n_il, n_xl, n_ta = sizes
+    return steps_of(sizes, traces, bin_steps)
+
+
+def steps_of(sizes, traces, bin_steps):
+    _, n_xl, n_ta = sizes
     rows, cols, length = traces.shape
     half, bins = rows // 2, cols // 2
     width = length + LANES
     out_len = length * P_SIZE // Q
     main = split_table(main_table(length))
     edge = split_table(edge_table(length))
-    vmem = pl.BlockSpec(memory_space=pltpu.VMEM)
-
-    rim = call(
+    dma = pltpu.SemaphoreType.DMA
+
+    to_left, to_right = call(
         rim_kernel,
-        [(rows, width)] * 2,
-        [pltpu.VMEM((rows, 8, length), F32)] * 2 + [pltpu.SemaphoreType.DMA((2,))],
-        [pl.BlockSpec(memory_space=pl.ANY), vmem],
-    )
-    to_left, to_right = rim(traces, bin_steps)
+        [HBM, HBM],
+        [vmem(rows, width)] * 2,
+        [pltpu.VMEM((rows, 8, length), F32)] * 2 + [pltpu.VMEM(bin_steps.shape, jnp.int32), dma((3,))],
+    )(in_hbm(traces), in_hbm(bin_steps))
     up = [(i, (i + 1) % n_xl) for i in range(n_xl)]
     down = [(j, i) for i, j in up]
     from_left = lax.ppermute(to_right, "xl", up)
     from_right = lax.ppermute(to_left, "xl", down)
 
     wide = pl.cdiv(cols, LANES) * LANES
-    (sums,) = call(
+    tables = (*main, *edge)
+    sums, *tables = call(
         bin_kernel,
-        [(half + 2, bins, width)],
-        [pltpu.VMEM((rows, wide), jnp.int32), pltpu.VMEM((half + 2, bins, LANES), F32)],
-    )(traces, bin_steps)
+        [VMEM, VMEM] + [HBM] * 4,
+        [vmem(half + 2, bins, width)] + [vmem(*t.shape, kind=BF16) for t in tables],
+        [pltpu.VMEM((rows, wide), jnp.int32), pltpu.VMEM((half + 2, bins, LANES), F32), dma((4,))],
+    )(traces, bin_steps, *[in_hbm(t) for t in tables])
+    main, edge = tables[:2], tables[2:]
     sums, payload, mine = call(
         join_xl_kernel,
-        [(half + 2, bins, width), (bins, width + LANES), (bins, LANES)],
+        [VMEM] * 3,
+        [vmem(half + 2, bins, width), vmem(bins, width + LANES), vmem(bins, LANES)],
         aliases={0: 0},
     )(sums, from_left, from_right)
 
     swap = [(0, 1), (1, 0)]
     got = lax.ppermute(payload, "il", swap)
-    (inner,) = call(resample_inner_kernel, [(half - 2, bins, out_len)])(sums, *main)
-    (chip,) = call(join_il_kernel, [(bins, LANES)])(payload, mine, got)
-
-    trades = []
-    for core in range(2):
-        for t in range(core, n_ta - 1, 2):
-            trades += [(core * n_ta + t, core * n_ta + t + 1), (core * n_ta + t + 1, core * n_ta + t)]
-    own = lax.ppermute(chip, ("il", "ta"), trades)
-    outer, folds = call(resample_outer_kernel, [(2, bins, out_len), (2, bins, LANES)])(sums, got, *main)
+    whole = (HBM, jax.ShapeDtypeStruct((half, bins, out_len), F32))
+    middle = out_len - 2 * LANES
+    out, inner = call(
+        resample_inner_kernel,
+        [VMEM] * 3,
+        [whole, vmem(half - 2, bins, 2 * LANES)],
+        [pltpu.VMEM((half - 2, bins, middle), F32), dma((half - 2,))],
+    )(sums, *main)
+    (chip,) = call(join_il_kernel, [VMEM] * 3, [vmem(bins, LANES)])(payload, mine, got)
+
+    trade = [(n_ta - 1, 2 * n_ta - 1), (n_ta, 0)]
+    for t in range(n_ta - 1):
+        trade += [(t, t + 1), (n_ta + t + 1, n_ta + t)]
+    own = lax.ppermute(chip, ("il", "ta"), trade)
+    out, outer, folds = call(
+        resample_outer_kernel,
+        [HBM] + [VMEM] * 4,
+        [whole, vmem(2, bins, 2 * LANES), vmem(2, bins, LANES)],
+        [pltpu.VMEM((2, bins, middle), F32), dma((2,))],
+        {0: 0},
+    )(out, sums, got, *main)
     other = lax.ppermute(own, "il", swap)
-    (out,) = call(finish_kernel, [(half, bins, out_len)])(sums, folds, inner, outer, own, other, *edge)
+    for mine, halo in ((True, own), (False, other)):
+        (out,) = call(
+            functools.partial(finish_kernel, mine),
+            [HBM] + [VMEM] * 7,
+            [whole],
+            [pltpu.VMEM((half, bins, LANES), F32), dma((half,))],
+            {0: 0},
+        )(out, sums, folds, inner, outer, halo, *edge)
     return out
 
 

time: 22.2 us -> 19.9 us (0.90)
  starting transfers between devices: 10.5 us -> 5.43 us
  local copies, waits for them, and re-layouts: 3.24 us -> 0.01 us
  Pallas kernels: 6.98 us -> 10.2 us
  waiting for transfers between devices: 1.1 us -> 3.96 us
    ppermute x5, starting transfers between devices: 10.5 us -> 5.43 us  [the longest x1 2.08 us: steps_of(): from_left = lax.ppermute(to_right, 'xl', up)]
    pallas_call x7 -> x8, Pallas kernels: 6.98 us -> 10.2 us  [run(): pl.pallas_call(kernel, in_specs=ins, out_specs=[spec for spec, _ in outs]...]
    unnamed x12 -> x4, local copies, waits for them, and re-layouts: 3.24 us -> 0.01 us
    ppermute x5, waiting for transfers between devices: 1.1 us -> 3.96 us  [the longest x1 2.86 us: steps_of(): own = lax.ppermute(chip, ('il', 'ta'), trade)]
  transfers between devices with their start and end apart: 5 -> 5, of which waited for: 1 -> 2; matrix products, arithmetic and copies ran while one was open for 0% -> 0% of each run, Pallas kernels for 20% -> 36%
where the time goes in v2:
time: 19.9 us; the launch traced here: 19.7 us
  Pallas kernels  10.2 us (51%)
  starting transfers between devices  5.43 us (27%)
  waiting for transfers between devices  3.96 us (20%)
    pallas_call x8, Pallas kernels, run(): pl.pallas_call(kernel, in_specs=ins, out_specs=[spec for spec, _ in outs]...  10.2 us
    ppermute x1, waiting for transfers between devices, steps_of(): own = lax.ppermute(chip, ('il', 'ta'), trade)  2.86 us
    ppermute x1, starting transfers between devices, steps_of(): from_left = lax.ppermute(to_right, 'xl', up)  2.08 us
    ppermute x1, waiting for transfers between devices, steps_of(): got = lax.ppermute(payload, 'il', swap)  1.09 us
    ppermute x1, starting transfers between devices, steps_of(): from_right = lax.ppermute(to_left, 'xl', down)  1.02 us
    ppermute x1, starting transfers between devices, steps_of(): got = lax.ppermute(payload, 'il', swap)  1.02 us
    ppermute x1, starting transfers between devices, steps_of(): other = lax.ppermute(own, 'il', swap)  0.92 us
  transfers between devices with their start and end apart: 5, of which 2 were waited for; matrix products, arithmetic and copies ran while one was open for 0% of the time, Pallas kernels for 36%

profile of v2, /device:TPU:1, one launch (start us, length us, event | category | flops | bytes accessed | tf_op | source)
XLA Modules:
  0.0 19.7 jit_solution(10258750921228186244)
XLA Ops:
  0.0 0.0 copy-start.1
  0.0 0.0 copy-start
  0.0 1.5 %shard_map.65 = (f32[16,384]{1,0:T(8,128)S(1)}, f32[16,384]{1,0:T(8,128)S(1)}) custom-call(f32[16,208,256]{2,1,0:T(8,128)} %traces.3, s32[2,16,208]{2,1,0:T(8,128)} %steps_hbm.1), custom_call_target="tpu_custom_call" | custom-call | tf_op jit(solution)/shard_map/pallas_call | solution.py:275
  1.5 2.1 %collective-permute-start = (f32[16,384]{1,0:T(8,128)S(1)}, f32[16,384]{1,0:T(8,128)S(1)}, u32[]{:S(2)}, u32[]{:S(2)}) collective-permute-start(f32[16,384]{1,0:T(8,128)S(1)} %get-tuple-element.21), channel_id=1, source_target_pairs={{0,4},{4,8},{8,12},{12,0},{1,5},{5,9},{9,13},{13,1},{2,6},{6,10},{... | collective-permute-start | bytes 73736 | tf_op jit(solution)/shard_map/ppermute | solution.py:318
  3.6 1.0 %collective-permute-start.1 = (f32[16,384]{1,0:T(8,128)S(1)}, f32[16,384]{1,0:T(8,128)S(1)}, u32[]{:S(2)}, u32[]{:S(2)}) collective-permute-start(f32[16,384]{1,0:T(8,128)S(1)} %get-tuple-element.22), channel_id=1, source_target_pairs={{4,0},{8,4},{12,8},{0,12},{5,1},{9,5},{13,9},{1,13},{6,2},{10,6},{... | collective-permute-start | bytes 73736 | tf_op jit(solution)/shard_map/ppermute | solution.py:319
  4.6 0.0 copy-done.1
  4.6 0.0 copy-done
  4.6 3.5 %shard_map.64 = (f32[10,104,384]{2,1,0:T(8,128)S(1)}, bf16[256,384]{1,0:T(8,128)(2,1)S(1)}, bf16[256,384]{1,0:T(8,128)(2,1)S(1)}, bf16[2,128,128]{2,1,0:T(8,128)(2,1)S(1)}, bf16[2,128,128]{2,1,0:T(8,128)(2,1)S(1)}) custom-call(f32[16,208,256]{2,1,0:T(8,128)S(1)} %copy-done, s32[2,16,208]{2,1,0:T(8,128)S(1)} %copy-done.1, ...), custom_call_target="tpu_custom_call" | custom-call | tf_op jit(solution)/shard_map/pallas_call | solution.py:275
  8.1 0.0 collective-permute-done.from_left
  8.1 0.0 collective-permute-done.1.from_right
  8.1 0.3 %shard_map.66 = (f32[10,104,384]{2,1,0:T(8,128)S(1)}, f32[104,512]{1,0:T(8,128)S(1)}, f32[104,128]{1,0:T(8,128)S(1)}) custom-call(f32[10,104,384]{2,1,0:T(8,128)S(1)} %get-tuple-element.20.sums_in, f32[16,384]{1,0:T(8,128)S(1)} %collective-permute-done.from_left, f32[16,384]{1,0:T(8,128)S(1)} %collective-permute-done.1.from_right), custom_call_target="tpu_custom_call", output_to_operand_aliasing={{0}: (0, {})} | custom-call | tf_op jit(solution)/shard_map/pallas_call | solution.py:275
  8.5 1.0 %collective-permute-start.2 = (f32[104,512]{1,0:T(8,128)S(1)}, f32[104,512]{1,0:T(8,128)S(1)}, u32[]{:S(2)}, u32[]{:S(2)}) collective-permute-start(f32[104,512]{1,0:T(8,128)S(1)} %get-tuple-element.27.payload), channel_id=1, source_target_pairs={{0,16},{16,0},{1,17},{17,1},{2,18},{18,2},{3,19},{19,3},{4,20},{20... | collective-permute-start | bytes 638984 | tf_op jit(solution)/shard_map/ppermute | solution.py:338
  9.5 1.1 %collective-permute-done.2.got = f32[104,512]{1,0:T(8,128)S(1)} collective-permute-done((f32[104,512]{1,0:T(8,128)S(1)}, f32[104,512]{1,0:T(8,128)S(1)}, u32[]{:S(2)}, u32[]{:S(2)}) %collective-permute-start.2) | collective-permute-done | bytes 213024 | tf_op jit(solution)/shard_map/ppermute | solution.py:338
  10.6 0.1 shard_map.69
  10.7 0.4 %collective-permute-start.3 = (f32[104,128]{1,0:T(8,128)S(1)}, f32[104,128]{1,0:T(8,128)S(1)}, u32[]{:S(2)}, u32[]{:S(2)}) collective-permute-start(f32[104,128]{1,0:T(8,128)S(1)} %shard_map.69), channel_id=1, source_target_pairs={{3,19},{16,0},{0,1},{17,16},{1,2},{18,17},{2,3},{19,18},{7,23},{20... | collective-permute-start | bytes 159752 | tf_op jit(solution)/shard_map/ppermute | solution.py:352
  11.1 2.9 %collective-permute-done.3.got = f32[104,128]{1,0:T(8,128)S(1)} collective-permute-done((f32[104,128]{1,0:T(8,128)S(1)}, f32[104,128]{1,0:T(8,128)S(1)}, u32[]{:S(2)}, u32[]{:S(2)}) %collective-permute-start.3) | collective-permute-done | bytes 53280 | tf_op jit(solution)/shard_map/ppermute | solution.py:352
  14.0 0.9 %collective-permute-start.4 = (f32[104,128]{1,0:T(8,128)S(1)}, f32[104,128]{1,0:T(8,128)S(1)}, u32[]{:S(2)}, u32[]{:S(2)}) collective-permute-start(f32[104,128]{1,0:T(8,128)S(1)} %collective-permute-done.3.got), channel_id=1, source_target_pairs={{0,16},{16,0},{1,17},{17,1},{2,18},{18,2},{3,19},{19,3},{4,20},{20... | collective-permute-start | bytes 159752 | tf_op jit(solution)/shard_map/ppermute | solution.py:360
  14.9 1.4 %shard_map.67 = (f32[8,104,384]{2,1,0:T(8,128)}, f32[6,104,256]{2,1,0:T(8,128)S(1)}) custom-call(f32[10,104,384]{2,1,0:T(8,128)S(1)} %get-tuple-element.23.sums, bf16[256,384]{1,0:T(8,128)(2,1)S(1)} %get-tuple-element.24.table_h, bf16[256,384]{1,0:T(8,128)(2,1)S(1)} %get-tuple-element.25.table_l), custom_call_target="tpu_custom_call" | custom-call | tf_op jit(solution)/shard_map/pallas_call | solution.py:275
  16.3 1.0 %shard_map.68 = (f32[8,104,384]{2,1,0:T(8,128)}, f32[2,104,256]{2,1,0:T(8,128)S(1)}, f32[2,104,128]{2,1,0:T(8,128)S(1)}) custom-call(f32[8,104,384]{2,1,0:T(8,128)} %get-tuple-element.26.out_in, f32[10,104,384]{2,1,0:T(8,128)S(1)} %get-tuple-element.23.sums, f32[104,512]{1,0:T(8,128)S(1)} %collective-permute-done.2.got, ...), custom_call_target="tpu_custom_call", output_to_operand_aliasing={{0}: (0, {})} | custom-call | tf_op jit(solution)/shard_map/pallas_call | solution.py:275
  17.3 1.2 %shard_map.70.out_in = f32[8,104,384]{2,1,0:T(8,128)} custom-call(f32[8,104,384]{2,1,0:T(8,128)} %get-tuple-element.28.out_in, f32[10,104,384]{2,1,0:T(8,128)S(1)} %get-tuple-element.23.sums, f32[2,104,128]{2,1,0:T(8,128)S(1)} %get-tuple-element.29.folds, f32[6,104,256]{2,1,0:T(8,128)S(1)} %get-tuple-element.30.inner, ...), custom_call_target="tpu_custom_call", output_to_operand_aliasing={{}: (0, {})} | custom-call | tf_op jit(solution)/shard_map/pallas_call | solution.py:275
  18.5 0.0 collective-permute-done.4.got
  18.5 1.2 %shard_map.71 = f32[8,104,384]{2,1,0:T(8,128)} custom-call(f32[8,104,384]{2,1,0:T(8,128)} %shard_map.70.out_in, f32[10,104,384]{2,1,0:T(8,128)S(1)} %get-tuple-element.23.sums, f32[2,104,128]{2,1,0:T(8,128)S(1)} %get-tuple-element.29.folds, f32[6,104,256]{2,1,0:T(8,128)S(1)} %get-tuple-element.30.inner, ...), custom_call_target="tpu_custom_call", output_to_operand_aliasing={{}: (0, {})} | custom-call | tf_op jit(solution)/shard_map/pallas_call | solution.py:275
Async XLA Ops:
  0.0 4.6 %copy-start.1 = (s32[2,16,208]{2,1,0:T(8,128)S(1)}, s32[2,16,208]{2,1,0:T(8,128)}, u32[]{:S(2)}) copy-start(s32[2,16,208]{2,1,0:T(8,128)} %steps_hbm.1) | copy-start | bytes 79876
  0.0 4.6 %copy-start = (f32[16,208,256]{2,1,0:T(8,128)S(1)}, f32[16,208,256]{2,1,0:T(8,128)}, u32[]{:S(2)}) copy-start(f32[16,208,256]{2,1,0:T(8,128)} %traces.3) | copy-start | bytes 10223620
  1.5 6.6 %collective-permute-start = (f32[16,384]{1,0:T(8,128)S(1)}, f32[16,384]{1,0:T(8,128)S(1)}, u32[]{:S(2)}, u32[]{:S(2)}) collective-permute-start(f32[16,384]{1,0:T(8,128)S(1)} %get-tuple-element.21), channel_id=1, source_target_pairs={{0,4},{4,8},{8,12},{12,0},{1,5},{5,9},{9,13},{13,1},{2,6},{6,10},{... | collective-permute-start | bytes 73736 | tf_op jit(solution)/shard_map/ppermute | solution.py:318
  3.6 4.6 %collective-permute-start.1 = (f32[16,384]{1,0:T(8,128)S(1)}, f32[16,384]{1,0:T(8,128)S(1)}, u32[]{:S(2)}, u32[]{:S(2)}) collective-permute-start(f32[16,384]{1,0:T(8,128)S(1)} %get-tuple-element.22), channel_id=1, source_target_pairs={{4,0},{8,4},{12,8},{0,12},{5,1},{9,5},{13,9},{1,13},{6,2},{10,6},{... | collective-permute-start | bytes 73736 | tf_op jit(solution)/shard_map/ppermute | solution.py:319
  8.5 2.1 %collective-permute-start.2 = (f32[104,512]{1,0:T(8,128)S(1)}, f32[104,512]{1,0:T(8,128)S(1)}, u32[]{:S(2)}, u32[]{:S(2)}) collective-permute-start(f32[104,512]{1,0:T(8,128)S(1)} %get-tuple-element.27.payload), channel_id=1, source_target_pairs={{0,16},{16,0},{1,17},{17,1},{2,18},{18,2},{3,19},{19,3},{4,20},{20... | collective-permute-start | bytes 638984 | tf_op jit(solution)/shard_map/ppermute | solution.py:338
  10.7 3.3 %collective-permute-start.3 = (f32[104,128]{1,0:T(8,128)S(1)}, f32[104,128]{1,0:T(8,128)S(1)}, u32[]{:S(2)}, u32[]{:S(2)}) collective-permute-start(f32[104,128]{1,0:T(8,128)S(1)} %shard_map.69), channel_id=1, source_target_pairs={{3,19},{16,0},{0,1},{17,16},{1,2},{18,17},{2,3},{19,18},{7,23},{20... | collective-permute-start | bytes 159752 | tf_op jit(solution)/shard_map/ppermute | solution.py:352
  14.0 4.6 %collective-permute-start.4 = (f32[104,128]{1,0:T(8,128)S(1)}, f32[104,128]{1,0:T(8,128)S(1)}, u32[]{:S(2)}, u32[]{:S(2)}) collective-permute-start(f32[104,128]{1,0:T(8,128)S(1)} %collective-permute-done.3.got), channel_id=1, source_target_pairs={{0,16},{16,0},{1,17},{17,1},{2,18},{18,2},{3,19},{19,3},{4,20},{20... | collective-permute-start | bytes 159752 | tf_op jit(solution)/shard_map/ppermute | solution.py:360

commit v3 on v2

v3 whole, which is shorter than its diff:
```python
import functools

import jax
import jax.numpy as jnp
import numpy as np
from jax import lax
from jax.experimental import pallas as pl
from jax.experimental.pallas import tpu as pltpu
from jax.sharding import PartitionSpec as P


TAPS = 16
P_SIZE = 3
Q = 2
REACH = TAPS // 2
LANES = 128
F32 = jnp.float32
BF16 = jnp.bfloat16
SPREAD = 16


def weight(x):
    inside = np.abs(x) < REACH
    return np.where(inside, np.sinc(x) * np.sinc(x / REACH), 0.0)


def split_table(table):
    high = table.astype(BF16)
    return high, (table - high.astype(np.float64)).astype(BF16)


def main_table(length):
    n = np.arange(length)[:, None]
    m = np.arange(length * P_SIZE // Q)[None, :]
    return weight((m * Q - n * P_SIZE) / P_SIZE)


def edge_table(length, count):
    out_len = length * P_SIZE // Q
    assert count * REACH <= LANES // 2 and count * SPREAD <= LANES and REACH * P_SIZE <= SPREAD * Q
    table = np.zeros((LANES, 2 * LANES))
    k = np.arange(REACH)[:, None]
    m = np.arange(SPREAD)[None, :]
    before = weight((m * Q - (k - REACH) * P_SIZE) / P_SIZE)
    after = weight(((m + out_len - SPREAD) * Q - (length + k) * P_SIZE) / P_SIZE)
    for b in range(count):
        r, c = b * REACH, b * SPREAD
        table[r : r + REACH, c : c + SPREAD] = before
        r, c = r + LANES // 2, c + LANES
        table[r : r + REACH, c : c + SPREAD] = after
    return table


def split(values):
    high = values.astype(BF16)
    return high, (values - high.astype(F32)).astype(BF16)


def dot(a, b, precision=None):
    return jnp.dot(a, b, precision=precision, preferred_element_type=F32)


def rim_kernel(traces, steps_hbm, left_out, right_out, left, right, steps, sems):
    rows, cols, length = traces.shape
    copy_s = pltpu.make_async_copy(steps_hbm, steps, sems.at[2])
    copy_l = pltpu.make_async_copy(traces.at[:, 0:8, :], left, sems.at[0])
    copy_r = pltpu.make_async_copy(traces.at[:, cols - 8 : cols, :], right, sems.at[1])
    copy_s.start()
    copy_l.start()
    copy_r.start()
    copy_s.wait()
    step_il = steps[0]
    step_xl = steps[1]
    masks = {}
    for side, spots in ((-1, (0, 1)), (1, (cols - 2, cols - 1))):
        for j in spots:
            for shift in (-1, 0, 1):
                hit = (step_xl[:, j : j + 1] == side) & (step_il[:, j : j + 1] == shift)
                masks[side, j, shift] = hit.astype(F32)
    copy_l.wait()
    copy_r.wait()
    parts = []
    for shift in (-1, 0, 1):
        row = []
        for side, buf, spots in ((-1, left, ((0, 0), (1, 1))), (1, right, ((cols - 2, 6), (cols - 1, 7)))):
            total, count = None, None
            for j, place in spots:
                mask = masks[side, j, shift]
                term = buf[:, place, :] * mask
                total = term if total is None else total + term
                count = mask if count is None else count + mask
            row += [total, jnp.broadcast_to(count, (rows, LANES))]
        parts.append(jnp.concatenate(row, axis=1))
    stacked = jnp.concatenate(parts, axis=0)
    r = lax.broadcasted_iota(jnp.int32, (rows, 3 * rows), 0)
    k = lax.broadcasted_iota(jnp.int32, (rows, 3 * rows), 1)
    pick = ((k % rows) // 2 + k // rows == r).astype(F32)
    both = dot(pick, stacked, lax.Precision.HIGHEST)
    left_out[...] = both[:, : length + LANES]
    right_out[...] = both[:, length + LANES :]


def groups_of(cols):
    assert cols % 16 == 0 and cols >= LANES
    bins, most, out = cols // 2, LANES // 2 - 8, []
    for low in range(0, bins, most):
        high = min(bins, low + most)
        start = min(max((2 * low - 2) // 16 * 16, 0), cols - LANES)
        assert start <= max(2 * low - 2, 0) and min(2 * high + 2, cols) <= start + LANES
        out.append((low, high, start))
    return out


def bin_kernel(traces, steps, *refs):
    tables, (sums, first, last, *copies), (keys, counts, sems) = refs[:4], refs[4:11], refs[11:]
    loads = [pltpu.make_async_copy(a, b, sems.at[n]) for n, (a, b) in enumerate(zip(tables, copies))]
    for load in loads:
        load.start()
    rows, cols, length = traces.shape
    bins = cols // 2
    groups = groups_of(cols)
    column = lax.broadcasted_iota(jnp.int32, (rows, cols), 1) // 2 + steps[1]
    row = steps[0] + 1
    for g, (low, high, start) in enumerate(groups):
        here, there = column[:, start : start + LANES], row[:, start : start + LANES]
        inside = (here >= low) & (here < high)
        keys[g] = jnp.where(inside, there * (high - low) + here - low, -1)
    sums[...] = jnp.zeros(sums.shape, F32)
    counts[...] = jnp.zeros(counts.shape, F32)

    def body(a, _):
        parts = [split(traces[2 * a + p]) for p in (0, 1)]
        for g, (low, high, start) in enumerate(groups):
            n = high - low
            slot = lax.broadcasted_iota(jnp.int32, (pl.cdiv(3 * n, 16) * 16, LANES), 0)
            hots = [jnp.where(slot == keys[g, pl.ds(2 * a + p, 1), :], 1.0, 0.0).astype(F32) for p in (0, 1)]
            count = hots[0] + hots[1]
            hot = jnp.concatenate(hots, axis=1).astype(BF16)
            total = None
            for level in (0, 1):
                window = [parts[p][level][start : start + LANES] for p in (0, 1)]
                term = dot(hot, jnp.concatenate(window, axis=0))
                total = term if total is None else total + term
            for s in range(3):
                sums[a + s, low:high, :length] += total[s * n : (s + 1) * n]
                counts[a + s, low:high] += count[s * n : (s + 1) * n]
        return 0

    lax.fori_loop(0, rows // 2, body, 0, unroll=True)
    for r in range(rows // 2 + 2):
        whole = jnp.sum(counts[r], axis=1, keepdims=True)
        sums[r, :, length:] = jnp.broadcast_to(whole, (bins, LANES))
    lane = lax.broadcasted_iota(jnp.int32, (bins, LANES), 1)
    heads = jnp.zeros((bins, LANES), F32)
    tails = jnp.zeros((bins, LANES), F32)
    for b in range(rows // 2):
        here = lane // REACH == b
        heads = jnp.where(here, edges(sums[b + 1], length, b * REACH, False), heads)
        tails = jnp.where(here, edges(sums[b + 1], length, b * REACH, True), tails)
    first[...] = heads
    last[...] = tails
    for load in loads:
        load.wait()


def edges(plane, length, lane0, tail):
    if tail:
        return pltpu.roll(plane[:, length - LANES : length], (lane0 + REACH) % LANES, 1)
    return pltpu.roll(plane[:, :LANES], lane0, 1) if lane0 else plane[:, :LANES]


def join_xl_kernel(sums_in, from_left, from_right, first_in, last_in, sums, rim, first, last):
    rows, bins, width = sums.shape
    length = width - LANES
    xl = lax.axis_index("xl")
    low = lax.axis_index("il") == 0
    left = jnp.where(xl > 0, from_left[...], 0.0)
    right = jnp.where(xl < lax.axis_size("xl") - 1, from_right[...], 0.0)
    sub = lax.broadcasted_iota(jnp.int32, (8, width), 0)
    for values, place, base in ((left, 0, 0), (right, 7, bins - 8)):
        for r in range(rows):
            gain = jnp.where(sub == place, jnp.broadcast_to(values[r : r + 1], (8, width)), 0.0)
            sums[r, base : base + 8, :] = sums_in[r, base : base + 8, :] + gain
        lane = lax.broadcasted_iota(jnp.int32, (8, LANES), 1)
        tile = sub[:, :LANES]
        for old, new, tail in ((first_in, first, False), (last_in, last, True)):
            gain = jnp.zeros((8, LANES), F32)
            for b in range(rows - 2):
                moved = edges(values[b + 1 : b + 2], length, b * REACH, tail)
                gain = jnp.where(lane // REACH == b, jnp.broadcast_to(moved, (8, LANES)), gain)
            gain = jnp.where(tile == place, gain, 0.0)
            new[base : base + 8, :] = old[base : base + 8, :] + gain
    rim[...] = sums[jnp.where(low, rows - 1, 0)]


def join_il_kernel(first, last, got, one, two):
    bins, width = got.shape
    length = width - LANES
    low = lax.axis_index("il") == 0
    half = LANES // 2
    lane = lax.broadcasted_iota(jnp.int32, (bins, LANES), 1)
    values = []
    for old, tail in ((first, False), (last, True)):
        edge = edges(got[...], length, 0, tail)
        edge = jnp.where(low, pltpu.roll(edge, half - REACH, 1), edge)
        there = lane // REACH == jnp.where(low, half // REACH - 1, 0)
        values.append(packed(old[...] + jnp.where(there, edge, 0.0)))
    one[...] = jnp.where(low, values[1], values[0])
    two[...] = jnp.where(low, values[0], values[1])


def split_row(bins):
    return pl.cdiv(bins, 16) * 8


def packed(values):
    bins = values.shape[0]
    cut = split_row(bins)
    rest = jnp.concatenate([values[cut:], jnp.zeros((2 * cut - bins, LANES), F32)], axis=0)
    lane = lax.broadcasted_iota(jnp.int32, (cut, LANES), 1)
    return jnp.where(lane < LANES // 2, values[:cut], pltpu.roll(rest, LANES // 2, 1))


def unpacked(values, bins):
    return jnp.concatenate([values, pltpu.roll(values, LANES // 2, 1)[: bins - values.shape[0]]], axis=0)


def resampled(planes, table_h, table_l):
    count, bins, width = planes.shape
    length = width - LANES
    scale = 1.0 / jnp.maximum(planes[:, :, length:], 1.0)
    values = planes[:, :, :length] * jnp.concatenate([scale] * (length // LANES), axis=2)
    high, low = split(values.reshape(count * bins, length))
    out = dot(high, table_h) + dot(low, table_h) + dot(high, table_l)
    return out.reshape(count, bins, -1)


def write_middle(values, ends, middle, places, out, sem):
    ends[:, :, :LANES] = values[:, :, :LANES]
    ends[:, :, LANES:] = values[:, :, values.shape[2] - LANES :]
    middle[...] = values[:, :, LANES : values.shape[2] - LANES]
    copies = []
    for n, place in enumerate(places):
        copies.append(
            pltpu.make_async_copy(middle.at[n], out.at[place, :, LANES : out.shape[2] - LANES], sem.at[n])
        )
    for copy in copies:
        copy.start()
    for copy in copies:
        copy.wait()


def resample_inner_kernel(sums, table_h, table_l, out, ends, middle, sem):
    rows = sums.shape[0]
    values = resampled(sums[2 : rows - 2], table_h[...], table_l[...])
    write_middle(values, ends, middle, range(1, rows - 3), out, sem)


def resample_outer_kernel(out_in, sums, got, table_h, table_l, out, ends, folds, middle, sem):
    rows, _, width = sums.shape
    low = lax.axis_index("il") == 0
    rim = got[:, :width]
    first = sums[1] + jnp.where(low, 0.0, rim)
    last = sums[rows - 2] + jnp.where(low, rim, 0.0)
    folds[0] = first[:, width - LANES :]
    folds[1] = last[:, width - LANES :]
    values = resampled(jnp.stack([first, last]), table_h[...], table_l[...])
    write_middle(values, ends, middle, (0, rows - 3), out, sem)


def finish_kernel(out_in, sums, folds, inner, outer, one, two, table_h, table_l, out, ends, sem):
    rows, bins, width = sums.shape
    length = width - LANES
    count = rows - 2
    ta = lax.axis_index("ta")
    low = lax.axis_index("il") == 0
    half = LANES // 2
    before = jnp.where(low, one[...], two[...])
    after = jnp.where(low, two[...], one[...])
    before = unpacked(jnp.where(ta > 0, before, 0.0), bins)
    after = unpacked(jnp.where(ta < lax.axis_size("ta") - 1, after, 0.0), bins)
    lane = lax.broadcasted_iota(jnp.int32, (bins, LANES), 1)
    values = jnp.where(lane < half, before, pltpu.roll(after, half, 1))
    high, low_part = split(values)
    fix = dot(high, table_h[...]) + dot(low_part, table_h[...]) + dot(high, table_l[...])
    head, tail = fix[:, :LANES], fix[:, LANES:]
    copies = []
    for b in range(count):
        if b in (0, count - 1):
            base, fold = outer.at[0 if b == 0 else 1], folds[0 if b == 0 else 1]
        else:
            base, fold = inner.at[b - 1], sums[b + 1, :, length:]
        scale = 1.0 / jnp.maximum(fold, 1.0)
        moved = pltpu.roll(head, LANES - b * SPREAD, 1) if b else head
        ends[b, 0] = base[:, :LANES] + jnp.where(lane < SPREAD, moved, 0.0) * scale
        moved = pltpu.roll(tail, (2 * LANES - (b + 1) * SPREAD) % LANES, 1)
        ends[b, 1] = base[:, LANES:] + jnp.where(lane >= LANES - SPREAD, moved, 0.0) * scale
        for side, start in ((0, 0), (1, out.shape[2] - LANES)):
            copies.append(
                pltpu.make_async_copy(ends.at[b, side], out.at[b, :, start : start + LANES], sem.at[b, side])
            )
            copies[-1].start()
    for copy in copies:
        copy.wait()


VMEM = pl.BlockSpec(memory_space=pltpu.VMEM)
HBM = pl.BlockSpec(memory_space=pltpu.HBM)


def call(kernel, ins, outs, scratch=(), aliases={}):
    def run(*args):
        return pl.pallas_call(
            kernel,
            in_specs=ins,
            out_specs=[spec for spec, _ in outs],
            out_shape=[shape for _, shape in outs],
            scratch_shapes=list(scratch),
            input_output_aliases=aliases,
            compiler_params=pltpu.CompilerParams(vmem_limit_bytes=24 << 20),
        )(*args)

    return run


def in_hbm(values):
    return pltpu.with_memory_space_constraint(values, pltpu.HBM)


def vmem(*dims, kind=F32):
    return VMEM, jax.ShapeDtypeStruct(dims, kind)


def shards(sizes, traces, bin_steps):
    return steps_of(sizes, traces, bin_steps)


def steps_of(sizes, traces, bin_steps):
    _, n_xl, n_ta = sizes
    rows, cols, length = traces.shape
    half, bins = rows // 2, cols // 2
    width = length + LANES
    out_len = length * P_SIZE // Q
    main = split_table(main_table(length))
    edge = split_table(edge_table(length, half))
    dma = pltpu.SemaphoreType.DMA

    to_left, to_right = call(
        rim_kernel,
        [HBM, HBM],
        [vmem(rows, width)] * 2,
        [pltpu.VMEM((rows, 8, length), F32)] * 2 + [pltpu.VMEM(bin_steps.shape, jnp.int32), dma((3,))],
    )(in_hbm(traces), in_hbm(bin_steps))
    up = [(i, (i + 1) % n_xl) for i in range(n_xl)]
    down = [(j, i) for i, j in up]
    from_left = lax.ppermute(to_right, "xl", up)
    from_right = lax.ppermute(to_left, "xl", down)

    tables = (*main, *edge)
    sums, first, last, *tables = call(
        bin_kernel,
        [VMEM, VMEM] + [HBM] * 4,
        [vmem(half + 2, bins, width)] + [vmem(bins, LANES)] * 2 + [vmem(*t.shape, kind=BF16) for t in tables],
        [pltpu.VMEM((len(groups_of(cols)), rows, LANES), jnp.int32), pltpu.VMEM((half + 2, bins, LANES), F32), dma((4,))],
    )(traces, bin_steps, *[in_hbm(t) for t in tables])
    main, edge = tables[:2], tables[2:]
    sums, rim, first, last = call(
        join_xl_kernel,
        [VMEM] * 5,
        [vmem(half + 2, bins, width), vmem(bins, width)] + [vmem(bins, LANES)] * 2,
        aliases={0: 0, 3: 2, 4: 3},
    )(sums, from_left, from_right, first, last)

    swap = [(0, 1), (1, 0)]
    got = lax.ppermute(rim, "il", swap)
    whole = (HBM, jax.ShapeDtypeStruct((half, bins, out_len), F32))
    middle = out_len - 2 * LANES
    out, inner = call(
        resample_inner_kernel,
        [VMEM] * 3,
        [whole, vmem(half - 2, bins, 2 * LANES)],
        [pltpu.VMEM((half - 2, bins, middle), F32), dma((half - 2,))],
    )(sums, *main)
    one, two = call(join_il_kernel, [VMEM] * 3, [vmem(split_row(bins), LANES)] * 2)(first, last, got)

    trade = [(n_ta - 1, 2 * n_ta - 1), (n_ta, 0)]
    for t in range(n_ta - 1):
        trade += [(t, t + 1), (n_ta + t + 1, n_ta + t)]
    one = lax.ppermute(one, ("il", "ta"), trade)
    two = lax.ppermute(two, ("il", "ta"), [(j, i) for i, j in trade])
    out, outer, folds = call(
        resample_outer_kernel,
        [HBM] + [VMEM] * 4,
        [whole, vmem(2, bins, 2 * LANES), vmem(2, bins, LANES)],
        [pltpu.VMEM((2, bins, middle), F32), dma((2,))],
        {0: 0},
    )(out, sums, got, *main)
    (out,) = call(
        finish_kernel, [HBM] + [VMEM] * 8, [whole], [pltpu.VMEM((half, 2, bins, LANES), F32), dma((half, 2))], {0: 0}
    )(out, sums, folds, inner, outer, one, two, *edge)
    return out


def solution(mesh):
    sizes = tuple(mesh.shape[axis] for axis in ("il", "xl", "ta"))
    assert sizes[0] == 2
    return jax.shard_map(
        functools.partial(shards, sizes),
        mesh=mesh,
        in_specs=(P("il", "xl", "ta"), P(None, "il", "xl")),
        out_specs=P("il", "xl", "ta"),
        check_vma=False,
    )
```

time: 19.9 us -> 17.3 us (0.87)
  the two profiles are of different devices: /device:TPU:1 before, /device:TPU:0 now
where the time goes in v3:
time: 17.3 us; the launch traced here: 17.2 us
  Pallas kernels  7.81 us (45%)
  starting transfers between devices  5.69 us (33%)
  waiting for transfers between devices  3.63 us (21%)
    pallas_call x7, Pallas kernels, run(): pl.pallas_call(kernel, in_specs=ins, out_specs=[spec for spec, _ in outs]...  7.81 us
    ppermute x1, starting transfers between devices, steps_of(): from_left = lax.ppermute(to_right, 'xl', up)  3.02 us
    ppermute x1, starting transfers between devices, steps_of(): one = lax.ppermute(one, ('il', 'ta'), trade)  1.58 us
    ppermute x1, waiting for transfers between devices, steps_of(): two = lax.ppermute(two, ('il', 'ta'), [(j, i) for i, j in trade])  1.4 us
    ppermute x1, waiting for transfers between devices, steps_of(): got = lax.ppermute(rim, 'il', swap)  1.38 us
    ppermute x1, starting transfers between devices, steps_of(): from_right = lax.ppermute(to_left, 'xl', down)  1.02 us
    ppermute x1, waiting for transfers between devices, steps_of(): from_right = lax.ppermute(to_left, 'xl', down)  0.84 us
  transfers between devices with their start and end apart: 5, of which 3 were waited for; matrix products, arithmetic and copies ran while one was open for 0% of the time, Pallas kernels for 25%

profile of v3, /device:TPU:0, one launch (start us, length us, event | category | flops | bytes accessed | tf_op | source)
XLA Modules:
  0.0 17.2 jit_solution(6958819010803437433)
XLA Ops:
  0.0 0.0 copy-start.1
  0.0 0.0 copy-start
  0.0 1.5 %shard_map.65 = (f32[16,384]{1,0:T(8,128)S(1)}, f32[16,384]{1,0:T(8,128)S(1)}) custom-call(f32[16,208,256]{2,1,0:T(8,128)} %traces.3, s32[2,16,208]{2,1,0:T(8,128)} %steps_hbm.1), custom_call_target="tpu_custom_call" | custom-call | tf_op jit(solution)/shard_map/pallas_call | solution.py:313
  1.5 3.0 %collective-permute-start = (f32[16,384]{1,0:T(8,128)S(1)}, f32[16,384]{1,0:T(8,128)S(1)}, u32[]{:S(2)}, u32[]{:S(2)}) collective-permute-start(f32[16,384]{1,0:T(8,128)S(1)} %get-tuple-element.26), channel_id=1, source_target_pairs={{0,4},{4,8},{8,12},{12,0},{1,5},{5,9},{9,13},{13,1},{2,6},{6,10},{... | collective-permute-start | bytes 73736 | tf_op jit(solution)/shard_map/ppermute | solution.py:356
  4.5 1.0 %collective-permute-start.1 = (f32[16,384]{1,0:T(8,128)S(1)}, f32[16,384]{1,0:T(8,128)S(1)}, u32[]{:S(2)}, u32[]{:S(2)}) collective-permute-start(f32[16,384]{1,0:T(8,128)S(1)} %get-tuple-element.27), channel_id=1, source_target_pairs={{4,0},{8,4},{12,8},{0,12},{5,1},{9,5},{13,9},{1,13},{6,2},{10,6},{... | collective-permute-start | bytes 73736 | tf_op jit(solution)/shard_map/ppermute | solution.py:357
  5.5 0.0 copy-done.1
  5.5 0.0 copy-done
  5.5 1.9 %shard_map.64 = (f32[10,104,384]{2,1,0:T(8,128)S(1)}, f32[104,128]{1,0:T(8,128)S(1)}, f32[104,128]{1,0:T(8,128)S(1)}, bf16[256,384]{1,0:T(8,128)(2,1)S(1)}, bf16...) custom-call(f32[16,208,256]{2,1,0:T(8,128)S(1)} %copy-done, ...), custom_call_target="tpu_custom_call" | custom-call | tf_op jit(solution)/shard_map/pallas_call | solution.py:313
  7.5 0.0 collective-permute-done.from_left
  7.5 0.8 %collective-permute-done.1.from_right = f32[16,384]{1,0:T(8,128)S(1)} collective-permute-done((f32[16,384]{1,0:T(8,128)S(1)}, f32[16,384]{1,0:T(8,128)S(1)}, u32[]{:S(2)}, u32[]{:S(2)}) %collective-permute-start.1) | collective-permute-done | bytes 24608 | tf_op jit(solution)/shard_map/ppermute | solution.py:357
  8.3 0.2 shard_map.66
  8.5 0.1 collective-permute-start.2
  8.6 1.4 %collective-permute-done.2.got = f32[104,384]{1,0:T(8,128)S(1)} collective-permute-done((f32[104,384]{1,0:T(8,128)S(1)}, f32[104,384]{1,0:T(8,128)S(1)}, u32[]{:S(2)}, u32[]{:S(2)}) %collective-permute-start.2) | collective-permute-done | bytes 159776 | tf_op jit(solution)/shard_map/ppermute | solution.py:375
  10.0 0.2 %shard_map.69 = (f32[56,128]{1,0:T(8,128)S(1)}, f32[56,128]{1,0:T(8,128)S(1)}) custom-call(f32[104,128]{1,0:T(8,128)S(1)} %get-tuple-element.39.first, f32[104,128]{1,0:T(8,128)S(1)} %get-tuple-element.40.last, f32[104,384]{1,0:T(8,128)S(1)} %collective-permute-done.2.got), custom_call_target="tpu_custom_call" | custom-call | tf_op jit(solution)/shard_map/pallas_call | solution.py:313
  10.2 1.6 %collective-permute-start.3 = (f32[56,128]{1,0:T(8,128)S(1)}, f32[56,128]{1,0:T(8,128)S(1)}, u32[]{:S(2)}, u32[]{:S(2)}) collective-permute-start(f32[56,128]{1,0:T(8,128)S(1)} %get-tuple-element.41), channel_id=1, source_target_pairs={{3,19},{16,0},{0,1},{17,16},{1,2},{18,17},{2,3},{19,18},{7,23},{20... | collective-permute-start | bytes 86024 | tf_op jit(solution)/shard_map/ppermute | solution.py:389
  11.8 0.0 collective-permute-start.4
  11.8 1.4 %shard_map.67 = (f32[8,104,384]{2,1,0:T(8,128)}, f32[6,104,256]{2,1,0:T(8,128)S(1)}) custom-call(f32[10,104,384]{2,1,0:T(8,128)S(1)} %get-tuple-element.30.sums, bf16[256,384]{1,0:T(8,128)(2,1)S(1)} %get-tuple-element.31.table_h, bf16[256,384]{1,0:T(8,128)(2,1)S(1)} %get-tuple-element.32.table_l), custom_call_target="tpu_custom_call" | custom-call | tf_op jit(solution)/shard_map/pallas_call | solution.py:313
  13.2 1.0 %shard_map.68 = (f32[8,104,384]{2,1,0:T(8,128)}, f32[2,104,256]{2,1,0:T(8,128)S(1)}, f32[2,104,128]{2,1,0:T(8,128)S(1)}) custom-call(f32[8,104,384]{2,1,0:T(8,128)} %get-tuple-element.33.out_in, f32[10,104,384]{2,1,0:T(8,128)S(1)} %get-tuple-element.30.sums, f32[104,384]{1,0:T(8,128)S(1)} %collective-permute-done.2.got, ...), custom_call_target="tpu_custom_call", output_to_operand_aliasing={{0}: (0, {})} | custom-call | tf_op jit(solution)/shard_map/pallas_call | solution.py:313
  14.2 0.0 collective-permute-done.3.one
  14.2 1.4 %collective-permute-done.4.two = f32[56,128]{1,0:T(8,128)S(1)} collective-permute-done((f32[56,128]{1,0:T(8,128)S(1)}, f32[56,128]{1,0:T(8,128)S(1)}, u32[]{:S(2)}, u32[]{:S(2)}) %collective-permute-start.4) | collective-permute-done | bytes 28704 | tf_op jit(solution)/shard_map/ppermute | solution.py:390
  15.6 1.6 %shard_map.70 = f32[8,104,384]{2,1,0:T(8,128)} custom-call(f32[8,104,384]{2,1,0:T(8,128)} %get-tuple-element.35.out_in, f32[10,104,384]{2,1,0:T(8,128)S(1)} %get-tuple-element.30.sums, f32[2,104,128]{2,1,0:T(8,128)S(1)} %get-tuple-element.36.folds, f32[6,104,256]{2,1,0:T(8,128)S(1)} %get-tuple-element.37.inner, ...), custom_call_target="tpu_custom_call", output_to_operand_aliasing={{}: (0, {})} | custom-call | tf_op jit(solution)/shard_map/pallas_call | solution.py:313
Async XLA Ops:
  0.0 5.5 %copy-start.1 = (s32[2,16,208]{2,1,0:T(8,128)S(1)}, s32[2,16,208]{2,1,0:T(8,128)}, u32[]{:S(2)}) copy-start(s32[2,16,208]{2,1,0:T(8,128)} %steps_hbm.1) | copy-start | bytes 79876
  0.0 5.5 %copy-start = (f32[16,208,256]{2,1,0:T(8,128)S(1)}, f32[16,208,256]{2,1,0:T(8,128)}, u32[]{:S(2)}) copy-start(f32[16,208,256]{2,1,0:T(8,128)} %traces.3) | copy-start | bytes 10223620
  1.5 6.0 %collective-permute-start = (f32[16,384]{1,0:T(8,128)S(1)}, f32[16,384]{1,0:T(8,128)S(1)}, u32[]{:S(2)}, u32[]{:S(2)}) collective-permute-start(f32[16,384]{1,0:T(8,128)S(1)} %get-tuple-element.26), channel_id=1, source_target_pairs={{0,4},{4,8},{8,12},{12,0},{1,5},{5,9},{9,13},{13,1},{2,6},{6,10},{... | collective-permute-start | bytes 73736 | tf_op jit(solution)/shard_map/ppermute | solution.py:356
  4.5 3.8 %collective-permute-start.1 = (f32[16,384]{1,0:T(8,128)S(1)}, f32[16,384]{1,0:T(8,128)S(1)}, u32[]{:S(2)}, u32[]{:S(2)}) collective-permute-start(f32[16,384]{1,0:T(8,128)S(1)} %get-tuple-element.27), channel_id=1, source_target_pairs={{4,0},{8,4},{12,8},{0,12},{5,1},{9,5},{13,9},{1,13},{6,2},{10,6},{... | collective-permute-start | bytes 73736 | tf_op jit(solution)/shard_map/ppermute | solution.py:357
  8.5 1.5 %collective-permute-start.2 = (f32[104,384]{1,0:T(8,128)S(1)}, f32[104,384]{1,0:T(8,128)S(1)}, u32[]{:S(2)}, u32[]{:S(2)}) collective-permute-start(f32[104,384]{1,0:T(8,128)S(1)} %get-tuple-element.34), channel_id=1, source_target_pairs={{0,16},{16,0},{1,17},{17,1},{2,18},{18,2},{3,19},{19,3},{4,20},{20... | collective-permute-start | bytes 479240 | tf_op jit(solution)/shard_map/ppermute | solution.py:375
  10.2 4.0 %collective-permute-start.3 = (f32[56,128]{1,0:T(8,128)S(1)}, f32[56,128]{1,0:T(8,128)S(1)}, u32[]{:S(2)}, u32[]{:S(2)}) collective-permute-start(f32[56,128]{1,0:T(8,128)S(1)} %get-tuple-element.41), channel_id=1, source_target_pairs={{3,19},{16,0},{0,1},{17,16},{1,2},{18,17},{2,3},{19,18},{7,23},{20... | collective-permute-start | bytes 86024 | tf_op jit(solution)/shard_map/ppermute | solution.py:389
  11.8 3.9 %collective-permute-start.4 = (f32[56,128]{1,0:T(8,128)S(1)}, f32[56,128]{1,0:T(8,128)S(1)}, u32[]{:S(2)}, u32[]{:S(2)}) collective-permute-start(f32[56,128]{1,0:T(8,128)S(1)} %get-tuple-element.42), channel_id=1, source_target_pairs={{19,3},{0,16},{1,0},{16,17},{2,1},{17,18},{3,2},{18,19},{23,7},{4,... | collective-permute-start | bytes 86024 | tf_op jit(solution)/shard_map/ppermute | solution.py:390

commit v4 on v3

v4 whole, which is shorter than its diff:
```python
import functools

import jax
import jax.numpy as jnp
import numpy as np
from jax import lax
from jax.experimental import pallas as pl
from jax.experimental.pallas import tpu as pltpu
from jax.sharding import PartitionSpec as P


TAPS = 16
P_SIZE = 3
Q = 2
REACH = TAPS // 2
LANES = 128
F32 = jnp.float32
BF16 = jnp.bfloat16
SPREAD = 16


def weight(x):
    inside = np.abs(x) < REACH
    return np.where(inside, np.sinc(x) * np.sinc(x / REACH), 0.0)


def split_table(table):
    high = table.astype(BF16)
    return high, (table - high.astype(np.float64)).astype(BF16)


def main_table(length):
    n = np.arange(length)[:, None]
    m = np.arange(length * P_SIZE // Q)[None, :]
    return weight((m * Q - n * P_SIZE) / P_SIZE)


def edge_table(length, count):
    out_len = length * P_SIZE // Q
    assert count * REACH <= LANES // 2 and count * SPREAD <= LANES and REACH * P_SIZE <= SPREAD * Q
    table = np.zeros((2, LANES, LANES))
    k = np.arange(REACH)[:, None]
    m = np.arange(SPREAD)[None, :]
    before = weight((m * Q - (k - REACH) * P_SIZE) / P_SIZE)
    after = weight(((m + out_len - SPREAD) * Q - (length + k) * P_SIZE) / P_SIZE)
    for b in range(count):
        r, c = b * REACH, b * SPREAD
        table[0, r : r + REACH, c : c + SPREAD] = before
        table[1, r : r + REACH, c : c + SPREAD] = after
    return table


def split(values):
    high = values.astype(BF16)
    return high, (values - high.astype(F32)).astype(BF16)


def dot(a, b, precision=None):
    return jnp.dot(a, b, precision=precision, preferred_element_type=F32)


def rim_kernel(traces, steps_hbm, keep, give, left, right, steps, sems):
    rows, cols, length = traces.shape
    copies = (
        pltpu.make_async_copy(steps_hbm, steps, sems.at[2]),
        pltpu.make_async_copy(traces.at[:, 0:8, :], left, sems.at[0]),
        pltpu.make_async_copy(traces.at[:, cols - 8 : cols, :], right, sems.at[1]),
    )
    for copy in copies:
        copy.start(priority=1)
    low = lax.axis_index("il") == 0
    g = lax.broadcasted_iota(jnp.int32, (rows, 6 * rows), 0) + jnp.where(low, 1, 1 - rows // 2)
    k = lax.broadcasted_iota(jnp.int32, (rows, 6 * rows), 1) % (3 * rows)
    pick = ((k % rows) // 2 + k // rows == g).astype(F32).astype(BF16)
    copies[0].wait()
    step_il = steps[0]
    step_xl = steps[1]
    masks = {}
    for side, spots in ((-1, (0, 1)), (1, (cols - 2, cols - 1))):
        for j in spots:
            for shift in (-1, 0, 1):
                hit = (step_xl[:, j : j + 1] == side) & (step_il[:, j : j + 1] == shift)
                masks[side, j, shift] = hit.astype(F32)
    copies[1].wait()
    copies[2].wait()
    sides = []
    for side, buf, spots in ((-1, left, ((0, 0), (1, 1))), (1, right, ((cols - 2, 6), (cols - 1, 7)))):
        parts = []
        for shift in (-1, 0, 1):
            total, count = None, None
            for j, place in spots:
                mask = masks[side, j, shift]
                term = buf[:, place, :] * mask
                total = term if total is None else total + term
                count = mask if count is None else count + mask
            parts.append(jnp.concatenate([total, jnp.broadcast_to(count, (rows, LANES))], axis=1))
        sides.append(jnp.concatenate(parts, axis=0))
    both = dot(pick, jnp.concatenate(split(jnp.concatenate(sides, axis=1)), axis=0))
    to_left, to_right = both[:, : length + LANES], both[:, length + LANES :]
    keep[...] = jnp.where(low, to_right, to_left)
    give[...] = jnp.where(low, to_left, to_right)


def groups_of(cols):
    assert cols % 16 == 0 and cols >= LANES
    bins, most, out = cols // 2, LANES // 2 - 8, []
    for low in range(0, bins, most):
        high = min(bins, low + most)
        start = min(max((2 * low - 2) // 16 * 16, 0), cols - LANES)
        assert start <= max(2 * low - 2, 0) and min(2 * high + 2, cols) <= start + LANES
        out.append((low, high, start))
    return out


def bin_kernel(traces, steps, *refs):
    tables, (sums, first, last, *copies), (keys, counts, sems) = refs[:4], refs[4:11], refs[11:]
    loads = [pltpu.make_async_copy(a, b, sems.at[n]) for n, (a, b) in enumerate(zip(tables, copies))]
    for load in loads:
        load.start()
    rows, cols, length = traces.shape
    bins = cols // 2
    groups = groups_of(cols)
    column = lax.broadcasted_iota(jnp.int32, (rows, cols), 1) // 2 + steps[1]
    row = steps[0] + 1
    for g, (low, high, start) in enumerate(groups):
        here, there = column[:, start : start + LANES], row[:, start : start + LANES]
        inside = (here >= low) & (here < high)
        keys[g] = jnp.where(inside, there * (high - low) + here - low, -1)
    sums[...] = jnp.zeros(sums.shape, F32)
    counts[...] = jnp.zeros(counts.shape, F32)

    def body(a, _):
        parts = [split(traces[2 * a + p]) for p in (0, 1)]
        for g, (low, high, start) in enumerate(groups):
            n = high - low
            slot = lax.broadcasted_iota(jnp.int32, (pl.cdiv(3 * n, 16) * 16, LANES), 0)
            hots = [jnp.where(slot == keys[g, pl.ds(2 * a + p, 1), :], 1.0, 0.0).astype(F32) for p in (0, 1)]
            count = hots[0] + hots[1]
            hot = jnp.concatenate(hots, axis=1).astype(BF16)
            total = None
            for level in (0, 1):
                window = [parts[p][level][start : start + LANES] for p in (0, 1)]
                term = dot(hot, jnp.concatenate(window, axis=0))
                total = term if total is None else total + term
            for s in range(3):
                sums[a + s, low:high, :length] += total[s * n : (s + 1) * n]
                counts[a + s, low:high] += count[s * n : (s + 1) * n]
        return 0

    lax.fori_loop(0, rows // 2, body, 0, unroll=True)
    for r in range(rows // 2 + 2):
        whole = jnp.sum(counts[r], axis=1, keepdims=True)
        sums[r, :, length:] = jnp.broadcast_to(whole, (bins, LANES))
    lane = lax.broadcasted_iota(jnp.int32, (bins, LANES), 1)
    heads = jnp.zeros((bins, LANES), F32)
    tails = jnp.zeros((bins, LANES), F32)
    for b in range(rows // 2):
        here = lane // REACH == b
        heads = jnp.where(here, edges(sums[b + 1], length, b * REACH, False), heads)
        tails = jnp.where(here, edges(sums[b + 1], length, b * REACH, True), tails)
    first[...] = heads
    last[...] = tails
    for load in loads:
        load.wait()


def edges(plane, length, lane0, tail):
    if tail:
        return pltpu.roll(plane[:, length - LANES : length], (lane0 + REACH) % LANES, 1)
    return pltpu.roll(plane[:, :LANES], lane0, 1) if lane0 else plane[:, :LANES]


def add_column(values, at_start, sums, first, last):
    rows, bins, width = sums.shape
    length = width - LANES
    sub = lax.broadcasted_iota(jnp.int32, (8, width), 0)
    place = jnp.where(at_start, 0, 7)
    base = pl.multiple_of(jnp.where(at_start, 0, bins - 8), 8)
    there = sub == place
    for b in range(rows - 2):
        gain = jnp.where(there, jnp.broadcast_to(values[b : b + 1], (8, width)), 0.0)
        sums[b + 1, pl.ds(base, 8), :] += gain
    lane = lax.broadcasted_iota(jnp.int32, (8, LANES), 1)
    for edge, tail in ((first, False), (last, True)):
        gain = jnp.zeros((8, LANES), F32)
        for b in range(rows - 2):
            row = edges(values[b : b + 1], length, b * REACH, tail)
            gain = jnp.where(lane // REACH == b, jnp.broadcast_to(row, (8, LANES)), gain)
        edge[pl.ds(base, 8), :] += jnp.where(there[:, :LANES], gain, 0.0)


def join_xl_kernel(sums_in, got, first_in, last_in, sums, payload, first, last):
    rows, bins, _ = sums.shape
    xl = lax.axis_index("xl")
    low = lax.axis_index("il") == 0
    there = jnp.where(low, xl > 0, xl < lax.axis_size("xl") - 1)
    count = rows - 2
    values = jnp.where(there, got[...], 0.0)
    payload[:bins, :] = sums[jnp.where(low, rows - 1, 0)]
    payload[bins:, :] = jnp.where(low, values[count:], values[:count])
    add_column(jnp.where(low, values[:count], values[count:]), low, sums, first, last)


def join_il_kernel(sums_in, first_in, last_in, got, sums, first, last, one, two):
    rows, bins, width = sums.shape
    length = width - LANES
    low = lax.axis_index("il") == 0
    half = LANES // 2
    add_column(got[bins:], ~low, sums, first, last)
    rim = got[:bins]
    sums[jnp.where(low, rows - 2, 1)] += rim
    lane = lax.broadcasted_iota(jnp.int32, (bins, LANES), 1)
    values = []
    for old, tail in ((first, False), (last, True)):
        edge = edges(rim, length, 0, tail)
        edge = jnp.where(low, pltpu.roll(edge, half - REACH, 1), edge)
        there = lane // REACH == jnp.where(low, half // REACH - 1, 0)
        values.append(packed(old[...] + jnp.where(there, edge, 0.0)))
    one[...] = jnp.where(low, values[1], values[0])
    two[...] = jnp.where(low, values[0], values[1])


def split_row(bins):
    return pl.cdiv(bins, 16) * 8


def packed(values):
    bins = values.shape[0]
    cut = split_row(bins)
    rest = jnp.concatenate([values[cut:], jnp.zeros((2 * cut - bins, LANES), F32)], axis=0)
    lane = lax.broadcasted_iota(jnp.int32, (cut, LANES), 1)
    return jnp.where(lane < LANES // 2, values[:cut], pltpu.roll(rest, LANES // 2, 1))


def unpacked(values, bins):
    return jnp.concatenate([values, pltpu.roll(values, LANES // 2, 1)[: bins - values.shape[0]]], axis=0)


def resample_kernel(sums, table_h, table_l, out, ends, scales, middle, sem):
    rows, bins, width = sums.shape
    length = width - LANES
    count = rows - 2
    out_len = out.shape[2]
    step = 2
    copies = []
    for start in range(0, count, step):
        planes = sums[start + 1 : start + 1 + step]
        scale = 1.0 / jnp.maximum(planes[:, :, length:], 1.0)
        scales[start : start + step] = scale
        values = planes[:, :, :length] * jnp.concatenate([scale] * (length // LANES), axis=2)
        high, low = split(values.reshape(step * bins, length))
        got = dot(high, table_h[...]) + dot(low, table_h[...]) + dot(high, table_l[...])
        got = got.reshape(step, bins, out_len)
        middle[start : start + step] = got[:, :, LANES : out_len - LANES]
        copies.append(
            pltpu.make_async_copy(
                middle.at[start : start + step],
                out.at[start : start + step, :, LANES : out_len - LANES],
                sem.at[start // step],
            )
        )
        copies[-1].start()
        ends[start : start + step, :, :LANES] = got[:, :, :LANES]
        ends[start : start + step, :, LANES:] = got[:, :, out_len - LANES :]
    for copy in copies:
        copy.wait()


def finish_kernel(first_trade, out_in, ends, scales, got, table_h, table_l, out, piece, sem):
    count, bins, _ = ends.shape
    ta = lax.axis_index("ta")
    low = lax.axis_index("il") == 0
    before = low if first_trade else ~low
    there = jnp.where(before, ta > 0, ta < lax.axis_size("ta") - 1)
    values = unpacked(jnp.where(there, got[...], 0.0), bins)
    high, low_part = split(values)
    side = jnp.where(before, 0, 1)
    start_h, start_l = table_h[side], table_l[side]
    fix = dot(high, start_h) + dot(low_part, start_h) + dot(high, start_l)
    fix = jnp.where(before, fix, pltpu.roll(fix, LANES - SPREAD, 1))
    lane = lax.broadcasted_iota(jnp.int32, (bins, LANES), 1)
    here = jnp.where(before, lane, LANES - 1 - lane) < SPREAD
    start = pl.multiple_of(jnp.where(before, 0, out.shape[2] - LANES), LANES)
    copies = []
    for b in range(count):
        base = jnp.where(before, ends[b, :, :LANES], ends[b, :, LANES:])
        moved = pltpu.roll(fix, LANES - b * SPREAD, 1) if b else fix
        piece[b] = base + jnp.where(here, moved, 0.0) * scales[b]
        copies.append(pltpu.make_async_copy(piece.at[b], out.at[b, :, pl.ds(start, LANES)], sem.at[b]))
        copies[-1].start()
    for copy in copies:
        copy.wait()


VMEM = pl.BlockSpec(memory_space=pltpu.VMEM)
HBM = pl.BlockSpec(memory_space=pltpu.HBM)


def call(kernel, ins, outs, scratch=(), aliases={}):
    def run(*args):
        return pl.pallas_call(
            kernel,
            in_specs=ins,
            out_specs=[spec for spec, _ in outs],
            out_shape=[shape for _, shape in outs],
            scratch_shapes=list(scratch),
            input_output_aliases=aliases,
            compiler_params=pltpu.CompilerParams(vmem_limit_bytes=24 << 20),
        )(*args)

    return run


def in_hbm(values):
    return pltpu.with_memory_space_constraint(values, pltpu.HBM)


def vmem(*dims, kind=F32):
    return VMEM, jax.ShapeDtypeStruct(dims, kind)


def shards(sizes, traces, bin_steps):
    return steps_of(sizes, traces, bin_steps)


def steps_of(sizes, traces, bin_steps):
    _, n_xl, n_ta = sizes
    rows, cols, length = traces.shape
    half, bins = rows // 2, cols // 2
    width = length + LANES
    out_len = length * P_SIZE // Q
    main = split_table(main_table(length))
    edge = split_table(edge_table(length, half))
    dma = pltpu.SemaphoreType.DMA

    keep, give = call(
        rim_kernel,
        [HBM, HBM],
        [vmem(rows, width)] * 2,
        [pltpu.VMEM((rows, 8, length), F32)] * 2 + [pltpu.VMEM(bin_steps.shape, jnp.int32), dma((3,))],
    )(in_hbm(traces), in_hbm(bin_steps))
    swap = [(0, 1), (1, 0)]
    chip_rims = keep + lax.ppermute(give, "il", swap)
    came = lax.ppermute(chip_rims, ("il", "xl"), turning(n_xl))

    tables = (*main, *edge)
    sums, first, last, *tables = call(
        bin_kernel,
        [VMEM, VMEM] + [HBM] * 4,
        [vmem(half + 2, bins, width)] + [vmem(bins, LANES)] * 2 + [vmem(*t.shape, kind=BF16) for t in tables],
        [pltpu.VMEM((len(groups_of(cols)), rows, LANES), jnp.int32), pltpu.VMEM((half + 2, bins, LANES), F32), dma((4,))],
    )(traces, bin_steps, *[in_hbm(t) for t in tables])
    main, edge = tables[:2], tables[2:]
    sums, payload, first, last = call(
        join_xl_kernel,
        [VMEM] * 4,
        [vmem(half + 2, bins, width), vmem(bins + half, width)] + [vmem(bins, LANES)] * 2,
        aliases={0: 0, 2: 2, 3: 3},
    )(sums, came, first, last)
    got = lax.ppermute(payload, "il", swap)
    sums, first, last, one, two = call(
        join_il_kernel,
        [VMEM] * 4,
        [vmem(half + 2, bins, width)] + [vmem(bins, LANES)] * 2 + [vmem(split_row(bins), LANES)] * 2,
        aliases={0: 0, 1: 1, 2: 2},
    )(sums, first, last, got)
    one = lax.ppermute(one, ("il", "ta"), turning(n_ta))
    two = lax.ppermute(two, ("il", "ta"), [(j, i) for i, j in turning(n_ta)])

    whole = (HBM, jax.ShapeDtypeStruct((half, bins, out_len), F32))
    out, ends, scales = call(
        resample_kernel,
        [VMEM] * 3,
        [whole, vmem(half, bins, 2 * LANES), vmem(half, bins, LANES)],
        [pltpu.VMEM((half, bins, out_len - 2 * LANES), F32), dma((half // 2,))],
    )(sums, *main)
    for first_trade, halo in ((True, one), (False, two)):
        (out,) = call(
            functools.partial(finish_kernel, first_trade),
            [HBM] + [VMEM] * 5,
            [whole],
            [pltpu.VMEM((half, bins, LANES), F32), dma((half,))],
            {0: 0},
        )(out, ends, scales, halo, *edge)
    return out


def turning(count):
    pairs = [(count - 1, 2 * count - 1), (count, 0)]
    for i in range(count - 1):
        pairs += [(i, i + 1), (count + i + 1, count + i)]
    return pairs


def solution(mesh):
    sizes = tuple(mesh.shape[axis] for axis in ("il", "xl", "ta"))
    assert sizes[0] == 2
    return jax.shard_map(
        functools.partial(shards, sizes),
        mesh=mesh,
        in_specs=(P("il", "xl", "ta"), P(None, "il", "xl")),
        out_specs=P("il", "xl", "ta"),
        check_vma=False,
    )
```

time: 17.3 us -> 16.3 us (0.942)
  starting transfers between devices: 5.69 us -> 5.04 us
  waiting for transfers between devices: 3.63 us -> 3.33 us
    ppermute x5, starting transfers between devices: 5.69 us -> 5.04 us  [the longest x1 2.82 us: steps_of(): came = lax.ppermute(chip_rims, ('il', 'xl'), turning(n_xl))]
    ppermute x5, waiting for transfers between devices: 3.63 us -> 3.33 us  [the longest x1 1.39 us: steps_of(): got = lax.ppermute(payload, 'il', swap)]
  transfers between devices with their start and end apart: 5 -> 5, of which waited for: 3 -> 3; matrix products, arithmetic and copies ran while one was open for 0% -> 0% of each run, Pallas kernels for 25% -> 29%
where the time goes in v4:
time: 16.3 us; the launch traced here: 16.2 us
  Pallas kernels  7.73 us (47%)
  starting transfers between devices  5.04 us (31%)
  waiting for transfers between devices  3.33 us (20%)
    pallas_call x7, Pallas kernels, run(): pl.pallas_call(kernel, in_specs=ins, out_specs=[spec for spec, _ in outs]...  7.73 us
    ppermute x1, starting transfers between devices, steps_of(): came = lax.ppermute(chip_rims, ('il', 'xl'), turning(n_xl))  2.82 us
    ppermute x1, starting transfers between devices, steps_of(): one = lax.ppermute(one, ('il', 'ta'), turning(n_ta))  1.58 us
    ppermute x1, waiting for transfers between devices, steps_of(): got = lax.ppermute(payload, 'il', swap)  1.39 us
    ppermute x1, waiting for transfers between devices, steps_of(): two = lax.ppermute(two, ('il', 'ta'), [(j, i) for i, j in turning(n_ta)])  1.04 us
    ppermute x1, waiting for transfers between devices, steps_of(): chip_rims = keep + lax.ppermute(give, 'il', swap)  0.85 us
    ppermute x1, starting transfers between devices, steps_of(): chip_rims = keep + lax.ppermute(give, 'il', swap)  0.56 us
  transfers between devices with their start and end apart: 5, of which 3 were waited for; matrix products, arithmetic and copies ran while one was open for 0% of the time, Pallas kernels for 29%

profile of v4, /device:TPU:0, one launch (start us, length us, event | category | flops | bytes accessed | tf_op | source)
XLA Modules:
  0.0 16.2 jit_solution(4141335942986733049)
XLA Ops:
  0.0 0.0 copy-start.1
  0.0 0.0 copy-start
  0.0 1.4 %shard_map.65 = (f32[16,384]{1,0:T(8,128)S(1)}, f32[16,384]{1,0:T(8,128)S(1)}) custom-call(f32[16,208,256]{2,1,0:T(8,128)} %traces.3, s32[2,16,208]{2,1,0:T(8,128)} %steps_hbm.1), custom_call_target="tpu_custom_call" | custom-call | tf_op jit(solution)/shard_map/pallas_call | solution.py:301
  1.5 0.6 %collective-permute-start = (f32[16,384]{1,0:T(8,128)S(1)}, f32[16,384]{1,0:T(8,128)S(1)}, u32[]{:S(2)}, u32[]{:S(2)}) collective-permute-start(f32[16,384]{1,0:T(8,128)S(1)} %get-tuple-element.26), channel_id=1, source_target_pairs={{0,16},{16,0},{1,17},{17,1},{2,18},{18,2},{3,19},{19,3},{4,20},{20... | collective-permute-start | bytes 73736 | tf_op jit(solution)/shard_map/ppermute | solution.py:343
  2.0 0.8 %collective-permute-done = f32[16,384]{1,0:T(8,128)S(1)} collective-permute-done((f32[16,384]{1,0:T(8,128)S(1)}, f32[16,384]{1,0:T(8,128)S(1)}, u32[]{:S(2)}, u32[]{:S(2)}) %collective-permute-start) | collective-permute-done | bytes 24608 | tf_op jit(solution)/shard_map/ppermute | solution.py:343
  2.9 2.8 %collective-permute-start.1 = (f32[16,384]{1,0:T(8,128)S(1)}, f32[16,384]{1,0:T(8,128)S(1)}, u32[]{:S(2)}, u32[]{:S(2)}) collective-permute-start(f32[16,384]{1,0:T(8,128)S(1)} %add.3), channel_id=1, source_target_pairs={{12,28},{16,0},{0,4},{20,16},{4,8},{24,20},{8,12},{28,24},{13,29},... | collective-permute-start | bytes 73736 | tf_op jit(solution)/shard_map/ppermute | solution.py:344
  5.7 0.0 copy-done.1
  5.7 0.0 copy-done
  5.7 1.9 %shard_map.64 = (f32[10,104,384]{2,1,0:T(8,128)S(1)}, f32[104,128]{1,0:T(8,128)S(1)}, f32[104,128]{1,0:T(8,128)S(1)}, bf16[256,384]{1,0:T(8,128)(2,1)S(1)}, bf16...) custom-call(f32[16,208,256]{2,1,0:T(8,128)S(1)} %copy-done, ...), custom_call_target="tpu_custom_call" | custom-call | tf_op jit(solution)/shard_map/pallas_call | solution.py:301
  7.6 0.0 collective-permute-done.1.got
  7.7 0.1 shard_map.66
  7.8 0.1 collective-permute-start.2
  7.8 1.4 %collective-permute-done.2.got = f32[112,384]{1,0:T(8,128)S(1)} collective-permute-done((f32[112,384]{1,0:T(8,128)S(1)}, f32[112,384]{1,0:T(8,128)S(1)}, u32[]{:S(2)}, u32[]{:S(2)}) %collective-permute-start.2) | collective-permute-done | bytes 172064 | tf_op jit(solution)/shard_map/ppermute | solution.py:360
  9.2 0.2 %shard_map.67 = (f32[10,104,384]{2,1,0:T(8,128)S(1)}, f32[104,128]{1,0:T(8,128)S(1)}, f32[104,128]{1,0:T(8,128)S(1)}, f32[56,128]{1,0:T(8,128)S(1)}, f32[56,128]{1,0:T(8,128)S(1)}) custom-call(f32[10,104,384]{2,1,0:T(8,128)S(1)} %get-tuple-element.29.sums_in, ...), custom_call_target="tpu_custom_call", output_to_operand_aliasing={{0}: (0, {}), {1}: (1, {}), {2}: (2, {})} | custom-call | tf_op jit(solution)/shard_map/pallas_call | solution.py:301
  9.5 1.6 %collective-permute-start.3 = (f32[56,128]{1,0:T(8,128)S(1)}, f32[56,128]{1,0:T(8,128)S(1)}, u32[]{:S(2)}, u32[]{:S(2)}) collective-permute-start(f32[56,128]{1,0:T(8,128)S(1)} %get-tuple-element.39), channel_id=1, source_target_pairs={{3,19},{16,0},{0,1},{17,16},{1,2},{18,17},{2,3},{19,18},{7,23},{20... | collective-permute-start | bytes 86024 | tf_op jit(solution)/shard_map/ppermute | solution.py:367
  11.0 0.0 collective-permute-start.4
  11.0 1.5 %shard_map.68 = (f32[8,104,384]{2,1,0:T(8,128)}, f32[8,104,256]{2,1,0:T(8,128)S(1)}, f32[8,104,128]{2,1,0:T(8,128)S(1)}) custom-call(f32[10,104,384]{2,1,0:T(8,128)S(1)} %get-tuple-element.33.sums, bf16[256,384]{1,0:T(8,128)(2,1)S(1)} %get-tuple-element.34.table_h, bf16[256,384]{1,0:T(8,128)(2,1)S(1)} %get-tuple-element.35.table_l), custom_call_target="tpu_custom_call" | custom-call | tf_op jit(solution)/shard_map/pallas_call | solution.py:301
  12.5 0.0 collective-permute-done.3.got
  12.6 1.3 %shard_map.69.out_in = f32[8,104,384]{2,1,0:T(8,128)} custom-call(f32[8,104,384]{2,1,0:T(8,128)} %get-tuple-element.36.out_in, f32[8,104,256]{2,1,0:T(8,128)S(1)} %get-tuple-element.37.ends, f32[8,104,128]{2,1,0:T(8,128)S(1)} %get-tuple-element.38.scales, f32[56,128]{1,0:T(8,128)S(1)} %collective-permute-done.3.got, ...), custom_call_target="tpu_custom_call", output_to_operand_aliasing={{}: (0, {})} | custom-call | tf_op jit(solution)/shard_map/pallas_call | solution.py:301
  13.9 1.0 %collective-permute-done.4.got = f32[56,128]{1,0:T(8,128)S(1)} collective-permute-done((f32[56,128]{1,0:T(8,128)S(1)}, f32[56,128]{1,0:T(8,128)S(1)}, u32[]{:S(2)}, u32[]{:S(2)}) %collective-permute-start.4) | collective-permute-done | bytes 28704 | tf_op jit(solution)/shard_map/ppermute | solution.py:368
  14.9 1.3 %shard_map.70 = f32[8,104,384]{2,1,0:T(8,128)} custom-call(f32[8,104,384]{2,1,0:T(8,128)} %shard_map.69.out_in, f32[8,104,256]{2,1,0:T(8,128)S(1)} %get-tuple-element.37.ends, f32[8,104,128]{2,1,0:T(8,128)S(1)} %get-tuple-element.38.scales, f32[56,128]{1,0:T(8,128)S(1)} %collective-permute-done.4.got, ...), custom_call_target="tpu_custom_call", output_to_operand_aliasing={{}: (0, {})} | custom-call | tf_op jit(solution)/shard_map/pallas_call | solution.py:301
  (1 shorter events, 0.0 us)
Async XLA Ops:
  0.0 5.7 %copy-start.1 = (s32[2,16,208]{2,1,0:T(8,128)S(1)}, s32[2,16,208]{2,1,0:T(8,128)}, u32[]{:S(2)}) copy-start(s32[2,16,208]{2,1,0:T(8,128)} %steps_hbm.1) | copy-start | bytes 79876
  0.0 5.7 %copy-start = (f32[16,208,256]{2,1,0:T(8,128)S(1)}, f32[16,208,256]{2,1,0:T(8,128)}, u32[]{:S(2)}) copy-start(f32[16,208,256]{2,1,0:T(8,128)} %traces.3) | copy-start | bytes 10223620
  1.5 1.4 %collective-permute-start = (f32[16,384]{1,0:T(8,128)S(1)}, f32[16,384]{1,0:T(8,128)S(1)}, u32[]{:S(2)}, u32[]{:S(2)}) collective-permute-start(f32[16,384]{1,0:T(8,128)S(1)} %get-tuple-element.26), channel_id=1, source_target_pairs={{0,16},{16,0},{1,17},{17,1},{2,18},{18,2},{3,19},{19,3},{4,20},{20... | collective-permute-start | bytes 73736 | tf_op jit(solution)/shard_map/ppermute | solution.py:343
  2.9 4.8 %collective-permute-start.1 = (f32[16,384]{1,0:T(8,128)S(1)}, f32[16,384]{1,0:T(8,128)S(1)}, u32[]{:S(2)}, u32[]{:S(2)}) collective-permute-start(f32[16,384]{1,0:T(8,128)S(1)} %add.3), channel_id=1, source_target_pairs={{12,28},{16,0},{0,4},{20,16},{4,8},{24,20},{8,12},{28,24},{13,29},... | collective-permute-start | bytes 73736 | tf_op jit(solution)/shard_map/ppermute | solution.py:344
  7.8 1.5 %collective-permute-start.2 = (f32[112,384]{1,0:T(8,128)S(1)}, f32[112,384]{1,0:T(8,128)S(1)}, u32[]{:S(2)}, u32[]{:S(2)}) collective-permute-start(f32[112,384]{1,0:T(8,128)S(1)} %get-tuple-element.32), channel_id=1, source_target_pairs={{0,16},{16,0},{1,17},{17,1},{2,18},{18,2},{3,19},{19,3},{4,20},{20... | collective-permute-start | bytes 516104 | tf_op jit(solution)/shard_map/ppermute | solution.py:360
  9.5 3.1 %collective-permute-start.3 = (f32[56,128]{1,0:T(8,128)S(1)}, f32[56,128]{1,0:T(8,128)S(1)}, u32[]{:S(2)}, u32[]{:S(2)}) collective-permute-start(f32[56,128]{1,0:T(8,128)S(1)} %get-tuple-element.39), channel_id=1, source_target_pairs={{3,19},{16,0},{0,1},{17,16},{1,2},{18,17},{2,3},{19,18},{7,23},{20... | collective-permute-start | bytes 86024 | tf_op jit(solution)/shard_map/ppermute | solution.py:367
  11.0 3.9 %collective-permute-start.4 = (f32[56,128]{1,0:T(8,128)S(1)}, f32[56,128]{1,0:T(8,128)S(1)}, u32[]{:S(2)}, u32[]{:S(2)}) collective-permute-start(f32[56,128]{1,0:T(8,128)S(1)} %get-tuple-element.42), channel_id=1, source_target_pairs={{19,3},{0,16},{1,0},{16,17},{2,1},{17,18},{3,2},{18,19},{23,7},{4,... | collective-permute-start | bytes 86024 | tf_op jit(solution)/shard_map/ppermute | solution.py:368

commit v5 on v4

--- a/solution.py
+++ b/solution.py
@@ -59,6 +59,35 @@
     return jnp.dot(a, b, precision=precision, preferred_element_type=F32)
 
 
+def sends_up():
+    return (lax.axis_index("il") + lax.axis_index("xl")) % 2 == 0
+
+
+def gets():
+    xl, last = lax.axis_index("xl"), lax.axis_size("xl") - 1
+    low = lax.axis_index("il") == 0
+    end = (xl == 0) | (xl == last)
+    return jnp.where(end, xl == 0, sends_up()), ~(end & low)
+
+
+def other_at_start():
+    xl, last = lax.axis_index("xl"), lax.axis_size("xl") - 1
+    end = (xl == 0) | (xl == last)
+    return jnp.where(end, xl == last, sends_up())
+
+
+def paired(count):
+    assert count % 2 == 0 and count > 2
+    last = count - 1
+    target = {i: i ^ 1 for i in range(count)}
+    for i in range(1, last, 2):
+        target[count + i], target[count + i + 1] = count + i + 1, count + i
+    for end in (0, last):
+        target[end ^ 1] = count + end
+        target[count + end] = end
+    return sorted(target.items())
+
+
 def rim_kernel(traces, steps_hbm, keep, give, left, right, steps, sems):
     rows, cols, length = traces.shape
     copies = (
@@ -69,6 +98,7 @@
     for copy in copies:
         copy.start(priority=1)
     low = lax.axis_index("il") == 0
+    up = sends_up()
     g = lax.broadcasted_iota(jnp.int32, (rows, 6 * rows), 0) + jnp.where(low, 1, 1 - rows // 2)
     k = lax.broadcasted_iota(jnp.int32, (rows, 6 * rows), 1) % (3 * rows)
     pick = ((k % rows) // 2 + k // rows == g).astype(F32).astype(BF16)
@@ -97,8 +127,8 @@
         sides.append(jnp.concatenate(parts, axis=0))
     both = dot(pick, jnp.concatenate(split(jnp.concatenate(sides, axis=1)), axis=0))
     to_left, to_right = both[:, : length + LANES], both[:, length + LANES :]
-    keep[...] = jnp.where(low, to_right, to_left)
-    give[...] = jnp.where(low, to_left, to_right)
+    keep[...] = jnp.where(up, to_right, to_left)
+    give[...] = jnp.where(up, to_left, to_right)
 
 
 def groups_of(cols):
@@ -113,7 +143,7 @@
 
 
 def bin_kernel(traces, steps, *refs):
-    tables, (sums, first, last, *copies), (keys, counts, sems) = refs[:4], refs[4:11], refs[11:]
+    tables, (sums, *copies), (keys, counts, sems) = refs[:4], refs[4:9], refs[9:]
     loads = [pltpu.make_async_copy(a, b, sems.at[n]) for n, (a, b) in enumerate(zip(tables, copies))]
     for load in loads:
         load.start()
@@ -126,10 +156,7 @@
         here, there = column[:, start : start + LANES], row[:, start : start + LANES]
         inside = (here >= low) & (here < high)
         keys[g] = jnp.where(inside, there * (high - low) + here - low, -1)
-    sums[...] = jnp.zeros(sums.shape, F32)
-    counts[...] = jnp.zeros(counts.shape, F32)
-
-    def body(a, _):
+    for a in range(rows // 2):
         parts = [split(traces[2 * a + p]) for p in (0, 1)]
         for g, (low, high, start) in enumerate(groups):
             n = high - low
@@ -143,23 +170,16 @@
                 term = dot(hot, jnp.concatenate(window, axis=0))
                 total = term if total is None else total + term
             for s in range(3):
-                sums[a + s, low:high, :length] += total[s * n : (s + 1) * n]
-                counts[a + s, low:high] += count[s * n : (s + 1) * n]
-        return 0
-
-    lax.fori_loop(0, rows // 2, body, 0, unroll=True)
+                piece, number = total[s * n : (s + 1) * n], count[s * n : (s + 1) * n]
+                if s == 2 or a == 0:
+                    sums[a + s, low:high, :length] = piece
+                    counts[a + s, low:high] = number
+                else:
+                    sums[a + s, low:high, :length] += piece
+                    counts[a + s, low:high] += number
     for r in range(rows // 2 + 2):
         whole = jnp.sum(counts[r], axis=1, keepdims=True)
         sums[r, :, length:] = jnp.broadcast_to(whole, (bins, LANES))
-    lane = lax.broadcasted_iota(jnp.int32, (bins, LANES), 1)
-    heads = jnp.zeros((bins, LANES), F32)
-    tails = jnp.zeros((bins, LANES), F32)
-    for b in range(rows // 2):
-        here = lane // REACH == b
-        heads = jnp.where(here, edges(sums[b + 1], length, b * REACH, False), heads)
-        tails = jnp.where(here, edges(sums[b + 1], length, b * REACH, True), tails)
-    first[...] = heads
-    last[...] = tails
     for load in loads:
         load.wait()
 
@@ -168,6 +188,16 @@
     if tail:
         return pltpu.roll(plane[:, length - LANES : length], (lane0 + REACH) % LANES, 1)
     return pltpu.roll(plane[:, :LANES], lane0, 1) if lane0 else plane[:, :LANES]
+
+
+def edge_kernel(sums, first, last):
+    rows, bins, width = sums.shape
+    lane = lax.broadcasted_iota(jnp.int32, (bins, LANES), 1)
+    for out, tail in ((first, False), (last, True)):
+        values = jnp.zeros((bins, LANES), F32)
+        for b in range(rows - 2):
+            values = jnp.where(lane // REACH == b, edges(sums[b + 1], width - LANES, b * REACH, tail), values)
+        out[...] = values
 
 
 def add_column(values, at_start, sums, first, last):
@@ -191,14 +221,13 @@
 
 def join_xl_kernel(sums_in, got, first_in, last_in, sums, payload, first, last):
     rows, bins, _ = sums.shape
-    xl = lax.axis_index("xl")
     low = lax.axis_index("il") == 0
-    there = jnp.where(low, xl > 0, xl < lax.axis_size("xl") - 1)
+    above, there = gets()
     count = rows - 2
     values = jnp.where(there, got[...], 0.0)
     payload[:bins, :] = sums[jnp.where(low, rows - 1, 0)]
     payload[bins:, :] = jnp.where(low, values[count:], values[:count])
-    add_column(jnp.where(low, values[:count], values[count:]), low, sums, first, last)
+    add_column(jnp.where(low, values[:count], values[count:]), ~above, sums, first, last)
 
 
 def join_il_kernel(sums_in, first_in, last_in, got, sums, first, last, one, two):
@@ -206,7 +235,7 @@
     length = width - LANES
     low = lax.axis_index("il") == 0
     half = LANES // 2
-    add_column(got[bins:], ~low, sums, first, last)
+    add_column(got[bins:], other_at_start(), sums, first, last)
     rim = got[:bins]
     sums[jnp.where(low, rows - 2, 1)] += rim
     lane = lax.broadcasted_iota(jnp.int32, (bins, LANES), 1)
@@ -341,16 +370,17 @@
     )(in_hbm(traces), in_hbm(bin_steps))
     swap = [(0, 1), (1, 0)]
     chip_rims = keep + lax.ppermute(give, "il", swap)
-    came = lax.ppermute(chip_rims, ("il", "xl"), turning(n_xl))
+    came = lax.ppermute(chip_rims, ("il", "xl"), paired(n_xl))
 
     tables = (*main, *edge)
-    sums, first, last, *tables = call(
+    sums, *tables = call(
         bin_kernel,
         [VMEM, VMEM] + [HBM] * 4,
-        [vmem(half + 2, bins, width)] + [vmem(bins, LANES)] * 2 + [vmem(*t.shape, kind=BF16) for t in tables],
+        [vmem(half + 2, bins, width)] + [vmem(*t.shape, kind=BF16) for t in tables],
         [pltpu.VMEM((len(groups_of(cols)), rows, LANES), jnp.int32), pltpu.VMEM((half + 2, bins, LANES), F32), dma((4,))],
     )(traces, bin_steps, *[in_hbm(t) for t in tables])
     main, edge = tables[:2], tables[2:]
+    first, last = call(edge_kernel, [VMEM], [vmem(bins, LANES)] * 2)(sums)
     sums, payload, first, last = call(
         join_xl_kernel,
         [VMEM] * 4,

time: 16.3 us -> 16 us (0.982)
  Pallas kernels: 7.73 us -> 7.44 us
    pallas_call x7 -> x8, Pallas kernels: 7.73 us -> 7.44 us  [run(): pl.pallas_call(kernel, in_specs=ins, out_specs=[spec for spec, _ in outs]...]
  transfers between devices with their start and end apart: 5 -> 5, of which waited for: 3 -> 3; matrix products, arithmetic and copies ran while one was open for 0% -> 0% of each run, Pallas kernels for 29% -> 28%
where the time goes in v5:
time: 16 us; the launch traced here: 15.9 us
  Pallas kernels  7.44 us (46%)
  starting transfers between devices  5.04 us (32%)
  waiting for transfers between devices  3.33 us (21%)
    pallas_call x8, Pallas kernels, run(): pl.pallas_call(kernel, in_specs=ins, out_specs=[spec for spec, _ in outs]...  7.44 us
    ppermute x1, starting transfers between devices, steps_of(): came = lax.ppermute(chip_rims, ('il', 'xl'), paired(n_xl))  2.82 us
    ppermute x1, starting transfers between devices, steps_of(): one = lax.ppermute(one, ('il', 'ta'), turning(n_ta))  1.58 us
    ppermute x1, waiting for transfers between devices, steps_of(): got = lax.ppermute(payload, 'il', swap)  1.39 us
    ppermute x1, waiting for transfers between devices, steps_of(): two = lax.ppermute(two, ('il', 'ta'), [(j, i) for i, j in turning(n_ta)])  1.04 us
    ppermute x1, waiting for transfers between devices, steps_of(): chip_rims = keep + lax.ppermute(give, 'il', swap)  0.85 us
    ppermute x1, starting transfers between devices, steps_of(): chip_rims = keep + lax.ppermute(give, 'il', swap)  0.56 us
  transfers between devices with their start and end apart: 5, of which 3 were waited for; matrix products, arithmetic and copies ran while one was open for 0% of the time, Pallas kernels for 28%

profile of v5, /device:TPU:0, one launch (start us, length us, event | category | flops | bytes accessed | tf_op | source)
XLA Modules:
  0.0 15.9 jit_solution(3584989270146896433)
XLA Ops:
  0.0 0.0 copy-start.1
  0.0 0.0 copy-start
  0.0 1.4 %shard_map.65 = (f32[16,384]{1,0:T(8,128)S(1)}, f32[16,384]{1,0:T(8,128)S(1)}) custom-call(f32[16,208,256]{2,1,0:T(8,128)} %traces.3, s32[2,16,208]{2,1,0:T(8,128)} %steps_hbm.1), custom_call_target="tpu_custom_call" | custom-call | tf_op jit(solution)/shard_map/pallas_call | solution.py:330
  1.5 0.6 %collective-permute-start = (f32[16,384]{1,0:T(8,128)S(1)}, f32[16,384]{1,0:T(8,128)S(1)}, u32[]{:S(2)}, u32[]{:S(2)}) collective-permute-start(f32[16,384]{1,0:T(8,128)S(1)} %get-tuple-element.26), channel_id=1, source_target_pairs={{0,16},{16,0},{1,17},{17,1},{2,18},{18,2},{3,19},{19,3},{4,20},{20... | collective-permute-start | bytes 73736 | tf_op jit(solution)/shard_map/ppermute | solution.py:372
  2.0 0.8 %collective-permute-done = f32[16,384]{1,0:T(8,128)S(1)} collective-permute-done((f32[16,384]{1,0:T(8,128)S(1)}, f32[16,384]{1,0:T(8,128)S(1)}, u32[]{:S(2)}, u32[]{:S(2)}) %collective-permute-start) | collective-permute-done | bytes 24608 | tf_op jit(solution)/shard_map/ppermute | solution.py:372
  2.9 2.8 %collective-permute-start.1 = (f32[16,384]{1,0:T(8,128)S(1)}, f32[16,384]{1,0:T(8,128)S(1)}, u32[]{:S(2)}, u32[]{:S(2)}) collective-permute-start(f32[16,384]{1,0:T(8,128)S(1)} %add.3), channel_id=1, source_target_pairs={{0,4},{4,16},{8,28},{12,8},{16,0},{20,24},{24,20},{28,12},{1,5},{5... | collective-permute-start | bytes 73736 | tf_op jit(solution)/shard_map/ppermute | solution.py:373
  5.7 0.0 copy-done.1
  5.7 0.0 copy-done
  5.7 1.4 %shard_map.64 = (f32[10,104,384]{2,1,0:T(8,128)S(1)}, bf16[256,384]{1,0:T(8,128)(2,1)S(1)}, bf16[256,384]{1,0:T(8,128)(2,1)S(1)}, bf16[2,128,128]{2,1,0:T(8,128)(2,1)S(1)}, bf16[2,128,128]{2,1,0:T(8,128)(2,1)S(1)}) custom-call(f32[16,208,256]{2,1,0:T(8,128)S(1)} %copy-done, s32[2,16,208]{2,1,0:T(8,128)S(1)} %copy-done.1, ...), custom_call_target="tpu_custom_call" | custom-call | tf_op jit(solution)/shard_map/pallas_call | solution.py:330
  7.1 0.3 %shard_map.66 = (f32[104,128]{1,0:T(8,128)S(1)}, f32[104,128]{1,0:T(8,128)S(1)}) custom-call(f32[10,104,384]{2,1,0:T(8,128)S(1)} %get-tuple-element.24.sums.sums_in), custom_call_target="tpu_custom_call" | custom-call | tf_op jit(solution)/shard_map/pallas_call | solution.py:330
  7.4 0.0 collective-permute-done.1.got
  7.4 0.1 shard_map.67
  7.5 0.1 collective-permute-start.2
  7.6 1.4 %collective-permute-done.2.got = f32[112,384]{1,0:T(8,128)S(1)} collective-permute-done((f32[112,384]{1,0:T(8,128)S(1)}, f32[112,384]{1,0:T(8,128)S(1)}, u32[]{:S(2)}, u32[]{:S(2)}) %collective-permute-start.2) | collective-permute-done | bytes 172064 | tf_op jit(solution)/shard_map/ppermute | solution.py:390
  9.0 0.2 %shard_map.68 = (f32[10,104,384]{2,1,0:T(8,128)S(1)}, f32[104,128]{1,0:T(8,128)S(1)}, f32[104,128]{1,0:T(8,128)S(1)}, f32[56,128]{1,0:T(8,128)S(1)}, f32[56,128]{1,0:T(8,128)S(1)}) custom-call(f32[10,104,384]{2,1,0:T(8,128)S(1)} %get-tuple-element.29.sums_in, ...), custom_call_target="tpu_custom_call", output_to_operand_aliasing={{0}: (0, {}), {1}: (1, {}), {2}: (2, {})} | custom-call | tf_op jit(solution)/shard_map/pallas_call | solution.py:330
  9.2 1.6 %collective-permute-start.3 = (f32[56,128]{1,0:T(8,128)S(1)}, f32[56,128]{1,0:T(8,128)S(1)}, u32[]{:S(2)}, u32[]{:S(2)}) collective-permute-start(f32[56,128]{1,0:T(8,128)S(1)} %get-tuple-element.39), channel_id=1, source_target_pairs={{3,19},{16,0},{0,1},{17,16},{1,2},{18,17},{2,3},{19,18},{7,23},{20... | collective-permute-start | bytes 86024 | tf_op jit(solution)/shard_map/ppermute | solution.py:397
  10.8 0.0 collective-permute-start.4
  10.8 1.5 %shard_map.69 = (f32[8,104,384]{2,1,0:T(8,128)}, f32[8,104,256]{2,1,0:T(8,128)S(1)}, f32[8,104,128]{2,1,0:T(8,128)S(1)}) custom-call(f32[10,104,384]{2,1,0:T(8,128)S(1)} %get-tuple-element.33.sums, bf16[256,384]{1,0:T(8,128)(2,1)S(1)} %get-tuple-element.34.table_h, bf16[256,384]{1,0:T(8,128)(2,1)S(1)} %get-tuple-element.35.table_l), custom_call_target="tpu_custom_call" | custom-call | tf_op jit(solution)/shard_map/pallas_call | solution.py:330
  12.3 0.0 collective-permute-done.3.got
  12.3 1.3 %shard_map.70.out_in = f32[8,104,384]{2,1,0:T(8,128)} custom-call(f32[8,104,384]{2,1,0:T(8,128)} %get-tuple-element.36.out_in, f32[8,104,256]{2,1,0:T(8,128)S(1)} %get-tuple-element.37.ends, f32[8,104,128]{2,1,0:T(8,128)S(1)} %get-tuple-element.38.scales, f32[56,128]{1,0:T(8,128)S(1)} %collective-permute-done.3.got, ...), custom_call_target="tpu_custom_call", output_to_operand_aliasing={{}: (0, {})} | custom-call | tf_op jit(solution)/shard_map/pallas_call | solution.py:330
  13.6 1.0 %collective-permute-done.4.got = f32[56,128]{1,0:T(8,128)S(1)} collective-permute-done((f32[56,128]{1,0:T(8,128)S(1)}, f32[56,128]{1,0:T(8,128)S(1)}, u32[]{:S(2)}, u32[]{:S(2)}) %collective-permute-start.4) | collective-permute-done | bytes 28704 | tf_op jit(solution)/shard_map/ppermute | solution.py:398
  14.6 1.3 %shard_map.71 = f32[8,104,384]{2,1,0:T(8,128)} custom-call(f32[8,104,384]{2,1,0:T(8,128)} %shard_map.70.out_in, f32[8,104,256]{2,1,0:T(8,128)S(1)} %get-tuple-element.37.ends, f32[8,104,128]{2,1,0:T(8,128)S(1)} %get-tuple-element.38.scales, f32[56,128]{1,0:T(8,128)S(1)} %collective-permute-done.4.got, ...), custom_call_target="tpu_custom_call", output_to_operand_aliasing={{}: (0, {})} | custom-call | tf_op jit(solution)/shard_map/pallas_call | solution.py:330
  (1 shorter events, 0.0 us)
Async XLA Ops:
  0.0 5.7 %copy-start.1 = (s32[2,16,208]{2,1,0:T(8,128)S(1)}, s32[2,16,208]{2,1,0:T(8,128)}, u32[]{:S(2)}) copy-start(s32[2,16,208]{2,1,0:T(8,128)} %steps_hbm.1) | copy-start | bytes 79876
  0.0 5.7 %copy-start = (f32[16,208,256]{2,1,0:T(8,128)S(1)}, f32[16,208,256]{2,1,0:T(8,128)}, u32[]{:S(2)}) copy-start(f32[16,208,256]{2,1,0:T(8,128)} %traces.3) | copy-start | bytes 10223620
  1.5 1.4 %collective-permute-start = (f32[16,384]{1,0:T(8,128)S(1)}, f32[16,384]{1,0:T(8,128)S(1)}, u32[]{:S(2)}, u32[]{:S(2)}) collective-permute-start(f32[16,384]{1,0:T(8,128)S(1)} %get-tuple-element.26), channel_id=1, source_target_pairs={{0,16},{16,0},{1,17},{17,1},{2,18},{18,2},{3,19},{19,3},{4,20},{20... | collective-permute-start | bytes 73736 | tf_op jit(solution)/shard_map/ppermute | solution.py:372
  2.9 4.5 %collective-permute-start.1 = (f32[16,384]{1,0:T(8,128)S(1)}, f32[16,384]{1,0:T(8,128)S(1)}, u32[]{:S(2)}, u32[]{:S(2)}) collective-permute-start(f32[16,384]{1,0:T(8,128)S(1)} %add.3), channel_id=1, source_target_pairs={{0,4},{4,16},{8,28},{12,8},{16,0},{20,24},{24,20},{28,12},{1,5},{5... | collective-permute-start | bytes 73736 | tf_op jit(solution)/shard_map/ppermute | solution.py:373
  7.5 1.5 %collective-permute-start.2 = (f32[112,384]{1,0:T(8,128)S(1)}, f32[112,384]{1,0:T(8,128)S(1)}, u32[]{:S(2)}, u32[]{:S(2)}) collective-permute-start(f32[112,384]{1,0:T(8,128)S(1)} %get-tuple-element.32), channel_id=1, source_target_pairs={{0,16},{16,0},{1,17},{17,1},{2,18},{18,2},{3,19},{19,3},{4,20},{20... | collective-permute-start | bytes 516104 | tf_op jit(solution)/shard_map/ppermute | solution.py:390
  9.2 3.1 %collective-permute-start.3 = (f32[56,128]{1,0:T(8,128)S(1)}, f32[56,128]{1,0:T(8,128)S(1)}, u32[]{:S(2)}, u32[]{:S(2)}) collective-permute-start(f32[56,128]{1,0:T(8,128)S(1)} %get-tuple-element.39), channel_id=1, source_target_pairs={{3,19},{16,0},{0,1},{17,16},{1,2},{18,17},{2,3},{19,18},{7,23},{20... | collective-permute-start | bytes 86024 | tf_op jit(solution)/shard_map/ppermute | solution.py:397
  10.8 3.9 %collective-permute-start.4 = (f32[56,128]{1,0:T(8,128)S(1)}, f32[56,128]{1,0:T(8,128)S(1)}, u32[]{:S(2)}, u32[]{:S(2)}) collective-permute-start(f32[56,128]{1,0:T(8,128)S(1)} %get-tuple-element.42), channel_id=1, source_target_pairs={{19,3},{0,16},{1,0},{16,17},{2,1},{17,18},{3,2},{18,19},{23,7},{4,... | collective-permute-start | bytes 86024 | tf_op jit(solution)/shard_map/ppermute | solution.py:398

commit v6 on v5

--- a/solution.py
+++ b/solution.py
@@ -142,13 +142,8 @@
     return out
 
 
-def bin_kernel(traces, steps, *refs):
-    tables, (sums, *copies), (keys, counts, sems) = refs[:4], refs[4:9], refs[9:]
-    loads = [pltpu.make_async_copy(a, b, sems.at[n]) for n, (a, b) in enumerate(zip(tables, copies))]
-    for load in loads:
-        load.start()
+def add_rows(traces, steps, pairs, fresh, sums, counts, keys):
     rows, cols, length = traces.shape
-    bins = cols // 2
     groups = groups_of(cols)
     column = lax.broadcasted_iota(jnp.int32, (rows, cols), 1) // 2 + steps[1]
     row = steps[0] + 1
@@ -156,7 +151,8 @@
         here, there = column[:, start : start + LANES], row[:, start : start + LANES]
         inside = (here >= low) & (here < high)
         keys[g] = jnp.where(inside, there * (high - low) + here - low, -1)
-    for a in range(rows // 2):
+    fresh = set(fresh)
+    for a in pairs:
         parts = [split(traces[2 * a + p]) for p in (0, 1)]
         for g, (low, high, start) in enumerate(groups):
             n = high - low
@@ -171,17 +167,44 @@
                 total = term if total is None else total + term
             for s in range(3):
                 piece, number = total[s * n : (s + 1) * n], count[s * n : (s + 1) * n]
-                if s == 2 or a == 0:
+                if a + s in fresh:
                     sums[a + s, low:high, :length] = piece
                     counts[a + s, low:high] = number
                 else:
                     sums[a + s, low:high, :length] += piece
                     counts[a + s, low:high] += number
-    for r in range(rows // 2 + 2):
-        whole = jnp.sum(counts[r], axis=1, keepdims=True)
-        sums[r, :, length:] = jnp.broadcast_to(whole, (bins, LANES))
-    for load in loads:
-        load.wait()
+        fresh -= {a, a + 1, a + 2}
+
+
+def fold_lanes(counts):
+    whole = jnp.sum(counts, axis=1, keepdims=True)
+    return jnp.broadcast_to(whole, counts.shape)
+
+
+def outer_pairs(count):
+    return sorted({0, min(1, count - 1), max(count - 2, 0), count - 1})
+
+
+def bin_outer_kernel(traces, steps, sums, counts, row, keys):
+    half = traces.shape[0] // 2
+    length = traces.shape[2]
+    add_rows(traces, steps, outer_pairs(half), range(half + 2), sums, counts, keys)
+    place = jnp.where(lax.axis_index("il") == 0, half + 1, 0)
+    row[:, :length] = sums[place, :, :length]
+    row[:, length:] = fold_lanes(counts[place])
+
+
+def bin_inner_kernel(traces, steps, sums_in, counts, sums, keys, number):
+    half = traces.shape[0] // 2
+    length = traces.shape[2]
+    done = outer_pairs(half)
+    written = {a + s for a in done for s in range(3)}
+    fresh = [r for r in range(half + 2) if r not in written]
+    for r in written:
+        number[r] = counts[r]
+    add_rows(traces, steps, [a for a in range(half) if a not in done], fresh, sums, number, keys)
+    for r in range(1, half + 1):
+        sums[r, :, length:] = fold_lanes(number[r])
 
 
 def edges(plane, length, lane0, tail):
@@ -190,63 +213,75 @@
     return pltpu.roll(plane[:, :LANES], lane0, 1) if lane0 else plane[:, :LANES]
 
 
-def edge_kernel(sums, first, last):
+def edge_kernel(sums_in, rim, sums, first, last):
     rows, bins, width = sums.shape
+    sums[jnp.where(lax.axis_index("il") == 0, rows - 2, 1)] += rim[...]
     lane = lax.broadcasted_iota(jnp.int32, (bins, LANES), 1)
     for out, tail in ((first, False), (last, True)):
         values = jnp.zeros((bins, LANES), F32)
         for b in range(rows - 2):
             values = jnp.where(lane // REACH == b, edges(sums[b + 1], width - LANES, b * REACH, tail), values)
-        out[...] = values
-
-
-def add_column(values, at_start, sums, first, last):
+        out[...] = packed(values)
+
+
+def corner(at_start, bins):
+    end = bins - 1 - split_row(bins)
+    row, lane = jnp.where(at_start, 0, end), jnp.where(at_start, 0, LANES // 2)
+    return pl.multiple_of(row // 8 * 8, 8), row % 8, lane
+
+
+def corner_edges(values, length, row, lane0):
+    count = values.shape[0]
+    sub = lax.broadcasted_iota(jnp.int32, (8, LANES), 0)
+    lane = lax.broadcasted_iota(jnp.int32, (1, LANES), 1)
+    out = []
+    for tail in (False, True):
+        line = jnp.zeros((1, LANES), F32)
+        for b in range(count):
+            line = jnp.where(lane // REACH == b, edges(values[b : b + 1], length, b * REACH, tail), line)
+        line = jnp.where(lane0 == 0, line, pltpu.roll(line, LANES // 2, 1))
+        out.append(jnp.where(sub == row, jnp.broadcast_to(line, (8, LANES)), 0.0))
+    return out
+
+
+def join_xl_kernel(got, first_in, last_in, mine, payload, first, last, *, bins):
+    width = got.shape[1]
+    length = width - LANES
+    count = got.shape[0] // 2
+    low = lax.axis_index("il") == 0
+    above, there = gets()
+    values = jnp.where(there, got[...], 0.0)
+    other = jnp.where(low, values[count:], values[:count])
+    own = jnp.where(low, values[:count], values[count:])
+    mine[...] = own
+    payload[:, :width] = other
+    tile, row, lane0 = corner(~above, bins)
+    payload[:, width : width + LANES], payload[:, width + LANES :] = corner_edges(other, length, row, lane0)
+    gains = corner_edges(own, length, row, lane0)
+    first[pl.ds(tile, 8), :] += gains[0]
+    last[pl.ds(tile, 8), :] += gains[1]
+
+
+def join_il_kernel(first, last, got, one, two, *, bins):
+    width = got.shape[1] - 2 * LANES
+    even = lax.axis_index("ta") % 2 == 0
+    head, tail = first[...], last[...]
+    one[...] = jnp.where(even, tail, head)
+    two[...] = jnp.where(even, head, tail)
+    tile, _, _ = corner(other_at_start(), bins)
+    head, tail = got[:, width : width + LANES], got[:, width + LANES :]
+    one[pl.ds(tile, 8), :] += jnp.where(even, tail, head)
+    two[pl.ds(tile, 8), :] += jnp.where(even, head, tail)
+
+
+def add_column(values, at_start, sums):
     rows, bins, width = sums.shape
-    length = width - LANES
     sub = lax.broadcasted_iota(jnp.int32, (8, width), 0)
-    place = jnp.where(at_start, 0, 7)
     base = pl.multiple_of(jnp.where(at_start, 0, bins - 8), 8)
-    there = sub == place
+    there = sub == jnp.where(at_start, 0, 7)
     for b in range(rows - 2):
         gain = jnp.where(there, jnp.broadcast_to(values[b : b + 1], (8, width)), 0.0)
         sums[b + 1, pl.ds(base, 8), :] += gain
-    lane = lax.broadcasted_iota(jnp.int32, (8, LANES), 1)
-    for edge, tail in ((first, False), (last, True)):
-        gain = jnp.zeros((8, LANES), F32)
-        for b in range(rows - 2):
-            row = edges(values[b : b + 1], length, b * REACH, tail)
-            gain = jnp.where(lane // REACH == b, jnp.broadcast_to(row, (8, LANES)), gain)
-        edge[pl.ds(base, 8), :] += jnp.where(there[:, :LANES], gain, 0.0)
-
-
-def join_xl_kernel(sums_in, got, first_in, last_in, sums, payload, first, last):
-    rows, bins, _ = sums.shape
-    low = lax.axis_index("il") == 0
-    above, there = gets()
-    count = rows - 2
-    values = jnp.where(there, got[...], 0.0)
-    payload[:bins, :] = sums[jnp.where(low, rows - 1, 0)]
-    payload[bins:, :] = jnp.where(low, values[count:], values[:count])
-    add_column(jnp.where(low, values[:count], values[count:]), ~above, sums, first, last)
-
-
-def join_il_kernel(sums_in, first_in, last_in, got, sums, first, last, one, two):
-    rows, bins, width = sums.shape
-    length = width - LANES
-    low = lax.axis_index("il") == 0
-    half = LANES // 2
-    add_column(got[bins:], other_at_start(), sums, first, last)
-    rim = got[:bins]
-    sums[jnp.where(low, rows - 2, 1)] += rim
-    lane = lax.broadcasted_iota(jnp.int32, (bins, LANES), 1)
-    values = []
-    for old, tail in ((first, False), (last, True)):
-        edge = edges(rim, length, 0, tail)
-        edge = jnp.where(low, pltpu.roll(edge, half - REACH, 1), edge)
-        there = lane // REACH == jnp.where(low, half // REACH - 1, 0)
-        values.append(packed(old[...] + jnp.where(there, edge, 0.0)))
-    one[...] = jnp.where(low, values[1], values[0])
-    two[...] = jnp.where(low, values[0], values[1])
 
 
 def split_row(bins):
@@ -265,41 +300,29 @@
     return jnp.concatenate([values, pltpu.roll(values, LANES // 2, 1)[: bins - values.shape[0]]], axis=0)
 
 
-def resample_kernel(sums, table_h, table_l, out, ends, scales, middle, sem):
+def resample_kernel(sums_in, mine, got, table_h, table_l, sums, tiles, scales):
     rows, bins, width = sums.shape
+    add_column(mine[...], ~gets()[0], sums)
+    add_column(got[:, :width], other_at_start(), sums)
     length = width - LANES
     count = rows - 2
-    out_len = out.shape[2]
     step = 2
-    copies = []
     for start in range(0, count, step):
         planes = sums[start + 1 : start + 1 + step]
         scale = 1.0 / jnp.maximum(planes[:, :, length:], 1.0)
         scales[start : start + step] = scale
         values = planes[:, :, :length] * jnp.concatenate([scale] * (length // LANES), axis=2)
         high, low = split(values.reshape(step * bins, length))
-        got = dot(high, table_h[...]) + dot(low, table_h[...]) + dot(high, table_l[...])
-        got = got.reshape(step, bins, out_len)
-        middle[start : start + step] = got[:, :, LANES : out_len - LANES]
-        copies.append(
-            pltpu.make_async_copy(
-                middle.at[start : start + step],
-                out.at[start : start + step, :, LANES : out_len - LANES],
-                sem.at[start // step],
-            )
-        )
-        copies[-1].start()
-        ends[start : start + step, :, :LANES] = got[:, :, :LANES]
-        ends[start : start + step, :, LANES:] = got[:, :, out_len - LANES :]
-    for copy in copies:
-        copy.wait()
-
-
-def finish_kernel(first_trade, out_in, ends, scales, got, table_h, table_l, out, piece, sem):
-    count, bins, _ = ends.shape
+        got_out = dot(high, table_h[...]) + dot(low, table_h[...]) + dot(high, table_l[...])
+        for tile in range(tiles.shape[0]):
+            piece = got_out[:, tile * LANES : (tile + 1) * LANES]
+            tiles[tile, start : start + step] = piece.reshape(step, bins, LANES)
+
+
+def end_pieces(first_trade, tiles, scales, got, table_h, table_l):
+    count, bins, _ = scales.shape
     ta = lax.axis_index("ta")
-    low = lax.axis_index("il") == 0
-    before = low if first_trade else ~low
+    before = ta % 2 == (1 if first_trade else 0)
     there = jnp.where(before, ta > 0, ta < lax.axis_size("ta") - 1)
     values = unpacked(jnp.where(there, got[...], 0.0), bins)
     high, low_part = split(values)
@@ -309,13 +332,36 @@
     fix = jnp.where(before, fix, pltpu.roll(fix, LANES - SPREAD, 1))
     lane = lax.broadcasted_iota(jnp.int32, (bins, LANES), 1)
     here = jnp.where(before, lane, LANES - 1 - lane) < SPREAD
-    start = pl.multiple_of(jnp.where(before, 0, out.shape[2] - LANES), LANES)
-    copies = []
+    tile = jnp.where(before, 0, tiles.shape[0] - 1)
     for b in range(count):
-        base = jnp.where(before, ends[b, :, :LANES], ends[b, :, LANES:])
         moved = pltpu.roll(fix, LANES - b * SPREAD, 1) if b else fix
-        piece[b] = base + jnp.where(here, moved, 0.0) * scales[b]
-        copies.append(pltpu.make_async_copy(piece.at[b], out.at[b, :, pl.ds(start, LANES)], sem.at[b]))
+        yield tile, b, tiles[tile, b] + jnp.where(here, moved, 0.0) * scales[b]
+
+
+def to_output(tiles, out, tile, rows, sem):
+    start = tile * LANES if isinstance(tile, int) else pl.multiple_of(tile * LANES, LANES)
+    return pltpu.make_async_copy(tiles.at[tile, rows], out.at[rows, :, pl.ds(start, LANES)], sem)
+
+
+def finish_one_kernel(tiles_in, scales, got, table_h, table_l, tiles):
+    for tile, b, piece in end_pieces(True, tiles, scales, got, table_h, table_l):
+        tiles[tile, b] = piece
+
+
+def finish_two_kernel(tiles_in, scales, got, table_h, table_l, out, tiles, sems):
+    count = scales.shape[0]
+    every = pl.ds(0, count)
+    ta = lax.axis_index("ta")
+    before = ta % 2 == 0
+    last = tiles_in.shape[0] - 1
+    copies = [to_output(tiles_in, out, n, every, sems.at[count + n]) for n in range(1, last)]
+    copies.append(to_output(tiles_in, out, jnp.where(before, last, 0), every, sems.at[count]))
+    for copy in copies:
+        copy.start()
+    for tile, b, piece in end_pieces(False, tiles_in, scales, got, table_h, table_l):
+        tiles[b] = piece
+        start = pl.multiple_of(tile * LANES, LANES)
+        copies.append(pltpu.make_async_copy(tiles.at[b], out.at[b, :, pl.ds(start, LANES)], sems.at[b]))
         copies[-1].start()
     for copy in copies:
         copy.wait()
@@ -369,57 +415,61 @@
         [pltpu.VMEM((rows, 8, length), F32)] * 2 + [pltpu.VMEM(bin_steps.shape, jnp.int32), dma((3,))],
     )(in_hbm(traces), in_hbm(bin_steps))
     swap = [(0, 1), (1, 0)]
-    chip_rims = keep + lax.ppermute(give, "il", swap)
-    came = lax.ppermute(chip_rims, ("il", "xl"), paired(n_xl))
-
-    tables = (*main, *edge)
-    sums, *tables = call(
-        bin_kernel,
-        [VMEM, VMEM] + [HBM] * 4,
-        [vmem(half + 2, bins, width)] + [vmem(*t.shape, kind=BF16) for t in tables],
-        [pltpu.VMEM((len(groups_of(cols)), rows, LANES), jnp.int32), pltpu.VMEM((half + 2, bins, LANES), F32), dma((4,))],
-    )(traces, bin_steps, *[in_hbm(t) for t in tables])
-    main, edge = tables[:2], tables[2:]
-    first, last = call(edge_kernel, [VMEM], [vmem(bins, LANES)] * 2)(sums)
-    sums, payload, first, last = call(
-        join_xl_kernel,
-        [VMEM] * 4,
-        [vmem(half + 2, bins, width), vmem(bins + half, width)] + [vmem(bins, LANES)] * 2,
-        aliases={0: 0, 2: 2, 3: 3},
-    )(sums, came, first, last)
+    shape = (half + 2, bins, width)
+    keys = pltpu.VMEM((len(groups_of(cols)), rows, LANES), jnp.int32)
+    other = lax.ppermute(give, "il", swap)
+    sums, counts, row = call(
+        bin_outer_kernel, [VMEM] * 2, [vmem(*shape), vmem(half + 2, bins, LANES), vmem(bins, width)], [keys]
+    )(traces, bin_steps)
+    came = lax.ppermute(keep + other, ("il", "xl"), paired(n_xl))
+    rim = lax.ppermute(row, "il", swap)
+
+    (sums,) = call(
+        bin_inner_kernel, [VMEM] * 4, [vmem(*shape)], [keys, pltpu.VMEM((half + 2, bins, LANES), F32)], {2: 0}
+    )(traces, bin_steps, sums, counts)
+    tall = split_row(bins)
+    sums, first, last = call(
+        edge_kernel, [VMEM] * 2, [vmem(*shape)] + [vmem(tall, LANES)] * 2, aliases={0: 0}
+    )(sums, rim)
+    mine, payload, first, last = call(
+        functools.partial(join_xl_kernel, bins=bins),
+        [VMEM] * 3,
+        [vmem(half, width), vmem(half, width + 2 * LANES)] + [vmem(tall, LANES)] * 2,
+        aliases={1: 2, 2: 3},
+    )(came, first, last)
     got = lax.ppermute(payload, "il", swap)
-    sums, first, last, one, two = call(
-        join_il_kernel,
-        [VMEM] * 4,
-        [vmem(half + 2, bins, width)] + [vmem(bins, LANES)] * 2 + [vmem(split_row(bins), LANES)] * 2,
-        aliases={0: 0, 1: 1, 2: 2},
-    )(sums, first, last, got)
-    one = lax.ppermute(one, ("il", "ta"), turning(n_ta))
-    two = lax.ppermute(two, ("il", "ta"), [(j, i) for i, j in turning(n_ta)])
-
-    whole = (HBM, jax.ShapeDtypeStruct((half, bins, out_len), F32))
-    out, ends, scales = call(
+    one, two = call(functools.partial(join_il_kernel, bins=bins), [VMEM] * 3, [vmem(tall, LANES)] * 2)(first, last, got)
+    ones, twos = trades(n_ta)
+    one = lax.ppermute(one, ("il", "ta"), ones)
+    two = lax.ppermute(two, ("il", "ta"), twos)
+
+    count = out_len // LANES
+    sums, tiles, scales = call(
         resample_kernel,
-        [VMEM] * 3,
-        [whole, vmem(half, bins, 2 * LANES), vmem(half, bins, LANES)],
-        [pltpu.VMEM((half, bins, out_len - 2 * LANES), F32), dma((half // 2,))],
-    )(sums, *main)
-    for first_trade, halo in ((True, one), (False, two)):
-        (out,) = call(
-            functools.partial(finish_kernel, first_trade),
-            [HBM] + [VMEM] * 5,
-            [whole],
-            [pltpu.VMEM((half, bins, LANES), F32), dma((half,))],
-            {0: 0},
-        )(out, ends, scales, halo, *edge)
+        [VMEM] * 5,
+        [vmem(*shape), vmem(count, half, bins, LANES), vmem(half, bins, LANES)],
+        aliases={0: 0},
+    )(sums, mine, got, *main)
+    (tiles,) = call(
+        finish_one_kernel, [VMEM] * 5, [vmem(count, half, bins, LANES)], aliases={0: 0}
+    )(tiles, scales, one, *edge)
+    (out,) = call(
+        finish_two_kernel,
+        [VMEM] * 5,
+        [(HBM, jax.ShapeDtypeStruct((half, bins, out_len), F32))],
+        [pltpu.VMEM((half, bins, LANES), F32), dma((half + count,))],
+    )(tiles, scales, two, *edge)
     return out
 
 
-def turning(count):
-    pairs = [(count - 1, 2 * count - 1), (count, 0)]
-    for i in range(count - 1):
-        pairs += [(i, i + 1), (count + i + 1, count + i)]
-    return pairs
+def trades(count):
+    assert count % 2 == 0
+    one = [(core * count + i, core * count + (i ^ 1)) for core in range(2) for i in range(count)]
+    two = [(0, count), (count, 0), (count - 1, 2 * count - 1), (2 * count - 1, count - 1)]
+    for core in range(2):
+        for i in range(1, count - 1, 2):
+            two += [(core * count + i, core * count + i + 1), (core * count + i + 1, core * count + i)]
+    return one, two
 
 
 def solution(mesh):

time: 16 us -> 18.8 us (1.18)
  the two profiles are of different devices: /device:TPU:0 before, /device:TPU:20 now
where the time goes in v6:
time: 18.8 us; the launch traced here: 18.5 us
  Pallas kernels  6.05 us (32%)
  waiting for transfers between devices  5.67 us (30%)
  starting transfers between devices  3.95 us (21%)
  local copies, waits for them, and re-layouts  2.76 us (15%)
    pallas_call x9, Pallas kernels, run(): pl.pallas_call(kernel, in_specs=ins, out_specs=[spec for spec, _ in outs]...  6.05 us
    unnamed x16, local copies, waits for them, and re-layouts  2.76 us
    ppermute x1, starting transfers between devices, steps_of(): one = lax.ppermute(one, ('il', 'ta'), ones)  1.64 us
    ppermute x1, starting transfers between devices, steps_of(): came = lax.ppermute(keep + other, ('il', 'xl'), paired(n_xl))  1.44 us
    ppermute x1, waiting for transfers between devices, steps_of(): one = lax.ppermute(one, ('il', 'ta'), ones)  1.38 us
    ppermute x1, waiting for transfers between devices, steps_of(): came = lax.ppermute(keep + other, ('il', 'xl'), paired(n_xl))  1.22 us
    ppermute x1, waiting for transfers between devices, steps_of(): two = lax.ppermute(two, ('il', 'ta'), twos)  1.13 us
    ppermute x1, waiting for transfers between devices, steps_of(): got = lax.ppermute(payload, 'il', swap)  1.09 us
  transfers between devices with their start and end apart: 6, of which 5 were waited for; matrix products, arithmetic and copies ran while one was open for 0% of the time, Pallas kernels for 21%

profile of v6, /device:TPU:20, one launch (start us, length us, event | category | flops | bytes accessed | tf_op | source)
XLA Modules:
  0.0 18.5 jit_solution(4003459003715568484)
XLA Ops:
  0.0 0.0 copy-start
  0.0 2.0 %copy-done = f32[16,208,256]{2,1,0:T(8,128)S(1)} copy-done((f32[16,208,256]{2,1,0:T(8,128)S(1)}, f32[16,208,256]{2,1,0:T(8,128)}, u32[]{:S(2)}) %copy-start) | copy-done | bytes 3407896
  2.0 0.0 copy-start.2
  2.0 0.8 %copy-done.2 = s32[2,16,208]{2,1,0:T(8,128)S(1)} copy-done((s32[2,16,208]{2,1,0:T(8,128)S(1)}, s32[2,16,208]{2,1,0:T(8,128)}, u32[]{:S(2)}) %copy-start.2) | copy-done | bytes 26648
  2.7 0.7 %shard_map.64 = (f32[10,104,384]{2,1,0:T(8,128)S(1)}, f32[10,104,128]{2,1,0:T(8,128)S(1)}, f32[104,384]{1,0:T(8,128)S(1)}) custom-call(f32[16,208,256]{2,1,0:T(8,128)S(1)} %copy-done, s32[2,16,208]{2,1,0:T(8,128)S(1)} %copy-done.2), custom_call_target="tpu_custom_call" | custom-call | tf_op jit(solution)/shard_map/pallas_call | solution.py:376
  3.4 0.0 copy-start.1
  3.5 0.0 copy-start.3
  3.5 0.1 collective-permute-start
  3.6 1.4 %shard_map.67 = (f32[16,384]{1,0:T(8,128)S(1)}, f32[16,384]{1,0:T(8,128)S(1)}) custom-call(f32[16,208,256]{2,1,0:T(8,128)} %traces.5, s32[2,16,208]{2,1,0:T(8,128)} %steps_hbm.1), custom_call_target="tpu_custom_call" | custom-call | tf_op jit(solution)/shard_map/pallas_call | solution.py:376
  5.0 0.7 %collective-permute-start.1 = (f32[16,384]{1,0:T(8,128)S(1)}, f32[16,384]{1,0:T(8,128)S(1)}, u32[]{:S(2)}, u32[]{:S(2)}) collective-permute-start(f32[16,384]{1,0:T(8,128)S(1)} %get-tuple-element.26), channel_id=1, source_target_pairs={{0,16},{16,0},{1,17},{17,1},{2,18},{18,2},{3,19},{19,3},{4,20},{20... | collective-permute-start | bytes 73736 | tf_op jit(solution)/shard_map/ppermute | solution.py:420
  5.7 0.8 %collective-permute-done.1 = f32[16,384]{1,0:T(8,128)S(1)} collective-permute-done((f32[16,384]{1,0:T(8,128)S(1)}, f32[16,384]{1,0:T(8,128)S(1)}, u32[]{:S(2)}, u32[]{:S(2)}) %collective-permute-start.1) | collective-permute-done | bytes 24608 | tf_op jit(solution)/shard_map/ppermute | solution.py:420
  6.5 1.4 %collective-permute-start.2 = (f32[16,384]{1,0:T(8,128)S(1)}, f32[16,384]{1,0:T(8,128)S(1)}, u32[]{:S(2)}, u32[]{:S(2)}) collective-permute-start(f32[16,384]{1,0:T(8,128)S(1)} %add.3), channel_id=1, source_target_pairs={{0,4},{4,16},{8,28},{12,8},{16,0},{20,24},{24,20},{28,12},{1,5},{5... | collective-permute-start | bytes 73736 | tf_op jit(solution)/shard_map/ppermute | solution.py:424
  8.0 0.0 copy-done.1
  8.0 0.0 copy-done.3
  8.0 0.7 %shard_map.65.sums_in = f32[10,104,384]{2,1,0:T(8,128)S(1)} custom-call(f32[16,208,256]{2,1,0:T(8,128)S(1)} %copy-done.1, s32[2,16,208]{2,1,0:T(8,128)S(1)} %copy-done.3, f32[10,104,384]{2,1,0:T(8,128)S(1)} %get-tuple-element.21.sums_in, f32[10,104,128]{2,1,0:T(8,128)S(1)} %get-tuple-element.22.counts), custom_call_target="tpu_custom_call", output_to_operand_aliasing={{}: (2, {})} | custom-call | tf_op jit(solution)/shard_map/pallas_call | solution.py:376
  8.7 0.0 copy-start.6
  8.7 0.0 copy-start.7
  8.7 0.0 copy-start.4
  8.7 0.0 copy-start.5
  8.8 0.0 collective-permute-done.rim
  8.8 0.4 %shard_map.66 = (f32[10,104,384]{2,1,0:T(8,128)S(1)}, f32[56,128]{1,0:T(8,128)S(1)}, f32[56,128]{1,0:T(8,128)S(1)}) custom-call(f32[10,104,384]{2,1,0:T(8,128)S(1)} %shard_map.65.sums_in, f32[104,384]{1,0:T(8,128)S(1)} %collective-permute-done.rim), custom_call_target="tpu_custom_call", output_to_operand_aliasing={{0}: (0, {})} | custom-call | tf_op jit(solution)/shard_map/pallas_call | solution.py:376
  9.2 1.2 %collective-permute-done.2.got = f32[16,384]{1,0:T(8,128)S(1)} collective-permute-done((f32[16,384]{1,0:T(8,128)S(1)}, f32[16,384]{1,0:T(8,128)S(1)}, u32[]{:S(2)}, u32[]{:S(2)}) %collective-permute-start.2) | collective-permute-done | bytes 24608 | tf_op jit(solution)/shard_map/ppermute | solution.py:424
  10.4 0.2 shard_map.68
  10.5 0.1 collective-permute-start.3
  10.6 1.1 %collective-permute-done.3.got = f32[8,640]{1,0:T(8,128)S(1)} collective-permute-done((f32[8,640]{1,0:T(8,128)S(1)}, f32[8,640]{1,0:T(8,128)S(1)}, u32[]{:S(2)}, u32[]{:S(2)}) %collective-permute-start.3) | collective-permute-done | bytes 20512 | tf_op jit(solution)/shard_map/ppermute | solution.py:440
  11.8 1.6 %collective-permute-start.4 = (f32[56,128]{1,0:T(8,128)S(1)}, f32[56,128]{1,0:T(8,128)S(1)}, u32[]{:S(2)}, u32[]{:S(2)}) collective-permute-start(f32[56,128]{1,0:T(8,128)S(1)} %get-tuple-element.35), channel_id=1, source_target_pairs={{0,1},{1,0},{2,3},{3,2},{16,17},{17,16},{18,19},{19,18},{4,5},{5,4... | collective-permute-start | bytes 86024 | tf_op jit(solution)/shard_map/ppermute | solution.py:443
  13.4 0.0 collective-permute-start.5
  13.4 0.0 copy-done.6
  13.4 0.0 copy-done.7
  13.4 0.9 %shard_map.69 = (f32[10,104,384]{2,1,0:T(8,128)S(1)}, f32[3,8,104,128]{3,2,1,0:T(8,128)S(1)}, f32[8,104,128]{2,1,0:T(8,128)S(1)}) custom-call(f32[10,104,384]{2,1,0:T(8,128)S(1)} %get-tuple-element.24.sums_in, f32[8,384]{1,0:T(8,128)S(1)} %get-tuple-element.29.mine, f32[8,640]{1,0:T(8,128)S(1)} %collective-permute-done.3.got, ...), custom_call_target="tpu_custom_call", output_to_operand_aliasing={{0}: (0, {})} | custom-call | tf_op jit(solution)/shard_map/pallas_call | solution.py:376
  14.3 1.4 %collective-permute-done.4.got = f32[56,128]{1,0:T(8,128)S(1)} collective-permute-done((f32[56,128]{1,0:T(8,128)S(1)}, f32[56,128]{1,0:T(8,128)S(1)}, u32[]{:S(2)}, u32[]{:S(2)}) %collective-permute-start.4) | collective-permute-done | bytes 28704 | tf_op jit(solution)/shard_map/ppermute | solution.py:443
  15.7 0.0 copy-done.4
  15.7 0.0 copy-done.5
  15.7 0.4 %shard_map.71.tiles_in = f32[3,8,104,128]{3,2,1,0:T(8,128)S(1)} custom-call(f32[3,8,104,128]{3,2,1,0:T(8,128)S(1)} %get-tuple-element.31.tiles_in, f32[8,104,128]{2,1,0:T(8,128)S(1)} %get-tuple-element.32.scales, f32[56,128]{1,0:T(8,128)S(1)} %collective-permute-done.4.got, bf16[2,128,128]{2,1,0:T(8,128)(2,1)S(1)} %copy-done.5, ...), custom_call_target="tpu_custom_call", output_to_operand_aliasing={{}: (0, {})} | custom-call | tf_op jit(solution)/shard_map/pallas_call | solution.py:376
  16.2 1.1 %collective-permute-done.5.got = f32[56,128]{1,0:T(8,128)S(1)} collective-permute-done((f32[56,128]{1,0:T(8,128)S(1)}, f32[56,128]{1,0:T(8,128)S(1)}, u32[]{:S(2)}, u32[]{:S(2)}) %collective-permute-start.5) | collective-permute-done | bytes 28704 | tf_op jit(solution)/shard_map/ppermute | solution.py:444
  17.3 1.3 %shard_map.72 = f32[8,104,384]{2,1,0:T(8,128)} custom-call(f32[3,8,104,128]{3,2,1,0:T(8,128)S(1)} %shard_map.71.tiles_in, f32[8,104,128]{2,1,0:T(8,128)S(1)} %get-tuple-element.32.scales, f32[56,128]{1,0:T(8,128)S(1)} %collective-permute-done.5.got, bf16[2,128,128]{2,1,0:T(8,128)(2,1)S(1)} %copy-done.5, bf16[2,128,128]{2,1,0:T(8,128)(2,1)S(1)} %copy-done.4), custom_call_target="tpu_custom_call" | custom-call | tf_op jit(solution)/shard_map/pallas_call | solution.py:376
  (2 shorter events, 0.0 us)
Async XLA Ops:
  0.0 2.0 %copy-start = (f32[16,208,256]{2,1,0:T(8,128)S(1)}, f32[16,208,256]{2,1,0:T(8,128)}, u32[]{:S(2)}) copy-start(f32[16,208,256]{2,1,0:T(8,128)} %traces.5) | copy-start | bytes 10223620
  2.0 0.8 %copy-start.2 = (s32[2,16,208]{2,1,0:T(8,128)S(1)}, s32[2,16,208]{2,1,0:T(8,128)}, u32[]{:S(2)}) copy-start(s32[2,16,208]{2,1,0:T(8,128)} %steps_hbm.1) | copy-start | bytes 79876
  3.4 4.5 %copy-start.1 = (f32[16,208,256]{2,1,0:T(8,128)S(1)}, f32[16,208,256]{2,1,0:T(8,128)}, u32[]{:S(2)}) copy-start(f32[16,208,256]{2,1,0:T(8,128)} %traces.5) | copy-start | bytes 10223620
  3.5 4.5 %copy-start.3 = (s32[2,16,208]{2,1,0:T(8,128)S(1)}, s32[2,16,208]{2,1,0:T(8,128)}, u32[]{:S(2)}) copy-start(s32[2,16,208]{2,1,0:T(8,128)} %steps_hbm.1) | copy-start | bytes 79876
  3.5 5.3 %collective-permute-start = (f32[104,384]{1,0:T(8,128)S(1)}, f32[104,384]{1,0:T(8,128)S(1)}, u32[]{:S(2)}, u32[]{:S(2)}) collective-permute-start(f32[104,384]{1,0:T(8,128)S(1)} %get-tuple-element.23), channel_id=1, source_target_pairs={{0,16},{16,0},{1,17},{17,1},{2,18},{18,2},{3,19},{19,3},{4,20},{20... | collective-permute-start | bytes 479240 | tf_op jit(solution)/shard_map/ppermute | solution.py:425
  5.0 1.5 %collective-permute-start.1 = (f32[16,384]{1,0:T(8,128)S(1)}, f32[16,384]{1,0:T(8,128)S(1)}, u32[]{:S(2)}, u32[]{:S(2)}) collective-permute-start(f32[16,384]{1,0:T(8,128)S(1)} %get-tuple-element.26), channel_id=1, source_target_pairs={{0,16},{16,0},{1,17},{17,1},{2,18},{18,2},{3,19},{19,3},{4,20},{20... | collective-permute-start | bytes 73736 | tf_op jit(solution)/shard_map/ppermute | solution.py:420
  6.5 3.8 %collective-permute-start.2 = (f32[16,384]{1,0:T(8,128)S(1)}, f32[16,384]{1,0:T(8,128)S(1)}, u32[]{:S(2)}, u32[]{:S(2)}) collective-permute-start(f32[16,384]{1,0:T(8,128)S(1)} %add.3), channel_id=1, source_target_pairs={{0,4},{4,16},{8,28},{12,8},{16,0},{20,24},{24,20},{28,12},{1,5},{5... | collective-permute-start | bytes 73736 | tf_op jit(solution)/shard_map/ppermute | solution.py:424
  8.7 4.7 %copy-start.6 = (bf16[256,384]{1,0:T(8,128)(2,1)S(1)}, bf16[256,384]{1,0:T(8,128)(2,1)}, u32[]{:S(2)}) copy-start(bf16[256,384]{1,0:T(8,128)(2,1)} %constant.9.clone.table_l) | copy-start | bytes 589828
  8.7 4.7 %copy-start.7 = (bf16[256,384]{1,0:T(8,128)(2,1)S(1)}, bf16[256,384]{1,0:T(8,128)(2,1)}, u32[]{:S(2)}) copy-start(bf16[256,384]{1,0:T(8,128)(2,1)} %constant.8.clone.table_h) | copy-start | bytes 589828
  8.7 7.0 %copy-start.4 = (bf16[2,128,128]{2,1,0:T(8,128)(2,1)S(1)}, bf16[2,128,128]{2,1,0:T(8,128)(2,1)}, u32[]{:S(2)}) copy-start(bf16[2,128,128]{2,1,0:T(8,128)(2,1)} %constant.11.clone.table_l) | copy-start | bytes 196612
  8.7 7.0 %copy-start.5 = (bf16[2,128,128]{2,1,0:T(8,128)(2,1)S(1)}, bf16[2,128,128]{2,1,0:T(8,128)(2,1)}, u32[]{:S(2)}) copy-start(bf16[2,128,128]{2,1,0:T(8,128)(2,1)} %constant.10.clone.table_h) | copy-start | bytes 196612
  10.5 1.2 %collective-permute-start.3 = (f32[8,640]{1,0:T(8,128)S(1)}, f32[8,640]{1,0:T(8,128)S(1)}, u32[]{:S(2)}, u32[]{:S(2)}) collective-permute-start(f32[8,640]{1,0:T(8,128)S(1)} %get-tuple-element.30), channel_id=1, source_target_pairs={{0,16},{16,0},{1,17},{17,1},{2,18},{18,2},{3,19},{19,3},{4,20},{20... | collective-permute-start | bytes 61448 | tf_op jit(solution)/shard_map/ppermute | solution.py:440
  11.8 3.9 %collective-permute-start.4 = (f32[56,128]{1,0:T(8,128)S(1)}, f32[56,128]{1,0:T(8,128)S(1)}, u32[]{:S(2)}, u32[]{:S(2)}) collective-permute-start(f32[56,128]{1,0:T(8,128)S(1)} %get-tuple-element.35), channel_id=1, source_target_pairs={{0,1},{1,0},{2,3},{3,2},{16,17},{17,16},{18,19},{19,18},{4,5},{5,4... | collective-permute-start | bytes 86024 | tf_op jit(solution)/shard_map/ppermute | solution.py:443
  13.4 3.9 %collective-permute-start.5 = (f32[56,128]{1,0:T(8,128)S(1)}, f32[56,128]{1,0:T(8,128)S(1)}, u32[]{:S(2)}, u32[]{:S(2)}) collective-permute-start(f32[56,128]{1,0:T(8,128)S(1)} %get-tuple-element.36), channel_id=1, source_target_pairs={{0,16},{16,0},{3,19},{19,3},{1,2},{2,1},{17,18},{18,17},{4,20},{20... | collective-permute-start | bytes 86024 | tf_op jit(solution)/shard_map/ppermute | solution.py:444

commit v7 on v6

--- a/solution.py
+++ b/solution.py
@@ -38,15 +38,18 @@
 def edge_table(length, count):
     out_len = length * P_SIZE // Q
     assert count * REACH <= LANES // 2 and count * SPREAD <= LANES and REACH * P_SIZE <= SPREAD * Q
-    table = np.zeros((2, LANES, LANES))
+    table = np.zeros((2, LANES, 2 * LANES))
     k = np.arange(REACH)[:, None]
     m = np.arange(SPREAD)[None, :]
     before = weight((m * Q - (k - REACH) * P_SIZE) / P_SIZE)
     after = weight(((m + out_len - SPREAD) * Q - (length + k) * P_SIZE) / P_SIZE)
-    for b in range(count):
-        r, c = b * REACH, b * SPREAD
-        table[0, r : r + REACH, c : c + SPREAD] = before
-        table[1, r : r + REACH, c : c + SPREAD] = after
+    for part in range(2):
+        for b in range(count):
+            r = part * LANES // 2 + b * REACH
+            c = b * SPREAD
+            for side, values in ((0, before), (1, after)):
+                to = part * LANES + (c + m[0] - side * SPREAD) % LANES
+                table[side, r : r + REACH, to] = values.T
     return table
 
 
@@ -90,11 +93,14 @@
 
 def rim_kernel(traces, steps_hbm, keep, give, left, right, steps, sems):
     rows, cols, length = traces.shape
-    copies = (
-        pltpu.make_async_copy(steps_hbm, steps, sems.at[2]),
-        pltpu.make_async_copy(traces.at[:, 0:8, :], left, sems.at[0]),
-        pltpu.make_async_copy(traces.at[:, cols - 8 : cols, :], right, sems.at[1]),
-    )
+    step = rows // 4
+    copies = [pltpu.make_async_copy(steps_hbm, steps, sems.at[0])]
+    for n, start in enumerate(range(0, rows, step)):
+        part = pl.ds(start, step)
+        copies += [
+            pltpu.make_async_copy(traces.at[part, 0:8, :], left.at[part], sems.at[2 * n + 1]),
+            pltpu.make_async_copy(traces.at[part, cols - 8 : cols, :], right.at[part], sems.at[2 * n + 2]),
+        ]
     for copy in copies:
         copy.start(priority=1)
     low = lax.axis_index("il") == 0
@@ -111,8 +117,8 @@
             for shift in (-1, 0, 1):
                 hit = (step_xl[:, j : j + 1] == side) & (step_il[:, j : j + 1] == shift)
                 masks[side, j, shift] = hit.astype(F32)
-    copies[1].wait()
-    copies[2].wait()
+    for copy in copies[1:]:
+        copy.wait()
     sides = []
     for side, buf, spots in ((-1, left, ((0, 0), (1, 1))), (1, right, ((cols - 2, 6), (cols - 1, 7)))):
         parts = []
@@ -296,17 +302,14 @@
     return jnp.where(lane < LANES // 2, values[:cut], pltpu.roll(rest, LANES // 2, 1))
 
 
-def unpacked(values, bins):
-    return jnp.concatenate([values, pltpu.roll(values, LANES // 2, 1)[: bins - values.shape[0]]], axis=0)
-
-
-def resample_kernel(sums_in, mine, got, table_h, table_l, sums, tiles, scales):
+def resample_kernel(sums_in, mine, got, table_h, table_l, sums, tiles, scales, out, sems):
     rows, bins, width = sums.shape
     add_column(mine[...], ~gets()[0], sums)
     add_column(got[:, :width], other_at_start(), sums)
     length = width - LANES
     count = rows - 2
     step = 2
+    copies = []
     for start in range(0, count, step):
         planes = sums[start + 1 : start + 1 + step]
         scale = 1.0 / jnp.maximum(planes[:, :, length:], 1.0)
@@ -317,6 +320,12 @@
         for tile in range(tiles.shape[0]):
             piece = got_out[:, tile * LANES : (tile + 1) * LANES]
             tiles[tile, start : start + step] = piece.reshape(step, bins, LANES)
+        for tile in range(1, tiles.shape[0] - 1):
+            for b in range(start, start + step):
+                copies.append(to_output(tiles, out, tile, b, sems.at[tile - 1, b]))
+                copies[-1].start()
+    for copy in copies:
+        copy.wait()
 
 
 def end_pieces(first_trade, tiles, scales, got, table_h, table_l):
@@ -324,12 +333,11 @@
     ta = lax.axis_index("ta")
     before = ta % 2 == (1 if first_trade else 0)
     there = jnp.where(before, ta > 0, ta < lax.axis_size("ta") - 1)
-    values = unpacked(jnp.where(there, got[...], 0.0), bins)
-    high, low_part = split(values)
+    high, low_part = split(jnp.where(there, got[...], 0.0))
     side = jnp.where(before, 0, 1)
     start_h, start_l = table_h[side], table_l[side]
     fix = dot(high, start_h) + dot(low_part, start_h) + dot(high, start_l)
-    fix = jnp.where(before, fix, pltpu.roll(fix, LANES - SPREAD, 1))
+    fix = jnp.concatenate([fix[:, :LANES], fix[: bins - fix.shape[0], LANES:]], axis=0)
     lane = lax.broadcasted_iota(jnp.int32, (bins, LANES), 1)
     here = jnp.where(before, lane, LANES - 1 - lane) < SPREAD
     tile = jnp.where(before, 0, tiles.shape[0] - 1)
@@ -338,9 +346,9 @@
         yield tile, b, tiles[tile, b] + jnp.where(here, moved, 0.0) * scales[b]
 
 
-def to_output(tiles, out, tile, rows, sem):
+def to_output(tiles, out, tile, b, sem):
     start = tile * LANES if isinstance(tile, int) else pl.multiple_of(tile * LANES, LANES)
-    return pltpu.make_async_copy(tiles.at[tile, rows], out.at[rows, :, pl.ds(start, LANES)], sem)
+    return pltpu.make_async_copy(tiles.at[tile, b], out.at[b, :, pl.ds(start, LANES)], sem)
 
 
 def finish_one_kernel(tiles_in, scales, got, table_h, table_l, tiles):
@@ -348,20 +356,19 @@
         tiles[tile, b] = piece
 
 
-def finish_two_kernel(tiles_in, scales, got, table_h, table_l, out, tiles, sems):
+def finish_two_kernel(out_in, tiles_in, scales, got, table_h, table_l, out, tiles, sems):
     count = scales.shape[0]
-    every = pl.ds(0, count)
     ta = lax.axis_index("ta")
     before = ta % 2 == 0
     last = tiles_in.shape[0] - 1
-    copies = [to_output(tiles_in, out, n, every, sems.at[count + n]) for n in range(1, last)]
-    copies.append(to_output(tiles_in, out, jnp.where(before, last, 0), every, sems.at[count]))
+    tile = jnp.where(before, last, 0)
+    copies = [to_output(tiles_in, out, tile, b, sems.at[1, b]) for b in range(count)]
     for copy in copies:
         copy.start()
     for tile, b, piece in end_pieces(False, tiles_in, scales, got, table_h, table_l):
         tiles[b] = piece
         start = pl.multiple_of(tile * LANES, LANES)
-        copies.append(pltpu.make_async_copy(tiles.at[b], out.at[b, :, pl.ds(start, LANES)], sems.at[b]))
+        copies.append(pltpu.make_async_copy(tiles.at[b], out.at[b, :, pl.ds(start, LANES)], sems.at[0, b]))
         copies[-1].start()
     for copy in copies:
         copy.wait()
@@ -412,7 +419,7 @@
         rim_kernel,
         [HBM, HBM],
         [vmem(rows, width)] * 2,
-        [pltpu.VMEM((rows, 8, length), F32)] * 2 + [pltpu.VMEM(bin_steps.shape, jnp.int32), dma((3,))],
+        [pltpu.VMEM((rows, 8, length), F32)] * 2 + [pltpu.VMEM(bin_steps.shape, jnp.int32), dma((9,))],
     )(in_hbm(traces), in_hbm(bin_steps))
     swap = [(0, 1), (1, 0)]
     shape = (half + 2, bins, width)
@@ -444,21 +451,20 @@
     two = lax.ppermute(two, ("il", "ta"), twos)
 
     count = out_len // LANES
-    sums, tiles, scales = call(
+    whole = (HBM, jax.ShapeDtypeStruct((half, bins, out_len), F32))
+    sums, tiles, scales, out = call(
         resample_kernel,
         [VMEM] * 5,
-        [vmem(*shape), vmem(count, half, bins, LANES), vmem(half, bins, LANES)],
-        aliases={0: 0},
+        [vmem(*shape), vmem(count, half, bins, LANES), vmem(half, bins, LANES), whole],
+        [dma((count - 2, half))],
+        {0: 0},
     )(sums, mine, got, *main)
     (tiles,) = call(
         finish_one_kernel, [VMEM] * 5, [vmem(count, half, bins, LANES)], aliases={0: 0}
     )(tiles, scales, one, *edge)
     (out,) = call(
-        finish_two_kernel,
-        [VMEM] * 5,
-        [(HBM, jax.ShapeDtypeStruct((half, bins, out_len), F32))],
-        [pltpu.VMEM((half, bins, LANES), F32), dma((half + count,))],
-    )(tiles, scales, two, *edge)
+        finish_two_kernel, [HBM] + [VMEM] * 5, [whole], [pltpu.VMEM((half, bins, LANES), F32), dma((2, half))], {0: 0}
+    )(out, tiles, scales, two, *edge)
     return out
 
 

time: 18.8 us -> 18.6 us (0.989)
  waiting for transfers between devices: 5.67 us -> 5.05 us
  Pallas kernels: 6.05 us -> 6.55 us
    ppermute x1, waiting for transfers between devices: 1.38 us -> 0.65 us  [steps_of(): one = lax.ppermute(one, ('il', 'ta'), ones)]
    pallas_call x9, Pallas kernels: 6.05 us -> 6.55 us  [run(): pl.pallas_call(kernel, in_specs=ins, out_specs=[spec for spec, _ in outs]...]
  transfers between devices with their start and end apart: 6 -> 6, of which waited for: 5 -> 5; matrix products, arithmetic and copies ran while one was open for 0% -> 0% of each run, Pallas kernels for 21% -> 24%
where the time goes in v7:
time: 18.6 us; the launch traced here: 18.4 us
  Pallas kernels  6.55 us (35%)
  waiting for transfers between devices  5.05 us (27%)
  starting transfers between devices  3.95 us (21%)
  local copies, waits for them, and re-layouts  2.76 us (15%)
    pallas_call x9, Pallas kernels, run(): pl.pallas_call(kernel, in_specs=ins, out_specs=[spec for spec, _ in outs]...  6.55 us
    unnamed x16, local copies, waits for them, and re-layouts  2.76 us
    ppermute x1, starting transfers between devices, steps_of(): one = lax.ppermute(one, ('il', 'ta'), ones)  1.64 us
    ppermute x1, starting transfers between devices, steps_of(): came = lax.ppermute(keep + other, ('il', 'xl'), paired(n_xl))  1.44 us
    ppermute x1, waiting for transfers between devices, steps_of(): two = lax.ppermute(two, ('il', 'ta'), twos)  1.23 us
    ppermute x1, waiting for transfers between devices, steps_of(): came = lax.ppermute(keep + other, ('il', 'xl'), paired(n_xl))  1.22 us
    ppermute x1, waiting for transfers between devices, steps_of(): got = lax.ppermute(payload, 'il', swap)  1.09 us
    ppermute x1, waiting for transfers between devices, steps_of(): other = lax.ppermute(give, 'il', swap)  0.85 us
  transfers between devices with their start and end apart: 6, of which 5 were waited for; matrix products, arithmetic and copies ran while one was open for 0% of the time, Pallas kernels for 24%

profile of v7, /device:TPU:20, one launch (start us, length us, event | category | flops | bytes accessed | tf_op | source)
XLA Modules:
  0.0 18.4 jit_solution(9018314581209588654)
XLA Ops:
  0.0 0.0 copy-start
  0.0 2.0 %copy-done = f32[16,208,256]{2,1,0:T(8,128)S(1)} copy-done((f32[16,208,256]{2,1,0:T(8,128)S(1)}, f32[16,208,256]{2,1,0:T(8,128)}, u32[]{:S(2)}) %copy-start) | copy-done | bytes 3407896
  2.0 0.0 copy-start.4
  2.0 0.8 %copy-done.4 = s32[2,16,208]{2,1,0:T(8,128)S(1)} copy-done((s32[2,16,208]{2,1,0:T(8,128)S(1)}, s32[2,16,208]{2,1,0:T(8,128)}, u32[]{:S(2)}) %copy-start.4) | copy-done | bytes 26648
  2.7 0.7 %shard_map.64 = (f32[10,104,384]{2,1,0:T(8,128)S(1)}, f32[10,104,128]{2,1,0:T(8,128)S(1)}, f32[104,384]{1,0:T(8,128)S(1)}) custom-call(f32[16,208,256]{2,1,0:T(8,128)S(1)} %copy-done, s32[2,16,208]{2,1,0:T(8,128)S(1)} %copy-done.4), custom_call_target="tpu_custom_call" | custom-call | tf_op jit(solution)/shard_map/pallas_call | solution.py:383
  3.4 0.0 copy-start.1
  3.5 0.0 copy-start.5
  3.5 0.1 collective-permute-start
  3.6 1.4 %shard_map.67 = (f32[16,384]{1,0:T(8,128)S(1)}, f32[16,384]{1,0:T(8,128)S(1)}) custom-call(f32[16,208,256]{2,1,0:T(8,128)} %traces.5, s32[2,16,208]{2,1,0:T(8,128)} %steps_hbm.1), custom_call_target="tpu_custom_call" | custom-call | tf_op jit(solution)/shard_map/pallas_call | solution.py:383
  5.0 0.7 %collective-permute-start.1 = (f32[16,384]{1,0:T(8,128)S(1)}, f32[16,384]{1,0:T(8,128)S(1)}, u32[]{:S(2)}, u32[]{:S(2)}) collective-permute-start(f32[16,384]{1,0:T(8,128)S(1)} %get-tuple-element.27), channel_id=1, source_target_pairs={{0,16},{16,0},{1,17},{17,1},{2,18},{18,2},{3,19},{19,3},{4,20},{20... | collective-permute-start | bytes 73736 | tf_op jit(solution)/shard_map/ppermute | solution.py:427
  5.6 0.8 %collective-permute-done.1 = f32[16,384]{1,0:T(8,128)S(1)} collective-permute-done((f32[16,384]{1,0:T(8,128)S(1)}, f32[16,384]{1,0:T(8,128)S(1)}, u32[]{:S(2)}, u32[]{:S(2)}) %collective-permute-start.1) | collective-permute-done | bytes 24608 | tf_op jit(solution)/shard_map/ppermute | solution.py:427
  6.5 1.4 %collective-permute-start.2 = (f32[16,384]{1,0:T(8,128)S(1)}, f32[16,384]{1,0:T(8,128)S(1)}, u32[]{:S(2)}, u32[]{:S(2)}) collective-permute-start(f32[16,384]{1,0:T(8,128)S(1)} %add.3), channel_id=1, source_target_pairs={{0,4},{4,16},{8,28},{12,8},{16,0},{20,24},{24,20},{28,12},{1,5},{5... | collective-permute-start | bytes 73736 | tf_op jit(solution)/shard_map/ppermute | solution.py:431
  7.9 0.0 copy-done.1
  7.9 0.0 copy-done.5
  7.9 0.7 %shard_map.65.sums_in = f32[10,104,384]{2,1,0:T(8,128)S(1)} custom-call(f32[16,208,256]{2,1,0:T(8,128)S(1)} %copy-done.1, s32[2,16,208]{2,1,0:T(8,128)S(1)} %copy-done.5, f32[10,104,384]{2,1,0:T(8,128)S(1)} %get-tuple-element.22.sums_in, f32[10,104,128]{2,1,0:T(8,128)S(1)} %get-tuple-element.23.counts), custom_call_target="tpu_custom_call", output_to_operand_aliasing={{}: (2, {})} | custom-call | tf_op jit(solution)/shard_map/pallas_call | solution.py:383
  8.7 0.0 copy-start.6
  8.7 0.0 copy-start.7
  8.7 0.0 copy-start.2
  8.7 0.0 copy-start.3
  8.7 0.0 collective-permute-done.rim
  8.7 0.4 %shard_map.66 = (f32[10,104,384]{2,1,0:T(8,128)S(1)}, f32[56,128]{1,0:T(8,128)S(1)}, f32[56,128]{1,0:T(8,128)S(1)}) custom-call(f32[10,104,384]{2,1,0:T(8,128)S(1)} %shard_map.65.sums_in, f32[104,384]{1,0:T(8,128)S(1)} %collective-permute-done.rim), custom_call_target="tpu_custom_call", output_to_operand_aliasing={{0}: (0, {})} | custom-call | tf_op jit(solution)/shard_map/pallas_call | solution.py:383
  9.1 1.2 %collective-permute-done.2.got = f32[16,384]{1,0:T(8,128)S(1)} collective-permute-done((f32[16,384]{1,0:T(8,128)S(1)}, f32[16,384]{1,0:T(8,128)S(1)}, u32[]{:S(2)}, u32[]{:S(2)}) %collective-permute-start.2) | collective-permute-done | bytes 24608 | tf_op jit(solution)/shard_map/ppermute | solution.py:431
  10.3 0.2 shard_map.68
  10.5 0.1 collective-permute-start.3
  10.6 1.1 %collective-permute-done.3.got = f32[8,640]{1,0:T(8,128)S(1)} collective-permute-done((f32[8,640]{1,0:T(8,128)S(1)}, f32[8,640]{1,0:T(8,128)S(1)}, u32[]{:S(2)}, u32[]{:S(2)}) %collective-permute-start.3) | collective-permute-done | bytes 20512 | tf_op jit(solution)/shard_map/ppermute | solution.py:447
  11.7 1.6 %collective-permute-start.4 = (f32[56,128]{1,0:T(8,128)S(1)}, f32[56,128]{1,0:T(8,128)S(1)}, u32[]{:S(2)}, u32[]{:S(2)}) collective-permute-start(f32[56,128]{1,0:T(8,128)S(1)} %get-tuple-element.37), channel_id=1, source_target_pairs={{0,1},{1,0},{2,3},{3,2},{16,17},{17,16},{18,19},{19,18},{4,5},{5,4... | collective-permute-start | bytes 86024 | tf_op jit(solution)/shard_map/ppermute | solution.py:450
  13.4 0.0 collective-permute-start.5
  13.4 0.0 copy-done.6
  13.4 0.0 copy-done.7
  13.4 1.6 %shard_map.69 = (f32[10,104,384]{2,1,0:T(8,128)S(1)}, f32[3,8,104,128]{3,2,1,0:T(8,128)S(1)}, f32[8,104,128]{2,1,0:T(8,128)S(1)}, f32[8,104,384]{2,1,0:T(8,128)}) custom-call(f32[10,104,384]{2,1,0:T(8,128)S(1)} %get-tuple-element.25.sums_in, f32[8,384]{1,0:T(8,128)S(1)} %get-tuple-element.30.mine, ...), custom_call_target="tpu_custom_call", output_to_operand_aliasing={{0}: (0, {})} | custom-call | tf_op jit(solution)/shard_map/pallas_call | solution.py:383
  15.0 0.7 %collective-permute-done.4.got = f32[56,128]{1,0:T(8,128)S(1)} collective-permute-done((f32[56,128]{1,0:T(8,128)S(1)}, f32[56,128]{1,0:T(8,128)S(1)}, u32[]{:S(2)}, u32[]{:S(2)}) %collective-permute-start.4) | collective-permute-done | bytes 28704 | tf_op jit(solution)/shard_map/ppermute | solution.py:450
  15.7 0.0 copy-done.2
  15.7 0.0 copy-done.3
  15.7 0.3 %shard_map.71.tiles_in = f32[3,8,104,128]{3,2,1,0:T(8,128)S(1)} custom-call(f32[3,8,104,128]{3,2,1,0:T(8,128)S(1)} %get-tuple-element.33.tiles_in, f32[8,104,128]{2,1,0:T(8,128)S(1)} %get-tuple-element.34.scales, f32[56,128]{1,0:T(8,128)S(1)} %collective-permute-done.4.got, bf16[2,128,256]{2,1,0:T(8,128)(2,1)S(1)} %copy-done.3, ...), custom_call_target="tpu_custom_call", output_to_operand_aliasing={{}: (0, {})} | custom-call | tf_op jit(solution)/shard_map/pallas_call | solution.py:383
  16.0 1.2 %collective-permute-done.5.got = f32[56,128]{1,0:T(8,128)S(1)} collective-permute-done((f32[56,128]{1,0:T(8,128)S(1)}, f32[56,128]{1,0:T(8,128)S(1)}, u32[]{:S(2)}, u32[]{:S(2)}) %collective-permute-start.5) | collective-permute-done | bytes 28704 | tf_op jit(solution)/shard_map/ppermute | solution.py:451
  17.2 1.2 %shard_map.72 = f32[8,104,384]{2,1,0:T(8,128)} custom-call(f32[8,104,384]{2,1,0:T(8,128)} %get-tuple-element.32.out_in, f32[3,8,104,128]{3,2,1,0:T(8,128)S(1)} %shard_map.71.tiles_in, f32[8,104,128]{2,1,0:T(8,128)S(1)} %get-tuple-element.34.scales, f32[56,128]{1,0:T(8,128)S(1)} %collective-permute-done.5.got, ...), custom_call_target="tpu_custom_call", output_to_operand_aliasing={{}: (0, {})} | custom-call | tf_op jit(solution)/shard_map/pallas_call | solution.py:383
  (2 shorter events, 0.0 us)
Async XLA Ops:
  0.0 2.0 %copy-start = (f32[16,208,256]{2,1,0:T(8,128)S(1)}, f32[16,208,256]{2,1,0:T(8,128)}, u32[]{:S(2)}) copy-start(f32[16,208,256]{2,1,0:T(8,128)} %traces.5) | copy-start | bytes 10223620
  2.0 0.8 %copy-start.4 = (s32[2,16,208]{2,1,0:T(8,128)S(1)}, s32[2,16,208]{2,1,0:T(8,128)}, u32[]{:S(2)}) copy-start(s32[2,16,208]{2,1,0:T(8,128)} %steps_hbm.1) | copy-start | bytes 79876
  3.4 4.5 %copy-start.1 = (f32[16,208,256]{2,1,0:T(8,128)S(1)}, f32[16,208,256]{2,1,0:T(8,128)}, u32[]{:S(2)}) copy-start(f32[16,208,256]{2,1,0:T(8,128)} %traces.5) | copy-start | bytes 10223620
  3.5 4.5 %copy-start.5 = (s32[2,16,208]{2,1,0:T(8,128)S(1)}, s32[2,16,208]{2,1,0:T(8,128)}, u32[]{:S(2)}) copy-start(s32[2,16,208]{2,1,0:T(8,128)} %steps_hbm.1) | copy-start | bytes 79876
  3.5 5.2 %collective-permute-start = (f32[104,384]{1,0:T(8,128)S(1)}, f32[104,384]{1,0:T(8,128)S(1)}, u32[]{:S(2)}, u32[]{:S(2)}) collective-permute-start(f32[104,384]{1,0:T(8,128)S(1)} %get-tuple-element.24), channel_id=1, source_target_pairs={{0,16},{16,0},{1,17},{17,1},{2,18},{18,2},{3,19},{19,3},{4,20},{20... | collective-permute-start | bytes 479240 | tf_op jit(solution)/shard_map/ppermute | solution.py:432
  5.0 1.5 %collective-permute-start.1 = (f32[16,384]{1,0:T(8,128)S(1)}, f32[16,384]{1,0:T(8,128)S(1)}, u32[]{:S(2)}, u32[]{:S(2)}) collective-permute-start(f32[16,384]{1,0:T(8,128)S(1)} %get-tuple-element.27), channel_id=1, source_target_pairs={{0,16},{16,0},{1,17},{17,1},{2,18},{18,2},{3,19},{19,3},{4,20},{20... | collective-permute-start | bytes 73736 | tf_op jit(solution)/shard_map/ppermute | solution.py:427
  6.5 3.8 %collective-permute-start.2 = (f32[16,384]{1,0:T(8,128)S(1)}, f32[16,384]{1,0:T(8,128)S(1)}, u32[]{:S(2)}, u32[]{:S(2)}) collective-permute-start(f32[16,384]{1,0:T(8,128)S(1)} %add.3), channel_id=1, source_target_pairs={{0,4},{4,16},{8,28},{12,8},{16,0},{20,24},{24,20},{28,12},{1,5},{5... | collective-permute-start | bytes 73736 | tf_op jit(solution)/shard_map/ppermute | solution.py:431
  8.7 4.7 %copy-start.6 = (bf16[256,384]{1,0:T(8,128)(2,1)S(1)}, bf16[256,384]{1,0:T(8,128)(2,1)}, u32[]{:S(2)}) copy-start(bf16[256,384]{1,0:T(8,128)(2,1)} %constant.9.clone.table_l) | copy-start | bytes 589828
  8.7 4.7 %copy-start.7 = (bf16[256,384]{1,0:T(8,128)(2,1)S(1)}, bf16[256,384]{1,0:T(8,128)(2,1)}, u32[]{:S(2)}) copy-start(bf16[256,384]{1,0:T(8,128)(2,1)} %constant.8.clone.table_h) | copy-start | bytes 589828
  8.7 7.0 %copy-start.2 = (bf16[2,128,256]{2,1,0:T(8,128)(2,1)S(1)}, bf16[2,128,256]{2,1,0:T(8,128)(2,1)}, u32[]{:S(2)}) copy-start(bf16[2,128,256]{2,1,0:T(8,128)(2,1)} %constant.11.clone.table_l) | copy-start | bytes 393220
  8.7 7.0 %copy-start.3 = (bf16[2,128,256]{2,1,0:T(8,128)(2,1)S(1)}, bf16[2,128,256]{2,1,0:T(8,128)(2,1)}, u32[]{:S(2)}) copy-start(bf16[2,128,256]{2,1,0:T(8,128)(2,1)} %constant.10.clone.table_h) | copy-start | bytes 393220
  10.5 1.2 %collective-permute-start.3 = (f32[8,640]{1,0:T(8,128)S(1)}, f32[8,640]{1,0:T(8,128)S(1)}, u32[]{:S(2)}, u32[]{:S(2)}) collective-permute-start(f32[8,640]{1,0:T(8,128)S(1)} %get-tuple-element.31), channel_id=1, source_target_pairs={{0,16},{16,0},{1,17},{17,1},{2,18},{18,2},{3,19},{19,3},{4,20},{20... | collective-permute-start | bytes 61448 | tf_op jit(solution)/shard_map/ppermute | solution.py:447
  11.7 3.9 %collective-permute-start.4 = (f32[56,128]{1,0:T(8,128)S(1)}, f32[56,128]{1,0:T(8,128)S(1)}, u32[]{:S(2)}, u32[]{:S(2)}) collective-permute-start(f32[56,128]{1,0:T(8,128)S(1)} %get-tuple-element.37), channel_id=1, source_target_pairs={{0,1},{1,0},{2,3},{3,2},{16,17},{17,16},{18,19},{19,18},{4,5},{5,4... | collective-permute-start | bytes 86024 | tf_op jit(solution)/shard_map/ppermute | solution.py:450
  13.4 3.9 %collective-permute-start.5 = (f32[56,128]{1,0:T(8,128)S(1)}, f32[56,128]{1,0:T(8,128)S(1)}, u32[]{:S(2)}, u32[]{:S(2)}) collective-permute-start(f32[56,128]{1,0:T(8,128)S(1)} %get-tuple-element.38), channel_id=1, source_target_pairs={{0,16},{16,0},{3,19},{19,3},{1,2},{2,1},{17,18},{18,17},{4,20},{20... | collective-permute-start | bytes 86024 | tf_op jit(solution)/shard_map/ppermute | solution.py:451
